TPU v7x, 256 devices: a whole 4x4x8 slice. The times are simulated.
256 devices in a mesh: ctx: 64 (over y, z, core), head: 4 (over x).
Axes of the slice: x: 4, y: 4, z: 8, core: 2. Of those that a mesh axis runs over, the one named last changes fastest.
Arguments:
- queries: bfloat16 [8192, 2048], P('ctx', 'head'), may hold values from -6 to 6
- keys: bfloat16 [8192, 2048], P('ctx', 'head'), may hold values from -6 to 6
- values: bfloat16 [8192, 4096], P('ctx', 'head'), may hold values from -6 to 6
- out_gate: bfloat16 [8192, 4096], P('ctx', 'head'), may hold values from -6 to 6
- log_decay: float32 [8192, 32], P('ctx', 'head'), may hold values from -1.5 to 0, as said below
- write_strength: float32 [8192, 32], P('ctx', 'head'), may hold values from 0 to 1
- segment_ids: int32 [8192], P('ctx'), may hold values from 0 to 3, never falling along the last dimension, each value on 1 to 4096 neighbouring positions
- head_order: int32 [32], replicated, may hold values from 0 to 31, each once
- out_weight: bfloat16 [4096, 2048], P('head'), may hold values from -0.09375 to 0.09375
Outputs:
- layer_out: bfloat16 [8192, 2048], P(('ctx', 'head'))
- decode_states: float32 [32, 16384], P('head', 'ctx')
Inputs may be any that keep to these rules, and one draw needn't show every extreme that they name: `log_decay`: Negative.
All inputs are finite; a program needn't handle non-finite values.
Results may differ from a plain program's by a relative error of at most 0.0049.
Values may be sent and summed in bfloat16 or wider, within the bound.
No kernel may reach another device: no remote copies, remote signals or barrier semaphores. Data moves between devices by JAX's collectives and lax.ppermute only.
A program may use at most 192 MiB of HBM per device.

v0:
```python
import jax
import jax.numpy as jnp
from jax import lax
from jax.sharding import PartitionSpec as P

DK = 128
DV = 128
BLOCK = 64


highest = lax.Precision.HIGHEST
norm_eps = 1e-06


def prefix(x, axis, combine, identity):
    peers, index = (lax.axis_size(axis), lax.axis_index(axis))
    everything = jax.tree.map(lambda part: lax.all_gather(part, axis), x)
    start = jax.tree.map(
        lambda part, zero: jnp.broadcast_to(jnp.asarray(zero, part.dtype), part.shape), x, identity
    )

    def step(k, before):
        reached = k < index
        new = combine(before, jax.tree.map(lambda part: part[k], everything))
        return jax.tree.map(lambda a, b: jnp.where(reached, a, b), new, before)

    return lax.fori_loop(0, peers, step, start)


def product(form, left, right):
    return jnp.einsum(form, left, right, precision=highest)


def unit_rows(raw_rows, scaling):
    widened = raw_rows.astype(jnp.float32)
    return (
        widened * lax.rsqrt(jnp.sum(widened * widened, axis=-1, keepdims=True) + norm_eps) * scaling
    )


def gated_norm(attention, gate_rows):
    mean_square = jnp.mean(attention * attention, axis=-1, keepdims=True)
    gated = (
        attention * lax.rsqrt(mean_square + norm_eps) * jax.nn.silu(gate_rows.astype(jnp.float32))
    )
    return gated.astype(jnp.bfloat16)


def inverse_unit_lower(coupling):
    block_size = coupling.shape[-1]
    identity_matrix = jnp.eye(block_size, dtype=jnp.float32)
    inverse = identity_matrix - coupling
    squared = coupling
    for doubling in range(block_size.bit_length() - 2):
        squared = product("...ij,...jk->...ik", squared, squared)
        inverse = product("...ij,...jk->...ik", inverse, identity_matrix + squared)
    return inverse


def block_parts(query_part, key_part, value_part, decay_rows, strength_rows, doc_rows, doc_before):
    block_size = doc_rows.shape[-1]
    token_positions = jnp.arange(block_size)
    causal = token_positions[:, None] >= token_positions[None, :]
    strict = token_positions[:, None] > token_positions[None, :]
    same_doc = (doc_rows[..., :, None] == doc_rows[..., None, :]) & causal
    continues = doc_rows == doc_before[..., None]
    cumulative = jnp.cumsum(decay_rows, axis=-1)
    decay_gap = cumulative[..., :, None] - cumulative[..., None, :]
    mixing = jnp.where(same_doc[..., None, :, :], jnp.exp(jnp.minimum(decay_gap, 0.0)), 0.0)
    entry_decay = jnp.where(continues[..., None, :], jnp.exp(cumulative), 0.0)
    key_intersection = product("...id,...jd->...ij", key_part, key_part)
    coupling = jnp.where(strict, strength_rows[..., :, None] * mixing * key_intersection, 0.0)
    inverse = inverse_unit_lower(coupling)
    weighted = product(
        "...ij,...jd->...id", inverse, (strength_rows * entry_decay)[..., None] * key_part
    )
    pseudo_values = product("...ij,...jd->...id", inverse, strength_rows[..., None] * value_part)
    masked_scores = mixing * product("...id,...jd->...ij", query_part, key_part)
    local_out = product("...ij,...jd->...id", masked_scores, pseudo_values)
    state_read = entry_decay[..., None] * query_part - product(
        "...ij,...jd->...id", masked_scores, weighted
    )
    last_keys = mixing[..., -1, :, None] * key_part
    identity_map = jnp.eye(key_part.shape[-1], dtype=jnp.float32)
    transition = entry_decay[..., -1, None, None] * identity_map - product(
        "...jd,...je->...de", last_keys, weighted
    )
    written = product("...jd,...je->...de", last_keys, pseudo_values)
    return (local_out, state_read, transition, written)


def combine_spans(earlier, later):
    linked = jnp.where((earlier[3] < 0) | (later[2] < 0) | (earlier[3] == later[2]), 1.0, 0.0)
    through = linked * product("hde,hef->hdf", later[0], earlier[0])
    reached = linked * product("hde,hef->hdf", later[0], earlier[1]) + later[1]
    first_doc = jnp.where(earlier[2] >= 0, earlier[2], later[2])
    last_doc = jnp.where(later[3] >= 0, later[3], earlier[3])
    return (through, reached, first_doc, last_doc)


def per_device(
    queries, keys, values, out_gate, log_decay, write_strength, segment_ids, head_order, out_weight
):
    tok_rows = queries.shape[0]
    heads_here = values.shape[1] // DV
    key_groups = queries.shape[1] // DK
    group_size = heads_here // key_groups
    blocks = tok_rows // BLOCK

    def head_major(raw_rows, scaling):
        unit_part = unit_rows(raw_rows.reshape(blocks, BLOCK, key_groups, DK), scaling)
        return jnp.repeat(unit_part, group_size, axis=2).transpose(0, 2, 1, 3)

    query_part = head_major(queries, DK ** (-0.5))
    key_part = head_major(keys, 1.0)
    value_part = (
        values.reshape(blocks, BLOCK, heads_here, DV).astype(jnp.float32).transpose(0, 2, 1, 3)
    )
    decay_rows = log_decay.reshape(blocks, BLOCK, heads_here).transpose(0, 2, 1)
    strength_rows = write_strength.reshape(blocks, BLOCK, heads_here).transpose(0, 2, 1)
    doc_blocks = segment_ids.reshape(blocks, BLOCK)
    doc_before = jnp.concatenate([doc_blocks[:1, 0], doc_blocks[:-1, -1]])
    local_out, state_read, transition, written = block_parts(
        query_part, key_part, value_part, decay_rows, strength_rows, doc_blocks, doc_before
    )
    identity_map = jnp.broadcast_to(jnp.eye(DK, dtype=jnp.float32), (heads_here, DK, DK))
    zero_state = jnp.zeros((heads_here, DK, DV), jnp.float32)

    def compose_only(carried, pieces):
        through, reached = carried
        step_map, step_add = pieces
        updated = (
            product("hde,hef->hdf", step_map, through),
            product("hde,hef->hdf", step_map, reached) + step_add,
        )
        return (updated, None)

    (whole_map, whole_add), ignored = lax.scan(
        compose_only, (identity_map, zero_state), (transition, written)
    )
    first_doc = doc_blocks[0, 0].astype(jnp.float32)
    last_doc = doc_blocks[-1, -1].astype(jnp.float32)
    identity = (identity_map, zero_state, jnp.float32(-1.0), jnp.float32(-1.0))
    before = prefix((whole_map, whole_add, first_doc, last_doc), "ctx", combine_spans, identity)
    linked = jnp.where((before[3] < 0) | (before[3] == first_doc), 1.0, 0.0)
    incoming = linked * before[1]

    def advance(carried, pieces):
        block_out, block_read, step_map, step_add = pieces
        attention_block = block_out + product("hid,hde->hie", block_read, carried)
        return (product("hde,hef->hdf", step_map, carried) + step_add, attention_block)

    final_state, attention = lax.scan(
        advance, incoming, (local_out, state_read, transition, written)
    )
    tokens_major = attention.transpose(0, 2, 1, 3).reshape(tok_rows, heads_here, DV)
    normed = gated_norm(tokens_major, out_gate.reshape(tok_rows, heads_here, DV)).reshape(
        tok_rows, heads_here * DV
    )
    summed = lax.psum_scatter(
        jnp.dot(normed, out_weight, preferred_element_type=jnp.float32),
        "head",
        scatter_dimension=0,
        tiled=True,
    )
    layer_out = summed.astype(jnp.bfloat16)
    groups = lax.axis_size("ctx")
    is_last = jnp.where(lax.axis_index("ctx") == groups - 1, 1.0, 0.0).astype(jnp.float32)
    own_columns = lax.psum_scatter(
        final_state.reshape(heads_here, DK * DV) * is_last, "ctx", scatter_dimension=1, tiled=True
    )
    every_head = lax.all_gather(own_columns, "head", axis=0, tiled=True)
    order_here = lax.dynamic_slice_in_dim(
        head_order, lax.axis_index("head") * heads_here, heads_here, 0
    )
    selector = (
        order_here[:, None] == jnp.arange(every_head.shape[0], dtype=jnp.int32)[None, :]
    ).astype(jnp.float32)
    decode_states = product("jh,hw->jw", selector, every_head)
    return (layer_out, decode_states)


def solution(mesh):
    in_specs = (
        P("ctx", "head"),
        P("ctx", "head"),
        P("ctx", "head"),
        P("ctx", "head"),
        P("ctx", "head"),
        P("ctx", "head"),
        P("ctx"),
        P(),
        P("head", None),
    )
    out_specs = (P(("ctx", "head"), None), P("head", "ctx"))
    return jax.shard_map(
        per_device, mesh=mesh, in_specs=in_specs, out_specs=out_specs, check_vma=False
    )
```

profile of v0, /device:TPU:1, one launch (start us, length us, event | category | flops | bytes accessed | tf_op | source)
XLA Modules:
  0.0 864.1 jit_solution(3925038144044435149)
XLA Ops:
  25.0 2.2 fusion.47
  27.2 2.0 convolution_subtract_fusion
  29.3 6.4 while.42
  41.5 132.0 %all-reduce.2 = (f32[64]{0:T(128)S(1)}, f32[64]{0:T(128)S(1)}) all-reduce(f32[64]{0:T(128)S(1)} %bitcast_dynamic-update-slice_fusion.1, f32[64]{0:T(128)S(1)} %bitcast_dynamic-update-slice_fusion), channel_id=2, replica_groups=mesh['ctx'=64,'head'=4] {'ctx'}, use_global_device_ids=true, to_apply=%add | all-reduce | flops 128 | bytes 1024 | tf_op jit(solution)/shard_map/all_gather | solution.py:17
  174.5 2.5 fusion.73
  177.0 2.5 convolution_subtract_fusion.1
  179.5 2.8 all-gather.9.cloned.1.call-done
  182.3 141.5 %all-gather.7.cloned.1.call-done = f32[512,128,128]{2,1,0:T(8,128)} async-done(((f32[8,128,128]{2,1,0:T(8,128)}), f32[512,128,128]{2,1,0:T(8,128)}) %all-gather.7.cloned.1.call-update) | async-done | bytes 33554448 | tf_op jit(solution)/shard_map/all_gather | solution.py:17
  323.8 362.5 %while.43 = (s32[]{:T(128)}, f32[8,128,128]{2,1,0:T(8,128)S(1)}, f32[]{:T(128)}, s32[]{:T(128)}, f32[64]{0:T(128)S(1)}, /*index=5*/f32[64,8,128,128]{3,2,1,0:T(8...) while((s32[]{:T(128)}, f32[8,128,128]{2,1,0:T(8,128)S(1)}, ...), condition=%wide.region_5.6_spmd.clone, body=%wide.region_4.5_spmd.clone.sunk | while | flops 201981968 | bytes 3673336 | solution.py:27
  327.6 1.9 fusion.131
  333.2 1.9 fusion.131
  355.9 1.9 fusion.131
  384.2 1.9 fusion.131
  457.8 1.9 fusion.131
  531.5 1.9 fusion.131
  605.1 1.9 fusion.131
  678.8 1.9 fusion.131
  686.4 6.1 while.41
  686.5 2.3 fusion.123
  689.5 2.3 fusion.123
  696.6 4.1 fusion.50
  700.8 124.3 %reduce-scatter.5.cloned.1.call-done = f32[8,256]{1,0:T(8,128)} async-done(((f32[8,16384]{1,0:T(8,128)}), f32[8,256]{1,0:T(8,128)}) %reduce-scatter.5.cloned.1.call-update) | async-done | bytes 8208 | tf_op jit(solution)/shard_map/reduce_scatter | solution.py:169
  825.1 9.6 %all_gather.35 = f32[32,256]{1,0:T(8,128)S(1)} all-gather(f32[8,256]{1,0:T(8,128)} %reduce-scatter.5.cloned.1.call-done), channel_id=1, replica_groups=mesh['ctx'=64,'head'=4] {'head'}, dimensions={0}, use_global_device_ids=true | all-gather | bytes 40960 | tf_op jit(solution)/shard_map/all_gather | solution.py:172
  835.5 20.5 %reduce-scatter.3.cloned.1.call-done = f32[32,2048]{1,0:T(8,128)} async-done(((f32[128,2048]{1,0:T(8,128)}), f32[32,2048]{1,0:T(8,128)}) %reduce-scatter.3.cloned.1.call-update) | async-done | bytes 262160 | tf_op jit(solution)/shard_map/reduce_scatter | solution.py:160
  (346 shorter events, 221.8 us)
Async XLA Ops:
  7.2 32.2 %copy-start.5 = (u32[256]{0:T(256)S(1)}, u32[256]{0:T(256)}, u32[]{:S(2)}) copy-start(u32[256]{0:T(256)} %constant.95) | copy-start | bytes 3076
  7.2 175.2 %all-gather.9.cloned.1.call-start = ((), (), s32[]{:S(2)}) async-start(), calls=%async_computation.5 | async-start | bytes 34078720 | tf_op jit(solution)/shard_map/all_gather | solution.py:17
  23.5 3.7 copy-start.2
  24.2 0.8 copy-start.1
  35.7 0.8 copy-start
  35.7 665.0 %copy-start.4 = (s32[32]{0:T(128)S(1)}, s32[32]{0:T(128)}, u32[]{:S(2)}) copy-start(s32[32]{0:T(128)} %param.22) | copy-start | bytes 388
  35.7 288.1 %all-gather.7.cloned.1.call-start = ((), (), s32[]{:S(2)}) async-start(), calls=%async_computation.4 | async-start | bytes 34078720 | tf_op jit(solution)/shard_map/all_gather | solution.py:17
  36.5 788.6 %reduce-scatter.5.cloned.1.call-start = ((), (), s32[]{:S(2)}) async-start(), calls=%async_computation.3 | async-start | bytes 532480 | tf_op jit(solution)/shard_map/reduce_scatter | solution.py:169
  173.6 523.1 %copy-start.3 = (bf16[128,1024]{1,0:T(8,128)(2,1)S(1)}, bf16[128,1024]{1,0:T(8,128)(2,1)}, u32[]{:S(2)}) copy-start(bf16[128,1024]{1,0:T(8,128)(2,1)} %param.18) | copy-start | bytes 786436
  693.7 162.3 %reduce-scatter.3.cloned.1.call-start = ((), (), s32[]{:S(2)}) async-start(), calls=%async_computation.2 | async-start | bytes 1310720 | tf_op jit(solution)/shard_map/reduce_scatter | solution.py:160
Sparse Core Ops, SparseCore 0:
  35.9 146.4 all-gather.8
  185.1 138.6 all-gather.6
  693.8 131.2 reduce-scatter.4
  827.5 28.3 reduce-scatter.2
where the time goes:
time: 869 us; the launch traced here: 864 us
  waiting for transfers between devices  289 us (33%)
  loops' own time  163 us (19%)
  matrix products  155 us (18%)
  blocking collectives  142 us (16%)
  local copies, waits for them, and re-layouts  92.9 us (11%)
  between operations  15.6 us (2%)
    another operation x1, loops' own time, prefix(): return lax.fori_loop(0, peers, step, start)  163 us
    dot_general x91, matrix products, product(): return jnp.einsum(form, left, right, precision=highest)  151 us
    all_gather x2, waiting for transfers between devices, prefix(): everything = jax.tree.map(lambda part: lax.all_gather(part, axis), x)  144 us
    all_gather x1, blocking collectives, prefix(): everything = jax.tree.map(lambda part: lax.all_gather(part, axis), x)  132 us
    reduce_scatter x1, waiting for transfers between devices, per_device(): lax.psum_scatter(final_state.reshape(heads_here, DK * DV) * is_last, 'ctx...  124 us
    dynamic_slice x128, local copies, waits for them, and re-layouts, step(): new = combine(before, jax.tree.map(lambda part: part[k], everything))  76.6 us
    reduce_scatter x1, waiting for transfers between devices, per_device(): lax.psum_scatter(jnp.dot(normed, out_weight, preferred_element_type=jnp.f...  20.5 us
  transfers between devices with their start and end apart: 4, of which 4 were waited for; matrix products, arithmetic and copies ran while one was open for 2% of the time, Pallas kernels for 0%

commit v1 on v0

v1 whole, which is shorter than its diff:
```python
import jax
import jax.numpy as jnp
from jax import lax
from jax.experimental import pallas as pl
from jax.experimental.pallas import tpu as pltpu
from jax.sharding import PartitionSpec as P

f32 = jnp.float32
bf16 = jnp.bfloat16
DK = 128
DV = 128
N = 128
ROWS = N + 16
EPS = 1e-06


def mm(a, b):
    return jnp.dot(a, b, preferred_element_type=f32)


def split(x):
    hi = x.astype(bf16)
    return hi, (x - hi.astype(f32)).astype(bf16)


def mm_left(a, b):
    hi, lo = split(a)
    return mm(jnp.concatenate([hi, lo], 1), jnp.concatenate([b, b], 0))


def mm_right(a, b):
    hi, lo = split(b)
    return mm(jnp.concatenate([a, a], 1), jnp.concatenate([hi, lo], 0))


def mm_both(a, b):
    ah, al = split(a)
    bh, bl = split(b)
    return mm(jnp.concatenate([ah, al], 1), jnp.concatenate([bh, bh], 0)) + mm(ah, bl)


def iota(shape, axis):
    return lax.broadcasted_iota(jnp.int32, shape, axis)


def places():
    ctx = lax.axis_index("ctx")
    return ctx % 2, (ctx // 2) % 4, (ctx // 8) % 2, ctx // 16


def lines(shape, values):
    row = iota(shape, 0)
    out = jnp.zeros(shape, f32)
    for i, value in enumerate(values):
        out = jnp.where(row == i, jnp.broadcast_to(value[:, :1], shape), out)
    return out


def pack_wide(ref, at, c, d, b, first, last):
    ref[at + (pl.ds(0, N), pl.ds(0, DK))] = d
    ref[at + (pl.ds(0, N), pl.ds(DK, DV))] = b
    ref[at + (pl.ds(N, 8), slice(None))] = lines((8, 256), (c, first, last))


def parse_wide(block):
    tail = block[N:, :DK]
    return tail[0:1], block[:N, :DK], block[:N, DK:], tail[1:2], tail[2:3]


def pack(ref, c, d, b, first, last):
    c0 = c.astype(bf16).astype(f32)
    c1 = (c - c0).astype(bf16).astype(f32)
    ref[:N, :DK] = d.astype(bf16)
    hi = b.astype(bf16)
    ref[:N, DK : 2 * DK] = hi
    if ref.shape[1] > 2 * DK:
        ref[:N, 2 * DK :] = (b - hi.astype(f32)).astype(bf16)
    ref[N:] = lines((16, ref.shape[1]), (c0, c1, c - c0 - c1, first, last)).astype(bf16)


def parse(block):
    tail = block[N:, :DK].astype(f32)
    c = tail[0:1] + tail[1:2] + tail[2:3]
    b = block[:N, DK : 2 * DK].astype(f32)
    if block.shape[1] > 2 * DK:
        b = b + block[:N, 2 * DK :].astype(f32)
    return c, block[:N, :DK], b, tail[3:4], tail[4:5]


def times(d, x):
    return mm_right(d, x) if d.dtype == bf16 else mm_both(d, x)


def compose(earlier, later):
    ce, de, be, fe, le = earlier
    cl, dl, bl, fl, ll = later
    link = jnp.where(le == fl, 1.0, 0.0)
    de = de.astype(f32)
    moved = times(dl, jnp.concatenate([de, be], 1))
    cl = cl * link
    d = cl * de + (link * ce) * dl.astype(f32) - link * moved[:, :DK]
    b = cl * be - link * moved[:, DK:] + bl
    return cl * ce, d, b, fe, ll


def apply_map(parts, link, state):
    c, d, b = parts[:3]
    return link * (c * state - times(d, state) + b)


def inverses(couplings):
    ii, jj = iota((N, N), 0), iota((N, N), 1)
    eye = jnp.where(ii == jj, 1.0, 0.0)
    inside = (ii // 16) == (jj // 16)
    squared = [jnp.where(inside, c, 0.0) for c in couplings]
    inv = [eye - s for s in squared]
    for _ in range(3):
        squared = [mm_both(s, s) for s in squared]
        inv = [x + mm_both(x, s) for x, s in zip(inv, squared)]
    for size in (16, 32, 64):
        ring = ((ii // (2 * size)) == (jj // (2 * size))) & ((ii // size) != (jj // size))
        below = [mm_both(jnp.where(ring, c, 0.0), x) for c, x in zip(couplings, inv)]
        inv = [x - mm_both(x, y) for x, y in zip(inv, below)]
    return inv


def masks(seg_ref):
    ii, jj = iota((N, N), 0), iota((N, N), 1)
    doc_row = jnp.broadcast_to(seg_ref[...].astype(f32), (N, N))
    doc_col = doc_row.T
    return ii, jj, doc_row, doc_col


def local_maps(q_ref, k_ref, v_ref, g_ref, b_ref, seg_ref, own, send, mixes, both, reads, pay):
    core = places()[0]
    ii, jj, doc_row, doc_col = masks(seg_ref)
    same = (doc_row == doc_col) & (ii >= jj)
    strict = same & (ii > jj)
    cont_row = doc_row[0:1] == doc_col[0:1]
    cont_col = doc_col[:, 0:1] == doc_row[:, 0:1]
    last_col = doc_col[:, 0:1] == doc_row[:, N - 1 : N]
    first_doc, last_doc = doc_col[0:1], doc_col[N - 1 : N]
    upper = jnp.where(ii <= jj, 1.0, 0.0).astype(bf16)
    g = g_ref[...]
    beta = b_ref[...]
    g0 = g.astype(bf16)
    g1 = (g - g0.astype(f32)).astype(bf16)
    g2 = (g - g0.astype(f32) - g1.astype(f32)).astype(bf16)
    rows = mm(g0, upper) + mm(g1, upper) + mm(g2, upper)
    heads = g.shape[0]
    groups = heads // 2
    ks = [k_ref[:, i * DK : (i + 1) * DK] for i in range(groups)]
    qs = [q_ref[:, i * DK : (i + 1) * DK] for i in range(groups)]

    def unit(x):
        x = x.astype(f32)
        return lax.rsqrt(jnp.sum(x * x, axis=-1, keepdims=True) + EPS)

    cols = jnp.concatenate([rows, beta, jnp.zeros((N - 2 * heads, N), f32)], 0).T
    cum = cols[:, :heads]
    rk = [unit(k) for k in ks]
    rq = [unit(q) * DK ** (-0.5) for q in qs]
    rk_row = [jnp.broadcast_to(r, (N, N)).T[0:1] for r in rk]
    kts = [k.astype(f32).T.astype(bf16) for k in ks]
    kk = [mm(k, kt) for k, kt in zip(ks, kts)]
    qk = [mm(q, kt) for q, kt in zip(qs, kts)]
    couplings = []
    for h in range(heads):
        i = h // 2
        gap = cum[:, h : h + 1] - rows[h : h + 1]
        mix = jnp.where(same, jnp.exp(jnp.minimum(gap, 0.0)), 0.0) * rk_row[i]
        couplings.append(jnp.where(strict, (cols[:, heads + h : heads + h + 1] * rk[i]) * (mix * kk[i]), 0.0))
        mixes[h] = rq[i] * (mix * qk[i])
    inv = inverses(couplings)
    for h in range(heads):
        i = h // 2
        entry_row = jnp.where(cont_row, jnp.exp(rows[h : h + 1]), 0.0)
        entry_col = jnp.where(cont_col, jnp.exp(cum[:, h : h + 1]), 0.0)
        beta_row = beta[h : h + 1]
        weighted = mm_left(inv[h] * (beta_row * entry_row * rk_row[i]), ks[i])
        pseudo = mm_left(inv[h] * beta_row, v_ref[:, h * DV : (h + 1) * DV])
        pair = jnp.concatenate([weighted, pseudo], 1)
        both[h] = pair
        reads[h] = (entry_col * rq[i]) * qs[i].astype(f32)
        last_gap = jnp.minimum(cum[N - 1 : N, h : h + 1] - cum[:, h : h + 1], 0.0)
        last_keys = jnp.where(last_col, jnp.exp(last_gap), 0.0) * rk[i]
        written = mm_right(kts[i], last_keys * pair)
        pack_wide(pay, (h,), entry_row[:, N - 1 :], written[:, :DK], written[:, DK:], first_doc, last_doc)
    half = heads // 2
    own[...] = pay[pl.ds(core * half, half)]
    send[...] = pay[pl.ds((1 - core) * half, half)]


def local_reads(mixes, both, reads, gate, local, read, silu):
    for h in range(mixes.shape[0]):
        mixed = mm_both(mixes[h], both[h])
        local[h] = mixed[:, DK:]
        read[h] = reads[h] - mixed[:, :DK]
        z = gate[:, h * DV : (h + 1) * DV].astype(f32)
        silu[:, h * DV : (h + 1) * DV] = z / (1.0 + jnp.exp(-z))


def pair_maps(own, got, *refs):
    outs, pair = refs[:4], refs[4]
    core, low, high, _ = places()
    pair[core] = own[...]
    pair[1 - core] = got[...]
    for s in range(4):
        j = low ^ s ^ (2 * high)
        pack(outs[s], *compose(parse_wide(pair[0, j]), parse_wide(pair[1, j])))


def quad_maps(m0, m1, m2, m3, total, prefix, prefix_row, maps):
    low = places()[1]
    for s, m in enumerate((m0, m1, m2, m3)):
        maps[low ^ s] = m[...]
    c, d, b, first, last = parse(maps[0])
    current = (c, d.astype(f32), b, first, last)
    for t in range(3):
        later = parse(maps[t + 1])
        prefix[t, :, :DK] = current[1]
        prefix[t, :, DK:] = current[2]
        row = iota((8, DK), 0)
        link = jnp.where(current[4] == later[3], 1.0, 0.0)
        prefix_row[t] = jnp.where(row == 0, current[0], link)
        current = compose(current, later)
    pack(total, *current)


def row_map(own, got, out, maps):
    high = places()[2]
    maps[high] = own[...]
    maps[1 - high] = got[...]
    pack(out, *compose(parse(maps[0]), parse(maps[1])))


def scan_states(r0, r1, r2, r3, own, got, prefix, prefix_row, o0, o1, o2, o3, maps, halves, final, pay):
    _, low, high, y = places()
    for s, r in enumerate((r0, r1, r2, r3)):
        maps[(y + 4 - s) % 4] = r[...]
    halves[high] = own[...]
    halves[1 - high] = got[...]
    state = jnp.zeros((DK, DV), f32)
    incoming = state
    before = jnp.full((1, DK), -1.0, f32)
    for t in range(4):
        row = parse(maps[t])
        entering = jnp.where(before == row[3], 1.0, 0.0) * state
        incoming = jnp.where(y == t, entering, incoming)
        state = apply_map(row, 1.0, entering)
        before = row[4]
    final[...] = state
    first_half = parse(halves[0])
    link = jnp.where(first_half[4] == parse(halves[1])[3], 1.0, 0.0)
    start = jnp.where(high == 1, apply_map(first_half, link, incoming), incoming)
    for t in range(4):
        here = start
        if t:
            c, link = prefix_row[t - 1, 0:1], prefix_row[t - 1, 1:2]
            here = apply_map((c, prefix[t - 1, :, :DK], prefix[t - 1, :, DK:]), link, start)
        pay[t, :DK] = here.astype(bf16)
        rows = final[pl.ds(4 * (y * 8 + high * 4 + t), 4)]
        hi = rows.astype(bf16).astype(f32)
        pay[t, DK:] = jnp.concatenate([hi, rows - hi, jnp.zeros((8, DV), f32)], 0).astype(bf16)
    for s, o in enumerate((o0, o1, o2, o3)):
        o[...] = pay[low ^ s]


def pair_states(s0, s1, s2, s3, own, got, own_out, send_out, pair, states, starts):
    core, low, high, _ = places()
    pair[core] = own[...]
    pair[1 - core] = got[...]
    for s, ref in enumerate((s0, s1, s2, s3)):
        starts[low ^ s ^ (2 * high)] = ref[...]
    for j in range(own.shape[0]):
        c, d, b, first, last = parse_wide(pair[0, j])
        link = jnp.where(last == parse_wide(pair[1, j])[3], 1.0, 0.0)
        start = starts[j, :DK]
        states[0, j, :DK] = start.astype(f32)
        states[1, j, :DK] = link * (c * start.astype(f32) - mm_left(d, start) + b)
        rows = starts[j, DK:].astype(f32)
        rows = jnp.concatenate([rows[:4] + rows[4:8], rows[8:12]], 0)
        states[0, j, DK:] = rows
        states[1, j, DK:] = rows
    own_out[...] = states[core]
    send_out[...] = states[1 - core]


def project(own, got, local, read, silu, w, acc, o1, o2, o3, tail, states, normed, total):
    core = places()[0]
    x = lax.axis_index("head")
    half = own.shape[0]
    states[pl.ds(core * half, half)] = own[...]
    states[pl.ds((1 - core) * half, half)] = got[...]
    finals = []
    for h in range(2 * half):
        attention = local[h] + mm_both(read[h], states[h, :DK])
        mean_square = jnp.mean(attention * attention, axis=-1, keepdims=True)
        gated = attention * lax.rsqrt(mean_square + EPS) * silu[:, h * DV : (h + 1) * DV]
        normed[:, h * DV : (h + 1) * DV] = gated.astype(bf16)
        rows = states[h, DK:]
        finals.append(jnp.where(core == 0, rows[0:2], rows[2:4]))
    finals = jnp.concatenate(finals, 0)
    hi = finals.astype(bf16).astype(f32)
    tail[...] = jnp.concatenate([hi, finals - hi], 0).astype(bf16)
    total[...] = mm(normed[...], w[...])
    acc[...] = total[pl.ds(x * 32, 32)]
    width = total.shape[1]
    for s, o in enumerate((o1, o2, o3)):
        o[:, :width] = total[pl.ds((x ^ (s + 1)) * 32, 32)].astype(bf16)
        o[:, width:] = tail[...]


def finish(order, acc, r1, r2, r3, tail, out, decode, final):
    x = lax.axis_index("head")
    total = acc[...]
    width = total.shape[1]
    for r in (r1, r2, r3):
        total = total + r[:, :width].astype(f32)
    out[...] = total.astype(bf16)
    slots = decode.shape[0]
    for s, block in enumerate((tail[...], r1[:, width:], r2[:, width:], r3[:, width:])):
        block = block.astype(f32)
        rows = block[:16] + block[16:]
        for h in range(slots):
            line = jnp.concatenate([rows[2 * h : 2 * h + 1], rows[2 * h + 1 : 2 * h + 2]], 1)
            final[pl.ds((x ^ s) * slots + h, 1)] = line
    for i in range(slots):
        decode[i : i + 1] = final[pl.ds(order[x * slots + i], 1)]


def shape(dims, dtype=bf16):
    return pltpu.VMEM(dims, dtype)


def call(kernel, outs, scratch, *args, name, smem=0, hbm=(), flops=None):
    specs = [pl.BlockSpec(memory_space=pltpu.SMEM)] * smem
    specs += [pl.BlockSpec(memory_space=pltpu.VMEM)] * (len(args) - smem)
    args = [
        a if i < smem or i in hbm else pltpu.with_memory_space_constraint(a, pltpu.VMEM)
        for i, a in enumerate(args)
    ]
    cost = None if flops is None else pl.CostEstimate(flops=flops, transcendentals=0, bytes_accessed=0)
    return pl.pallas_call(
        kernel,
        out_shape=outs,
        scratch_shapes=scratch,
        name=name,
        in_specs=specs,
        cost_estimate=cost,
        compiler_params=pltpu.CompilerParams(vmem_limit_bytes=24 * 2**20),
    )(*args)


def xor_peers(count, bit):
    return [(i, i ^ bit) for i in range(count)]


def per_device(
    queries, keys, values, out_gate, log_decay, write_strength, segment_ids, head_order, out_weight
):
    heads = values.shape[1] // DV
    half = heads // 2
    peers = lax.axis_size("ctx")
    model = out_weight.shape[1]
    wide = (N + 8, 256)
    block = (ROWS, 256)
    block3 = (ROWS, 384)
    seg = segment_ids.reshape(1, N)
    own, send, mixes, both, reads = call(
        local_maps,
        [shape((half,) + wide, f32)] * 2
        + [shape((heads, N, N), f32), shape((heads, N, 256), f32), shape((heads, N, DK), f32)],
        [pltpu.VMEM((heads,) + wide, f32)],
        queries, keys, values, log_decay.T, write_strength.T, seg,
        name="local_maps",
    )
    got = lax.ppermute(send, "ctx", xor_peers(peers, 1))
    m0, m1, m2, m3 = call(
        pair_maps,
        [shape(block)] * 4,
        [pltpu.VMEM((2, half) + wide, f32)],
        own, got,
        name="pair_maps",
    )
    m1, m2, m3 = [lax.ppermute(m, "ctx", xor_peers(peers, 2 * s)) for s, m in ((1, m1), (2, m2), (3, m3))]
    local, read, silu = call(
        local_reads,
        [shape((heads, N, DV), f32), shape((heads, N, DK), f32), shape((N, heads * DV), f32)],
        [],
        mixes, both, reads, out_gate,
        name="local_reads",
        flops=2 * 10**9,
    )
    total, prefix, prefix_row = call(
        quad_maps,
        [shape(block3), shape((3, DK, 256), f32), shape((3, 8, DK), f32)],
        [pltpu.VMEM((4,) + block, bf16)],
        m0, m1, m2, m3,
        name="quad_maps",
    )
    total_got = lax.ppermute(total, "ctx", xor_peers(peers, 12))
    r0 = call(
        row_map,
        shape(block3),
        [pltpu.VMEM((2,) + block3, bf16)],
        total, total_got,
        name="row_map",
    )
    r1, r2, r3 = [
        lax.ppermute(r0, "ctx", [(i, (i + 16 * s) % peers) for i in range(peers)]) for s in (1, 2, 3)
    ]
    s0, s1, s2, s3 = call(
        scan_states,
        [shape((ROWS, DV))] * 4,
        [
            pltpu.VMEM((4,) + block3, bf16),
            pltpu.VMEM((2,) + block3, bf16),
            pltpu.VMEM((DK, DV), f32),
            pltpu.VMEM((4, ROWS, DV), bf16),
        ],
        r0, r1, r2, r3, total, total_got, prefix, prefix_row,
        name="scan_states",
    )
    s1, s2, s3 = [lax.ppermute(m, "ctx", xor_peers(peers, 2 * s)) for s, m in ((1, s1), (2, s2), (3, s3))]
    own_state, send_state = call(
        pair_states,
        [shape((half, N + 8, DV), f32)] * 2,
        [
            pltpu.VMEM((2, half) + wide, f32),
            pltpu.VMEM((2, half, N + 8, DV), f32),
            pltpu.VMEM((half, ROWS, DV), bf16),
        ],
        s0, s1, s2, s3, own, got,
        name="pair_states",
    )
    got_state = lax.ppermute(send_state, "ctx", xor_peers(peers, 1))
    acc, o1, o2, o3, tail = call(
        project,
        [shape((32, model), f32)] + [shape((32, model + DV))] * 3 + [shape((32, DV))],
        [
            pltpu.VMEM((heads, N + 8, DV), f32),
            pltpu.VMEM((N, heads * DV), bf16),
            pltpu.VMEM((N, model), f32),
        ],
        own_state, got_state, local, read, silu, out_weight,
        name="project",
    )
    o1, o2, o3 = [lax.ppermute(o, "head", xor_peers(4, s)) for s, o in ((1, o1), (2, o2), (3, o3))]
    return call(
        finish,
        [jax.ShapeDtypeStruct((32, model), bf16), jax.ShapeDtypeStruct((heads, 256), f32)],
        [pltpu.VMEM((4 * heads, 256), f32)],
        head_order, acc, o1, o2, o3, tail,
        name="finish",
        smem=1,
    )


def solution(mesh):
    in_specs = (
        P("ctx", "head"),
        P("ctx", "head"),
        P("ctx", "head"),
        P("ctx", "head"),
        P("ctx", "head"),
        P("ctx", "head"),
        P("ctx"),
        P(),
        P("head", None),
    )
    out_specs = (P(("ctx", "head"), None), P("head", "ctx"))

    def run(*args):
        return tuple(per_device(*args))

    return jax.shard_map(run, mesh=mesh, in_specs=in_specs, out_specs=out_specs, check_vma=False)
```

time: 869 us -> 72.8 us (0.08)
  waiting for transfers between devices: 289 us -> 25.5 us
  loops' own time: 163 us -> 0 us
  matrix products: 155 us -> 0 us
  blocking collectives: 142 us -> 0 us
  local copies, waits for them, and re-layouts: 92.9 us -> 4.79 us
  starting transfers between devices: 0.16 us -> 30.4 us
  between operations: 15.6 us -> 0.72 us
  Pallas kernels: 0 us -> 11.2 us
    another operation x3 -> x0, loops' own time: 163 us -> none  [the longest x1 163 us: prefix(): return lax.fori_loop(0, peers, step, start)]
    dot_general x92 -> x0, matrix products: 155 us -> none  [the longest x91 151 us: product(): return jnp.einsum(form, left, right, precision=highest)]
    reduce_scatter x2 -> x0, waiting for transfers between devices: 145 us -> none  [the longest x1 124 us: per_device(): lax.psum_scatter(final_state.reshape(heads_here, DK * DV) * is_last, 'ctx...]
    all_gather x2 -> x0, waiting for transfers between devices: 144 us -> none  [prefix(): everything = jax.tree.map(lambda part: lax.all_gather(part, axis), x)]
    all_gather x2 -> x0, blocking collectives: 142 us -> none  [the longest x1 132 us: prefix(): everything = jax.tree.map(lambda part: lax.all_gather(part, axis), x)]
    dynamic_slice x129 -> x0, local copies, waits for them, and re-layouts: 76.6 us -> none  [the longest x128 76.6 us: step(): new = combine(before, jax.tree.map(lambda part: part[k], everything))]
    ppermute x0 -> x15, starting transfers between devices: none -> 30.4 us  [the longest x6 7.72 us: per_device(): lax.ppermute(m, 'ctx', xor_peers(peers, 2 * s))]
    ppermute x0 -> x15, waiting for transfers between devices: none -> 25.5 us  [the longest x3 8.61 us: per_device(): lax.ppermute(o, 'head', xor_peers(4, s))]
  transfers between devices with their start and end apart: 4 -> 15, of which waited for: 4 -> 13; matrix products, arithmetic and copies ran while one was open for 2% -> 0% of each run, Pallas kernels for 0% -> 1%
where the time goes in v1:
time: 72.8 us; the launch traced here: 72.6 us
  starting transfers between devices  30.4 us (42%)
  waiting for transfers between devices  25.5 us (35%)
  Pallas kernels  11.2 us (15%)
  local copies, waits for them, and re-layouts  4.79 us (7%)
    pallas_call x9, Pallas kernels, call(): pl.pallas_call(kernel, out_shape=outs, scratch_shapes=scratch, name=name,...  11.2 us
    ppermute x3, waiting for transfers between devices, per_device(): lax.ppermute(o, 'head', xor_peers(4, s))  8.61 us
    ppermute x6, starting transfers between devices, per_device(): lax.ppermute(m, 'ctx', xor_peers(peers, 2 * s))  7.72 us
    ppermute x6, waiting for transfers between devices, per_device(): lax.ppermute(m, 'ctx', xor_peers(peers, 2 * s))  7.14 us
    ppermute x1, starting transfers between devices, per_device(): got_state = lax.ppermute(send_state, 'ctx', xor_peers(peers, 1))  5.98 us
    ppermute x1, starting transfers between devices, per_device(): total_got = lax.ppermute(total, 'ctx', xor_peers(peers, 12))  5.6 us
    ppermute x3, waiting for transfers between devices, per_device(): lax.ppermute(r0, 'ctx', [(i, (i + 16 * s) % peers) for i in range(peers)])  5.25 us
    unnamed x18, local copies, waits for them, and re-layouts  4.79 us
  transfers between devices with their start and end apart: 15, of which 13 were waited for; matrix products, arithmetic and copies ran while one was open for 0% of the time, Pallas kernels for 1%

profile of v1, /device:TPU:1, one launch (start us, length us, event | category | flops | bytes accessed | tf_op | source)
XLA Modules:
  0.0 72.6 jit_solution(9947242702314239687)
XLA Ops:
  5.4 5.6 %local_maps.1 = (f32[4,136,256]{2,1,0:T(8,128)S(1)}, f32[4,136,256]{2,1,0:T(8,128)S(1)}, f32[8,128,128]{2,1,0:T(8,128)S(1)}, f32[8,128,256]{2,1,0:T(8,128)S(1)}, f32[8,128,128]{2,1,0:T(8,128)S(1)}) custom-call(bf16[128,512]{1,0:T(8,128)(2,1)S(1)} %copy-done.2, bf16[128,512]{1,0:T(8,128)(2,1)S(1)} %copy-done.3, bf16[128,1024]{1,0:T(8,128)(2,1)S(1)} %copy-done.1, ...), custom_call_target="tpu_custom_call" | custom-call | tf_op jit(solution)/shard_map/local_maps/pallas_call | solution.py:344
  11.1 3.3 %collective-permute-start = (f32[4,136,256]{2,1,0:T(8,128)S(1)}, f32[4,136,256]{2,1,0:T(8,128)S(1)}, u32[]{:S(2)}, u32[]{:S(2)}) collective-permute-start(f32[4,136,256]{2,1,0:T(8,128)S(1)} %get-tuple-element.29), channel_id=1, source_target_pairs={{0,4},{4,0},{8,12},{12,8},{16,20},{20,16},{24,28},{28,24},{32,36},... | collective-permute-start | bytes 1671176 | tf_op jit(solution)/shard_map/ppermute | solution.py:378
  14.3 1.6 %collective-permute-done.got = f32[4,136,256]{2,1,0:T(8,128)S(1)} collective-permute-done((f32[4,136,256]{2,1,0:T(8,128)S(1)}, f32[4,136,256]{2,1,0:T(8,128)S(1)}, u32[]{:S(2)}, u32[]{:S(2)}) %collective-permute-start) | collective-permute-done | bytes 557088 | tf_op jit(solution)/shard_map/ppermute | solution.py:378
  16.5 2.9 %collective-permute-start.2 = (bf16[144,256]{1,0:T(8,128)(2,1)S(1)}, bf16[144,256]{1,0:T(8,128)(2,1)S(1)}, u32[]{:S(2)}, u32[]{:S(2)}) collective-permute-start(bf16[144,256]{1,0:T(8,128)(2,1)S(1)} %get-tuple-element.32), channel_id=1, source_target_pairs={{0,16},{4,20},{8,24},{12,28},{16,0},{20,4},{24,8},{28,12},{32,48},... | collective-permute-start | bytes 221192 | tf_op jit(solution)/shard_map/ppermute | solution.py:386
  20.0 1.6 %collective-permute-done.2.m2 = bf16[144,256]{1,0:T(8,128)(2,1)S(1)} collective-permute-done((bf16[144,256]{1,0:T(8,128)(2,1)S(1)}, bf16[144,256]{1,0:T(8,128)(2,1)S(1)}, u32[]{:S(2)}, u32[]{:S(2)}) %collective-permute-start.2) | collective-permute-done | bytes 73760 | tf_op jit(solution)/shard_map/ppermute | solution.py:386
  21.7 2.7 %collective-permute-done.3.m3 = bf16[144,256]{1,0:T(8,128)(2,1)S(1)} collective-permute-done((bf16[144,256]{1,0:T(8,128)(2,1)S(1)}, bf16[144,256]{1,0:T(8,128)(2,1)S(1)}, u32[]{:S(2)}, u32[]{:S(2)}) %collective-permute-start.3) | collective-permute-done | bytes 73760 | tf_op jit(solution)/shard_map/ppermute | solution.py:386
  25.0 5.6 %collective-permute-start.4 = (bf16[144,384]{1,0:T(8,128)(2,1)S(1)}, bf16[144,384]{1,0:T(8,128)(2,1)S(1)}, u32[]{:S(2)}, u32[]{:S(2)}) collective-permute-start(bf16[144,384]{1,0:T(8,128)(2,1)S(1)} %get-tuple-element.34.own), channel_id=1, source_target_pairs={{0,48},{4,52},{8,56},{12,60},{16,32},{20,36},{24,40},{28,44},{32,1... | collective-permute-start | bytes 331784 | tf_op jit(solution)/shard_map/ppermute | solution.py:402
  30.5 2.2 %collective-permute-done.4.got = bf16[144,384]{1,0:T(8,128)(2,1)S(1)} collective-permute-done((bf16[144,384]{1,0:T(8,128)(2,1)S(1)}, bf16[144,384]{1,0:T(8,128)(2,1)S(1)}, u32[]{:S(2)}, u32[]{:S(2)}) %collective-permute-start.4) | collective-permute-done | bytes 110624 | tf_op jit(solution)/shard_map/ppermute | solution.py:402
  33.0 2.8 %collective-permute-start.7 = (bf16[144,384]{1,0:T(8,128)(2,1)S(1)}, bf16[144,384]{1,0:T(8,128)(2,1)S(1)}, u32[]{:S(2)}, u32[]{:S(2)}) collective-permute-start(bf16[144,384]{1,0:T(8,128)(2,1)S(1)} %row_map.1.r0), channel_id=1, source_target_pairs={{0,192},{4,196},{8,200},{12,204},{16,208},{20,212},{24,216},{28,22... | collective-permute-start | bytes 331784 | tf_op jit(solution)/shard_map/ppermute | solution.py:411
  36.9 1.8 %collective-permute-done.7.r3 = bf16[144,384]{1,0:T(8,128)(2,1)S(1)} collective-permute-done((bf16[144,384]{1,0:T(8,128)(2,1)S(1)}, bf16[144,384]{1,0:T(8,128)(2,1)S(1)}, u32[]{:S(2)}, u32[]{:S(2)}) %collective-permute-start.7) | collective-permute-done | bytes 110624 | tf_op jit(solution)/shard_map/ppermute | solution.py:411
  38.7 2.3 %collective-permute-done.6.r2 = bf16[144,384]{1,0:T(8,128)(2,1)S(1)} collective-permute-done((bf16[144,384]{1,0:T(8,128)(2,1)S(1)}, bf16[144,384]{1,0:T(8,128)(2,1)S(1)}, u32[]{:S(2)}, u32[]{:S(2)}) %collective-permute-start.6) | collective-permute-done | bytes 110624 | tf_op jit(solution)/shard_map/ppermute | solution.py:411
  41.0 1.1 %collective-permute-done.5.r1 = bf16[144,384]{1,0:T(8,128)(2,1)S(1)} collective-permute-done((bf16[144,384]{1,0:T(8,128)(2,1)S(1)}, bf16[144,384]{1,0:T(8,128)(2,1)S(1)}, u32[]{:S(2)}, u32[]{:S(2)}) %collective-permute-start.5) | collective-permute-done | bytes 110624 | tf_op jit(solution)/shard_map/ppermute | solution.py:411
  42.1 1.0 %scan_states.1 = (bf16[144,128]{1,0:T(8,128)(2,1)S(1)}, bf16[144,128]{1,0:T(8,128)(2,1)S(1)}, bf16[144,128]{1,0:T(8,128)(2,1)S(1)}, bf16[144,128]{1,0:T(8,128)(2,1)S(1)}) custom-call(bf16[144,384]{1,0:T(8,128)(2,1)S(1)} %row_map.1.r0, bf16[144,384]{1,0:T(8,128)(2,1)S(1)} %collective-permute-done.5.r1, bf16[144,384]{1,0:T(8,128)(2,1)S(1)} %collective-permute-done.6.r2, ...), custom_call_target="tpu_custom_call" | custom-call | tf_op jit(solution)/shard_map/scan_states/pallas_call | solution.py:344
  43.1 1.9 %collective-permute-start.8 = (bf16[144,128]{1,0:T(8,128)(2,1)S(1)}, bf16[144,128]{1,0:T(8,128)(2,1)S(1)}, u32[]{:S(2)}, u32[]{:S(2)}) collective-permute-start(bf16[144,128]{1,0:T(8,128)(2,1)S(1)} %get-tuple-element.38), channel_id=1, source_target_pairs={{0,8},{4,12},{8,0},{12,4},{16,24},{20,28},{24,16},{28,20},{32,40},... | collective-permute-start | bytes 110600 | tf_op jit(solution)/shard_map/ppermute | solution.py:425
  45.3 1.8 %collective-permute-start.10 = (bf16[144,128]{1,0:T(8,128)(2,1)S(1)}, bf16[144,128]{1,0:T(8,128)(2,1)S(1)}, u32[]{:S(2)}, u32[]{:S(2)}) collective-permute-start(bf16[144,128]{1,0:T(8,128)(2,1)S(1)} %get-tuple-element.40), channel_id=1, source_target_pairs={{0,24},{4,28},{8,16},{12,20},{16,8},{20,12},{24,0},{28,4},{32,56},... | collective-permute-start | bytes 110600 | tf_op jit(solution)/shard_map/ppermute | solution.py:425
  47.2 1.7 %collective-permute-done.9.s2 = bf16[144,128]{1,0:T(8,128)(2,1)S(1)} collective-permute-done((bf16[144,128]{1,0:T(8,128)(2,1)S(1)}, bf16[144,128]{1,0:T(8,128)(2,1)S(1)}, u32[]{:S(2)}, u32[]{:S(2)}) %collective-permute-start.9) | collective-permute-done | bytes 36896 | tf_op jit(solution)/shard_map/ppermute | solution.py:425
  48.9 1.0 %collective-permute-done.10.s3 = bf16[144,128]{1,0:T(8,128)(2,1)S(1)} collective-permute-done((bf16[144,128]{1,0:T(8,128)(2,1)S(1)}, bf16[144,128]{1,0:T(8,128)(2,1)S(1)}, u32[]{:S(2)}, u32[]{:S(2)}) %collective-permute-start.10) | collective-permute-done | bytes 36896 | tf_op jit(solution)/shard_map/ppermute | solution.py:425
  50.3 6.0 %collective-permute-start.11 = (f32[4,136,128]{2,1,0:T(8,128)S(1)}, f32[4,136,128]{2,1,0:T(8,128)S(1)}, u32[]{:S(2)}, u32[]{:S(2)}) collective-permute-start(f32[4,136,128]{2,1,0:T(8,128)S(1)} %get-tuple-element.42), channel_id=1, source_target_pairs={{0,4},{4,0},{8,12},{12,8},{16,20},{20,16},{24,28},{28,24},{32,36},... | collective-permute-start | bytes 835592 | tf_op jit(solution)/shard_map/ppermute | solution.py:437
  57.5 1.2 %project.1 = (f32[32,2048]{1,0:T(8,128)S(1)}, bf16[32,2176]{1,0:T(8,128)(2,1)S(1)}, bf16[32,2176]{1,0:T(8,128)(2,1)S(1)}, bf16[32,2176]{1,0:T(8,128)(2,1)S(1)}, bf16[32,128]{1,0:T(8,128)(2,1)S(1)}) custom-call(f32[4,136,128]{2,1,0:T(8,128)S(1)} %get-tuple-element.41.own, f32[4,136,128]{2,1,0:T(8,128)S(1)} %collective-permute-done.11.got, ...), custom_call_target="tpu_custom_call" | custom-call | tf_op jit(solution)/shard_map/project/pallas_call | solution.py:344
  58.7 1.3 %collective-permute-start.12 = (bf16[32,2176]{1,0:T(8,128)(2,1)S(1)}, bf16[32,2176]{1,0:T(8,128)(2,1)S(1)}, u32[]{:S(2)}, u32[]{:S(2)}) collective-permute-start(bf16[32,2176]{1,0:T(8,128)(2,1)S(1)} %get-tuple-element.50), channel_id=1, source_target_pairs={{0,1},{1,0},{2,3},{3,2},{4,5},{5,4},{6,7},{7,6},{8,9},{9,8},{10,11... | collective-permute-start | bytes 417800 | tf_op jit(solution)/shard_map/ppermute | solution.py:449
  60.0 2.4 %collective-permute-start.13 = (bf16[32,2176]{1,0:T(8,128)(2,1)S(1)}, bf16[32,2176]{1,0:T(8,128)(2,1)S(1)}, u32[]{:S(2)}, u32[]{:S(2)}) collective-permute-start(bf16[32,2176]{1,0:T(8,128)(2,1)S(1)} %get-tuple-element.51), channel_id=1, source_target_pairs={{0,2},{1,3},{2,0},{3,1},{4,6},{5,7},{6,4},{7,5},{8,10},{9,11},{10,... | collective-permute-start | bytes 417800 | tf_op jit(solution)/shard_map/ppermute | solution.py:449
  63.5 5.2 %collective-permute-done.13.r2 = bf16[32,2176]{1,0:T(8,128)(2,1)S(1)} collective-permute-done((bf16[32,2176]{1,0:T(8,128)(2,1)S(1)}, bf16[32,2176]{1,0:T(8,128)(2,1)S(1)}, u32[]{:S(2)}, u32[]{:S(2)}) %collective-permute-start.13) | collective-permute-done | bytes 139296 | tf_op jit(solution)/shard_map/ppermute | solution.py:449
  68.8 2.5 %collective-permute-done.14.r3 = bf16[32,2176]{1,0:T(8,128)(2,1)S(1)} collective-permute-done((bf16[32,2176]{1,0:T(8,128)(2,1)S(1)}, bf16[32,2176]{1,0:T(8,128)(2,1)S(1)}, u32[]{:S(2)}, u32[]{:S(2)}) %collective-permute-start.14) | collective-permute-done | bytes 139296 | tf_op jit(solution)/shard_map/ppermute | solution.py:449
  71.3 1.3 %finish.1 = (bf16[32,2048]{1,0:T(8,128)(2,1)}, f32[8,256]{1,0:T(8,128)}) custom-call(s32[32]{0:T(128)S(1)} %copy-done.7, f32[32,2048]{1,0:T(8,128)S(1)} %get-tuple-element.49.acc, bf16[32,2176]{1,0:T(8,128)(2,1)S(1)} %collective-permute-done.12.r1, bf16[32,2176]{1,0:T(8,128)(2,1)S(1)} %collective-permute-done.13.r2, ...), custom_call_target="tpu_custom_call" | custom-call | tf_op jit(solution)/shard_map/finish/pallas_call | solution.py:344
  (33 shorter events, 10.7 us)
Async XLA Ops:
  0.6 1.0 %copy-start.1 = (bf16[128,1024]{1,0:T(8,128)(2,1)S(1)}, bf16[128,1024]{1,0:T(8,128)(2,1)}, u32[]{:S(2)}) copy-start(bf16[128,1024]{1,0:T(8,128)(2,1)} %v_ref.1) | copy-start | bytes 786436
  1.6 0.9 %copy-start.2 = (bf16[128,512]{1,0:T(8,128)(2,1)S(1)}, bf16[128,512]{1,0:T(8,128)(2,1)}, u32[]{:S(2)}) copy-start(bf16[128,512]{1,0:T(8,128)(2,1)} %q_ref.1) | copy-start | bytes 393220
  2.5 0.9 %copy-start.3 = (bf16[128,512]{1,0:T(8,128)(2,1)S(1)}, bf16[128,512]{1,0:T(8,128)(2,1)}, u32[]{:S(2)}) copy-start(bf16[128,512]{1,0:T(8,128)(2,1)} %k_ref.1) | copy-start | bytes 393220
  3.4 0.7 copy-start.4
  4.1 0.7 copy-start.5
  4.8 0.7 copy-start.6
  5.4 50.9 %copy-start.8 = (bf16[128,1024]{1,0:T(8,128)(2,1)S(1)}, bf16[128,1024]{1,0:T(8,128)(2,1)}, u32[]{:S(2)}) copy-start(bf16[128,1024]{1,0:T(8,128)(2,1)} %gate.1) | copy-start | bytes 786436
  11.1 4.9 %collective-permute-start = (f32[4,136,256]{2,1,0:T(8,128)S(1)}, f32[4,136,256]{2,1,0:T(8,128)S(1)}, u32[]{:S(2)}, u32[]{:S(2)}) collective-permute-start(f32[4,136,256]{2,1,0:T(8,128)S(1)} %get-tuple-element.29), channel_id=1, source_target_pairs={{0,4},{4,0},{8,12},{12,8},{16,20},{20,16},{24,28},{28,24},{32,36},... | collective-permute-start | bytes 1671176 | tf_op jit(solution)/shard_map/ppermute | solution.py:378
  16.4 3.6 %collective-permute-start.1 = (bf16[144,256]{1,0:T(8,128)(2,1)S(1)}, bf16[144,256]{1,0:T(8,128)(2,1)S(1)}, u32[]{:S(2)}, u32[]{:S(2)}) collective-permute-start(bf16[144,256]{1,0:T(8,128)(2,1)S(1)} %get-tuple-element.31), channel_id=1, source_target_pairs={{0,8},{4,12},{8,0},{12,4},{16,24},{20,28},{24,16},{28,20},{32,40},... | collective-permute-start | bytes 221192 | tf_op jit(solution)/shard_map/ppermute | solution.py:386
  16.5 5.2 %collective-permute-start.2 = (bf16[144,256]{1,0:T(8,128)(2,1)S(1)}, bf16[144,256]{1,0:T(8,128)(2,1)S(1)}, u32[]{:S(2)}, u32[]{:S(2)}) collective-permute-start(bf16[144,256]{1,0:T(8,128)(2,1)S(1)} %get-tuple-element.32), channel_id=1, source_target_pairs={{0,16},{4,20},{8,24},{12,28},{16,0},{20,4},{24,8},{28,12},{32,48},... | collective-permute-start | bytes 221192 | tf_op jit(solution)/shard_map/ppermute | solution.py:386
  19.4 5.0 %collective-permute-start.3 = (bf16[144,256]{1,0:T(8,128)(2,1)S(1)}, bf16[144,256]{1,0:T(8,128)(2,1)S(1)}, u32[]{:S(2)}, u32[]{:S(2)}) collective-permute-start(bf16[144,256]{1,0:T(8,128)(2,1)S(1)} %get-tuple-element.33), channel_id=1, source_target_pairs={{0,24},{4,28},{8,16},{12,20},{16,8},{20,12},{24,0},{28,4},{32,56},... | collective-permute-start | bytes 221192 | tf_op jit(solution)/shard_map/ppermute | solution.py:386
  25.0 7.8 %collective-permute-start.4 = (bf16[144,384]{1,0:T(8,128)(2,1)S(1)}, bf16[144,384]{1,0:T(8,128)(2,1)S(1)}, u32[]{:S(2)}, u32[]{:S(2)}) collective-permute-start(bf16[144,384]{1,0:T(8,128)(2,1)S(1)} %get-tuple-element.34.own), channel_id=1, source_target_pairs={{0,48},{4,52},{8,56},{12,60},{16,32},{20,36},{24,40},{28,44},{32,1... | collective-permute-start | bytes 331784 | tf_op jit(solution)/shard_map/ppermute | solution.py:402
  33.0 5.7 %collective-permute-start.7 = (bf16[144,384]{1,0:T(8,128)(2,1)S(1)}, bf16[144,384]{1,0:T(8,128)(2,1)S(1)}, u32[]{:S(2)}, u32[]{:S(2)}) collective-permute-start(bf16[144,384]{1,0:T(8,128)(2,1)S(1)} %row_map.1.r0), channel_id=1, source_target_pairs={{0,192},{4,196},{8,200},{12,204},{16,208},{20,212},{24,216},{28,22... | collective-permute-start | bytes 331784 | tf_op jit(solution)/shard_map/ppermute | solution.py:411
  35.8 5.2 %collective-permute-start.6 = (bf16[144,384]{1,0:T(8,128)(2,1)S(1)}, bf16[144,384]{1,0:T(8,128)(2,1)S(1)}, u32[]{:S(2)}, u32[]{:S(2)}) collective-permute-start(bf16[144,384]{1,0:T(8,128)(2,1)S(1)} %row_map.1.r0), channel_id=1, source_target_pairs={{0,128},{4,132},{8,136},{12,140},{16,144},{20,148},{24,152},{28,15... | collective-permute-start | bytes 331784 | tf_op jit(solution)/shard_map/ppermute | solution.py:411
  36.2 5.9 %collective-permute-start.5 = (bf16[144,384]{1,0:T(8,128)(2,1)S(1)}, bf16[144,384]{1,0:T(8,128)(2,1)S(1)}, u32[]{:S(2)}, u32[]{:S(2)}) collective-permute-start(bf16[144,384]{1,0:T(8,128)(2,1)S(1)} %row_map.1.r0), channel_id=1, source_target_pairs={{0,64},{4,68},{8,72},{12,76},{16,80},{20,84},{24,88},{28,92},{32,9... | collective-permute-start | bytes 331784 | tf_op jit(solution)/shard_map/ppermute | solution.py:411
  43.1 4.1 %collective-permute-start.8 = (bf16[144,128]{1,0:T(8,128)(2,1)S(1)}, bf16[144,128]{1,0:T(8,128)(2,1)S(1)}, u32[]{:S(2)}, u32[]{:S(2)}) collective-permute-start(bf16[144,128]{1,0:T(8,128)(2,1)S(1)} %get-tuple-element.38), channel_id=1, source_target_pairs={{0,8},{4,12},{8,0},{12,4},{16,24},{20,28},{24,16},{28,20},{32,40},... | collective-permute-start | bytes 110600 | tf_op jit(solution)/shard_map/ppermute | solution.py:425
  45.0 3.9 %collective-permute-start.9 = (bf16[144,128]{1,0:T(8,128)(2,1)S(1)}, bf16[144,128]{1,0:T(8,128)(2,1)S(1)}, u32[]{:S(2)}, u32[]{:S(2)}) collective-permute-start(bf16[144,128]{1,0:T(8,128)(2,1)S(1)} %get-tuple-element.39), channel_id=1, source_target_pairs={{0,16},{4,20},{8,24},{12,28},{16,0},{20,4},{24,8},{28,12},{32,48},... | collective-permute-start | bytes 110600 | tf_op jit(solution)/shard_map/ppermute | solution.py:425
  45.3 4.6 %collective-permute-start.10 = (bf16[144,128]{1,0:T(8,128)(2,1)S(1)}, bf16[144,128]{1,0:T(8,128)(2,1)S(1)}, u32[]{:S(2)}, u32[]{:S(2)}) collective-permute-start(bf16[144,128]{1,0:T(8,128)(2,1)S(1)} %get-tuple-element.40), channel_id=1, source_target_pairs={{0,24},{4,28},{8,16},{12,20},{16,8},{20,12},{24,0},{28,4},{32,56},... | collective-permute-start | bytes 110600 | tf_op jit(solution)/shard_map/ppermute | solution.py:425
  50.0 7.6 %copy-start = (bf16[1024,2048]{1,0:T(8,128)(2,1)S(1)}, bf16[1024,2048]{1,0:T(8,128)(2,1)}, u32[]{:S(2)}) copy-start(bf16[1024,2048]{1,0:T(8,128)(2,1)} %w.1) | copy-start | bytes 12582916
  50.3 7.2 %collective-permute-start.11 = (f32[4,136,128]{2,1,0:T(8,128)S(1)}, f32[4,136,128]{2,1,0:T(8,128)S(1)}, u32[]{:S(2)}, u32[]{:S(2)}) collective-permute-start(f32[4,136,128]{2,1,0:T(8,128)S(1)} %get-tuple-element.42), channel_id=1, source_target_pairs={{0,4},{4,0},{8,12},{12,8},{16,20},{20,16},{24,28},{28,24},{32,36},... | collective-permute-start | bytes 835592 | tf_op jit(solution)/shard_map/ppermute | solution.py:437
  56.8 14.5 %copy-start.7 = (s32[32]{0:T(128)S(1)}, s32[32]{0:T(128)}, u32[]{:S(2)}) copy-start(s32[32]{0:T(128)} %order.1) | copy-start | bytes 388
  58.7 4.8 %collective-permute-start.12 = (bf16[32,2176]{1,0:T(8,128)(2,1)S(1)}, bf16[32,2176]{1,0:T(8,128)(2,1)S(1)}, u32[]{:S(2)}, u32[]{:S(2)}) collective-permute-start(bf16[32,2176]{1,0:T(8,128)(2,1)S(1)} %get-tuple-element.50), channel_id=1, source_target_pairs={{0,1},{1,0},{2,3},{3,2},{4,5},{5,4},{6,7},{7,6},{8,9},{9,8},{10,11... | collective-permute-start | bytes 417800 | tf_op jit(solution)/shard_map/ppermute | solution.py:449
  60.0 8.7 %collective-permute-start.13 = (bf16[32,2176]{1,0:T(8,128)(2,1)S(1)}, bf16[32,2176]{1,0:T(8,128)(2,1)S(1)}, u32[]{:S(2)}, u32[]{:S(2)}) collective-permute-start(bf16[32,2176]{1,0:T(8,128)(2,1)S(1)} %get-tuple-element.51), channel_id=1, source_target_pairs={{0,2},{1,3},{2,0},{3,1},{4,6},{5,7},{6,4},{7,5},{8,10},{9,11},{10,... | collective-permute-start | bytes 417800 | tf_op jit(solution)/shard_map/ppermute | solution.py:449
  62.5 8.8 %collective-permute-start.14 = (bf16[32,2176]{1,0:T(8,128)(2,1)S(1)}, bf16[32,2176]{1,0:T(8,128)(2,1)S(1)}, u32[]{:S(2)}, u32[]{:S(2)}) collective-permute-start(bf16[32,2176]{1,0:T(8,128)(2,1)S(1)} %get-tuple-element.52), channel_id=1, source_target_pairs={{0,3},{1,2},{2,1},{3,0},{4,7},{5,6},{6,5},{7,4},{8,11},{9,10},{10,... | collective-permute-start | bytes 417800 | tf_op jit(solution)/shard_map/ppermute | solution.py:449

commit v2 on v1

--- a/solution.py
+++ b/solution.py
@@ -4,6 +4,7 @@
 from jax.experimental import pallas as pl
 from jax.experimental.pallas import tpu as pltpu
 from jax.sharding import PartitionSpec as P
+
 
 f32 = jnp.float32
 bf16 = jnp.bfloat16
@@ -124,16 +125,10 @@
     return inv
 
 
-def masks(seg_ref):
+def local_maps(heads, groups, q_ref, k_ref, v_ref, g, beta, seg_ref, out, mixes, both, reads):
     ii, jj = iota((N, N), 0), iota((N, N), 1)
     doc_row = jnp.broadcast_to(seg_ref[...].astype(f32), (N, N))
     doc_col = doc_row.T
-    return ii, jj, doc_row, doc_col
-
-
-def local_maps(q_ref, k_ref, v_ref, g_ref, b_ref, seg_ref, own, send, mixes, both, reads, pay):
-    core = places()[0]
-    ii, jj, doc_row, doc_col = masks(seg_ref)
     same = (doc_row == doc_col) & (ii >= jj)
     strict = same & (ii > jj)
     cont_row = doc_row[0:1] == doc_col[0:1]
@@ -141,23 +136,21 @@
     last_col = doc_col[:, 0:1] == doc_row[:, N - 1 : N]
     first_doc, last_doc = doc_col[0:1], doc_col[N - 1 : N]
     upper = jnp.where(ii <= jj, 1.0, 0.0).astype(bf16)
-    g = g_ref[...]
-    beta = b_ref[...]
+    count = g.shape[0]
+    g = jnp.concatenate([g, jnp.zeros((8 - count, N), f32)], 0)
     g0 = g.astype(bf16)
     g1 = (g - g0.astype(f32)).astype(bf16)
     g2 = (g - g0.astype(f32) - g1.astype(f32)).astype(bf16)
     rows = mm(g0, upper) + mm(g1, upper) + mm(g2, upper)
-    heads = g.shape[0]
-    groups = heads // 2
-    ks = [k_ref[:, i * DK : (i + 1) * DK] for i in range(groups)]
-    qs = [q_ref[:, i * DK : (i + 1) * DK] for i in range(groups)]
+    ks = [k_ref[:, pl.ds(pl.multiple_of((groups + i) * DK, DK), DK)] for i in range(count // 2)]
+    qs = [q_ref[:, pl.ds(pl.multiple_of((groups + i) * DK, DK), DK)] for i in range(count // 2)]
 
     def unit(x):
         x = x.astype(f32)
         return lax.rsqrt(jnp.sum(x * x, axis=-1, keepdims=True) + EPS)
 
-    cols = jnp.concatenate([rows, beta, jnp.zeros((N - 2 * heads, N), f32)], 0).T
-    cum = cols[:, :heads]
+    cols = jnp.concatenate([rows, beta, jnp.zeros((N - 8 - count, N), f32)], 0).T
+    cum = cols[:, :count]
     rk = [unit(k) for k in ks]
     rq = [unit(q) * DK ** (-0.5) for q in qs]
     rk_row = [jnp.broadcast_to(r, (N, N)).T[0:1] for r in rk]
@@ -165,39 +158,69 @@
     kk = [mm(k, kt) for k, kt in zip(ks, kts)]
     qk = [mm(q, kt) for q, kt in zip(qs, kts)]
     couplings = []
-    for h in range(heads):
+    for h in range(count):
         i = h // 2
         gap = cum[:, h : h + 1] - rows[h : h + 1]
         mix = jnp.where(same, jnp.exp(jnp.minimum(gap, 0.0)), 0.0) * rk_row[i]
-        couplings.append(jnp.where(strict, (cols[:, heads + h : heads + h + 1] * rk[i]) * (mix * kk[i]), 0.0))
+        couplings.append(jnp.where(strict, (cols[:, 8 + h : 9 + h] * rk[i]) * (mix * kk[i]), 0.0))
         mixes[h] = rq[i] * (mix * qk[i])
     inv = inverses(couplings)
-    for h in range(heads):
+    for h in range(count):
         i = h // 2
         entry_row = jnp.where(cont_row, jnp.exp(rows[h : h + 1]), 0.0)
         entry_col = jnp.where(cont_col, jnp.exp(cum[:, h : h + 1]), 0.0)
         beta_row = beta[h : h + 1]
         weighted = mm_left(inv[h] * (beta_row * entry_row * rk_row[i]), ks[i])
-        pseudo = mm_left(inv[h] * beta_row, v_ref[:, h * DV : (h + 1) * DV])
+        pseudo = mm_left(inv[h] * beta_row, v_ref[:, pl.ds(pl.multiple_of((heads + h) * DV, DV), DV)])
         pair = jnp.concatenate([weighted, pseudo], 1)
         both[h] = pair
         reads[h] = (entry_col * rq[i]) * qs[i].astype(f32)
         last_gap = jnp.minimum(cum[N - 1 : N, h : h + 1] - cum[:, h : h + 1], 0.0)
         last_keys = jnp.where(last_col, jnp.exp(last_gap), 0.0) * rk[i]
         written = mm_right(kts[i], last_keys * pair)
-        pack_wide(pay, (h,), entry_row[:, N - 1 :], written[:, :DK], written[:, DK:], first_doc, last_doc)
-    half = heads // 2
-    own[...] = pay[pl.ds(core * half, half)]
-    send[...] = pay[pl.ds((1 - core) * half, half)]
-
-
-def local_reads(mixes, both, reads, gate, local, read, silu):
-    for h in range(mixes.shape[0]):
-        mixed = mm_both(mixes[h], both[h])
-        local[h] = mixed[:, DK:]
-        read[h] = reads[h] - mixed[:, :DK]
-        z = gate[:, h * DV : (h + 1) * DV].astype(f32)
-        silu[:, h * DV : (h + 1) * DV] = z / (1.0 + jnp.exp(-z))
+        pack_wide(out, (h,), entry_row[:, N - 1 :], written[:, :DK], written[:, DK:], first_doc, last_doc)
+
+
+def send_maps(q, k, v, g, b, seg, out, mixes, both, reads, q_in, k_in, v_in, g_in, b_in, seg_in, sems):
+    moves = [
+        pltpu.make_async_copy(src, dst, sems.at[i])
+        for i, (src, dst) in enumerate(
+            ((seg, seg_in), (g, g_in), (b, b_in), (k, k_in), (q, q_in), (v, v_in))
+        )
+    ]
+    for move in moves:
+        move.start()
+    for move in moves:
+        move.wait()
+    half = out.shape[0]
+    heads = (1 - places()[0]) * half
+    local_maps(
+        heads, heads // 2, q_in, k_in, v_in, g_in[pl.ds(heads, half)], b_in[pl.ds(heads, half)], seg_in,
+        out, mixes, both, reads,
+    )
+
+
+def own_maps(q, k, v, g, b, seg, out, mixes, both, reads):
+    half = out.shape[0]
+    heads = places()[0] * half
+    local_maps(
+        heads, heads // 2, q, k, v, g[pl.ds(heads, half)], b[pl.ds(heads, half)], seg,
+        out, mixes, both, reads,
+    )
+
+
+def local_reads(mixes0, both0, reads0, mixes1, both1, reads1, gate, local, read, silu):
+    core = places()[0]
+    half = mixes0.shape[0]
+    width = half * DV
+    for part, (mixes, both, reads) in enumerate(((mixes0, both0, reads0), (mixes1, both1, reads1))):
+        for h in range(half):
+            mixed = mm_both(mixes[h], both[h])
+            local[part * half + h] = mixed[:, DK:]
+            read[part * half + h] = reads[h] - mixed[:, :DK]
+        first = pl.multiple_of((core ^ part) * width, width)
+        z = gate[:, pl.ds(first, width)].astype(f32)
+        silu[:, part * width : (part + 1) * width] = z / (1.0 + jnp.exp(-z))
 
 
 def pair_maps(own, got, *refs):
@@ -273,7 +296,7 @@
     for s, ref in enumerate((s0, s1, s2, s3)):
         starts[low ^ s ^ (2 * high)] = ref[...]
     for j in range(own.shape[0]):
-        c, d, b, first, last = parse_wide(pair[0, j])
+        c, d, b, _, last = parse_wide(pair[0, j])
         link = jnp.where(last == parse_wide(pair[1, j])[3], 1.0, 0.0)
         start = starts[j, :DK]
         states[0, j, :DK] = start.astype(f32)
@@ -286,19 +309,25 @@
     send_out[...] = states[1 - core]
 
 
-def project(own, got, local, read, silu, w, acc, o1, o2, o3, tail, states, normed, total):
+def project(own, got, local, read, silu, w, acc, o1, o2, o3, tail, normed, total, lasts):
     core = places()[0]
     x = lax.axis_index("head")
     half = own.shape[0]
-    states[pl.ds(core * half, half)] = own[...]
-    states[pl.ds((1 - core) * half, half)] = got[...]
+    width = half * DV
+    for part, states in enumerate((own, got)):
+        gated = []
+        for h in range(half):
+            at = part * half + h
+            attention = local[at] + mm_both(read[at], states[h, :DK])
+            mean_square = jnp.mean(attention * attention, axis=-1, keepdims=True)
+            weight = lax.rsqrt(mean_square + EPS) * silu[:, at * DV : (at + 1) * DV]
+            gated.append((attention * weight).astype(bf16))
+            lasts[(core ^ part) * half + h] = states[h, DK:]
+        first = pl.multiple_of((core ^ part) * width, width)
+        normed[:, pl.ds(first, width)] = jnp.concatenate(gated, 1)
     finals = []
     for h in range(2 * half):
-        attention = local[h] + mm_both(read[h], states[h, :DK])
-        mean_square = jnp.mean(attention * attention, axis=-1, keepdims=True)
-        gated = attention * lax.rsqrt(mean_square + EPS) * silu[:, h * DV : (h + 1) * DV]
-        normed[:, h * DV : (h + 1) * DV] = gated.astype(bf16)
-        rows = states[h, DK:]
+        rows = lasts[h]
         finals.append(jnp.where(core == 0, rows[0:2], rows[2:4]))
     finals = jnp.concatenate(finals, 0)
     hi = finals.astype(bf16).astype(f32)
@@ -333,11 +362,13 @@
     return pltpu.VMEM(dims, dtype)
 
 
-def call(kernel, outs, scratch, *args, name, smem=0, hbm=(), flops=None):
+def call(kernel, outs, scratch, *args, smem=0, hbm=(), flops=None):
     specs = [pl.BlockSpec(memory_space=pltpu.SMEM)] * smem
-    specs += [pl.BlockSpec(memory_space=pltpu.VMEM)] * (len(args) - smem)
+    specs += [
+        pl.BlockSpec(memory_space=pltpu.HBM if i in hbm else pltpu.VMEM) for i in range(smem, len(args))
+    ]
     args = [
-        a if i < smem or i in hbm else pltpu.with_memory_space_constraint(a, pltpu.VMEM)
+        a if i < smem else pltpu.with_memory_space_constraint(a, pltpu.HBM if i in hbm else pltpu.VMEM)
         for i, a in enumerate(args)
     ]
     cost = None if flops is None else pl.CostEstimate(flops=flops, transcendentals=0, bytes_accessed=0)
@@ -345,11 +376,14 @@
         kernel,
         out_shape=outs,
         scratch_shapes=scratch,
-        name=name,
         in_specs=specs,
         cost_estimate=cost,
         compiler_params=pltpu.CompilerParams(vmem_limit_bytes=24 * 2**20),
     )(*args)
+
+
+def move(x, axis, pairs):
+    return lax.ppermute(x, axis, pairs)
 
 
 def xor_peers(count, bit):
@@ -367,29 +401,34 @@
     block = (ROWS, 256)
     block3 = (ROWS, 384)
     seg = segment_ids.reshape(1, N)
-    own, send, mixes, both, reads = call(
-        local_maps,
-        [shape((half,) + wide, f32)] * 2
-        + [shape((heads, N, N), f32), shape((heads, N, 256), f32), shape((heads, N, DK), f32)],
-        [pltpu.VMEM((heads,) + wide, f32)],
-        queries, keys, values, log_decay.T, write_strength.T, seg,
-        name="local_maps",
+    maps = [
+        shape((half,) + wide, f32),
+        shape((half, N, N), f32),
+        shape((half, N, 256), f32),
+        shape((half, N, DK), f32),
+    ]
+    inputs = (queries, keys, values, log_decay.T, write_strength.T, seg)
+    send, mixes1, both1, reads1, *held = call(
+        send_maps,
+        maps + [shape(a.shape, a.dtype) for a in inputs],
+        [pltpu.SemaphoreType.DMA((6,))],
+        *inputs,
+        hbm=range(6),
     )
     got = lax.ppermute(send, "ctx", xor_peers(peers, 1))
+    own, mixes0, both0, reads0 = call(own_maps, maps, [], *held, flops=10**9)
     m0, m1, m2, m3 = call(
         pair_maps,
         [shape(block)] * 4,
         [pltpu.VMEM((2, half) + wide, f32)],
         own, got,
-        name="pair_maps",
-    )
-    m1, m2, m3 = [lax.ppermute(m, "ctx", xor_peers(peers, 2 * s)) for s, m in ((1, m1), (2, m2), (3, m3))]
+    )
+    m1, m2, m3 = [move(m, "ctx", xor_peers(peers, 2 * s)) for s, m in ((1, m1), (2, m2), (3, m3))]
     local, read, silu = call(
         local_reads,
         [shape((heads, N, DV), f32), shape((heads, N, DK), f32), shape((N, heads * DV), f32)],
         [],
-        mixes, both, reads, out_gate,
-        name="local_reads",
+        mixes0, both0, reads0, mixes1, both1, reads1, out_gate,
         flops=2 * 10**9,
     )
     total, prefix, prefix_row = call(
@@ -397,7 +436,6 @@
         [shape(block3), shape((3, DK, 256), f32), shape((3, 8, DK), f32)],
         [pltpu.VMEM((4,) + block, bf16)],
         m0, m1, m2, m3,
-        name="quad_maps",
     )
     total_got = lax.ppermute(total, "ctx", xor_peers(peers, 12))
     r0 = call(
@@ -405,11 +443,10 @@
         shape(block3),
         [pltpu.VMEM((2,) + block3, bf16)],
         total, total_got,
-        name="row_map",
-    )
-    r1, r2, r3 = [
-        lax.ppermute(r0, "ctx", [(i, (i + 16 * s) % peers) for i in range(peers)]) for s in (1, 2, 3)
-    ]
+    )
+    rows = [[(i, (i + 16 * s) % peers) for i in range(peers)] for s in (1, 2, 3)]
+    rows[2] = [(i, i - 16) for i in range(peers // 2, peers)]
+    r1, r2, r3 = [move(r0, "ctx", pairs) for pairs in rows]
     s0, s1, s2, s3 = call(
         scan_states,
         [shape((ROWS, DV))] * 4,
@@ -420,9 +457,8 @@
             pltpu.VMEM((4, ROWS, DV), bf16),
         ],
         r0, r1, r2, r3, total, total_got, prefix, prefix_row,
-        name="scan_states",
-    )
-    s1, s2, s3 = [lax.ppermute(m, "ctx", xor_peers(peers, 2 * s)) for s, m in ((1, s1), (2, s2), (3, s3))]
+    )
+    s1, s2, s3 = [move(m, "ctx", xor_peers(peers, 2 * s)) for s, m in ((1, s1), (2, s2), (3, s3))]
     own_state, send_state = call(
         pair_states,
         [shape((half, N + 8, DV), f32)] * 2,
@@ -432,27 +468,24 @@
             pltpu.VMEM((half, ROWS, DV), bf16),
         ],
         s0, s1, s2, s3, own, got,
-        name="pair_states",
     )
     got_state = lax.ppermute(send_state, "ctx", xor_peers(peers, 1))
     acc, o1, o2, o3, tail = call(
         project,
         [shape((32, model), f32)] + [shape((32, model + DV))] * 3 + [shape((32, DV))],
         [
-            pltpu.VMEM((heads, N + 8, DV), f32),
             pltpu.VMEM((N, heads * DV), bf16),
             pltpu.VMEM((N, model), f32),
+            pltpu.VMEM((heads, 8, DV), f32),
         ],
         own_state, got_state, local, read, silu, out_weight,
-        name="project",
-    )
-    o1, o2, o3 = [lax.ppermute(o, "head", xor_peers(4, s)) for s, o in ((1, o1), (2, o2), (3, o3))]
+    )
+    o1, o2, o3 = [move(o, "head", xor_peers(4, s)) for s, o in ((1, o1), (2, o2), (3, o3))]
     return call(
         finish,
         [jax.ShapeDtypeStruct((32, model), bf16), jax.ShapeDtypeStruct((heads, 256), f32)],
         [pltpu.VMEM((4 * heads, 256), f32)],
         head_order, acc, o1, o2, o3, tail,
-        name="finish",
         smem=1,
     )
 

time: 72.8 us -> 68.5 us (0.941)
  local copies, waits for them, and re-layouts: 4.79 us -> 0.01 us
  Pallas kernels: 11.2 us -> 13.8 us
  waiting for transfers between devices: 25.5 us -> 24.1 us
  starting transfers between devices: 30.4 us -> 29.6 us
    unnamed x18 -> x6, local copies, waits for them, and re-layouts: 4.79 us -> 0.01 us
    pallas_call x9 -> x10, Pallas kernels: 11.2 us -> 13.8 us  [call(): pl.pallas_call(kernel, out_shape=outs, scratch_shapes=scratch, in_specs=s...]
    ppermute x1, starting transfers between devices: 5.98 us -> 3.79 us  [per_device(): got_state = lax.ppermute(send_state, 'ctx', xor_peers(peers, 1))]
    ppermute x1, waiting for transfers between devices: 1.58 us -> 0.01 us  [per_device(): got = lax.ppermute(send, 'ctx', xor_peers(peers, 1))]
    ppermute x1, waiting for transfers between devices: 2.24 us -> 3.57 us  [per_device(): total_got = lax.ppermute(total, 'ctx', xor_peers(peers, 12))]
    ppermute x12, waiting for transfers between devices: 21 us -> 19.9 us  [move(): return lax.ppermute(x, axis, pairs)]
    ppermute x12, starting transfers between devices: 15.5 us -> 16.4 us  [move(): return lax.ppermute(x, axis, pairs)]
  transfers between devices with their start and end apart: 15 -> 15, of which waited for: 13 -> 12; matrix products, arithmetic and copies ran while one was open for 0% -> 0% of each run, Pallas kernels for 1% -> 6%
where the time goes in v2:
time: 68.5 us; the launch traced here: 68.2 us
  starting transfers between devices  29.6 us (43%)
  waiting for transfers between devices  24.1 us (35%)
  Pallas kernels  13.8 us (20%)
  between operations  0.74 us (1%)
    ppermute x12, waiting for transfers between devices, move(): return lax.ppermute(x, axis, pairs)  19.9 us
    ppermute x12, starting transfers between devices, move(): return lax.ppermute(x, axis, pairs)  16.4 us
    pallas_call x10, Pallas kernels, call(): pl.pallas_call(kernel, out_shape=outs, scratch_shapes=scratch, in_specs=s...  13.8 us
    ppermute x1, starting transfers between devices, per_device(): total_got = lax.ppermute(total, 'ctx', xor_peers(peers, 12))  6.08 us
    ppermute x1, starting transfers between devices, per_device(): got_state = lax.ppermute(send_state, 'ctx', xor_peers(peers, 1))  3.79 us
    ppermute x1, waiting for transfers between devices, per_device(): total_got = lax.ppermute(total, 'ctx', xor_peers(peers, 12))  3.57 us
    ppermute x1, starting transfers between devices, per_device(): got = lax.ppermute(send, 'ctx', xor_peers(peers, 1))  3.29 us
  transfers between devices with their start and end apart: 15, of which 12 were waited for; matrix products, arithmetic and copies ran while one was open for 0% of the time, Pallas kernels for 6%

profile of v2, /device:TPU:1, one launch (start us, length us, event | category | flops | bytes accessed | tf_op | source)
XLA Modules:
  0.0 68.2 jit_solution(15766473085691772823)
XLA Ops:
  0.6 4.7 %shard_map.104 = (f32[4,136,256]{2,1,0:T(8,128)S(1)}, f32[4,128,128]{2,1,0:T(8,128)S(1)}, f32[4,128,256]{2,1,0:T(8,128)S(1)}, f32[4,128,128]{2,1,0:T(8,128)S(1)}...) custom-call(bf16[128,512]{1,0:T(8,128)(2,1)} %q.1, ...), custom_call_target="tpu_custom_call" | custom-call | tf_op jit(solution)/shard_map/pallas_call | solution.py:375
  5.3 3.3 %collective-permute-start = (f32[4,136,256]{2,1,0:T(8,128)S(1)}, f32[4,136,256]{2,1,0:T(8,128)S(1)}, u32[]{:S(2)}, u32[]{:S(2)}) collective-permute-start(f32[4,136,256]{2,1,0:T(8,128)S(1)} %get-tuple-element.44), channel_id=1, source_target_pairs={{0,4},{4,0},{8,12},{12,8},{16,20},{20,16},{24,28},{28,24},{32,36},... | collective-permute-start | bytes 1671176 | tf_op jit(solution)/shard_map/ppermute | solution.py:418
  8.6 3.4 %shard_map.105 = (f32[4,136,256]{2,1,0:T(8,128)S(1)}, f32[4,128,128]{2,1,0:T(8,128)S(1)}, f32[4,128,256]{2,1,0:T(8,128)S(1)}, f32[4,128,128]{2,1,0:T(8,128)S(1)}) custom-call(bf16[128,512]{1,0:T(8,128)(2,1)S(1)} %get-tuple-element.37.q, bf16[128,512]{1,0:T(8,128)(2,1)S(1)} %get-tuple-element.38.k, bf16[128,1024]{1,0:T(8,128)(2,1)S(1)} %get-tuple-element.39.v, ...), custom_call_target="tpu_custom_call" | custom-call | flops 1000000000 | tf_op jit(solution)/shard_map/pallas_call | solution.py:375
  12.7 2.9 %collective-permute-start.2 = (bf16[144,256]{1,0:T(8,128)(2,1)S(1)}, bf16[144,256]{1,0:T(8,128)(2,1)S(1)}, u32[]{:S(2)}, u32[]{:S(2)}) collective-permute-start(bf16[144,256]{1,0:T(8,128)(2,1)S(1)} %get-tuple-element.47), channel_id=1, source_target_pairs={{0,16},{4,20},{8,24},{12,28},{16,0},{20,4},{24,8},{28,12},{32,48},... | collective-permute-start | bytes 221192 | tf_op jit(solution)/shard_map/ppermute | solution.py:386
  16.5 1.6 %collective-permute-done.2.m2 = bf16[144,256]{1,0:T(8,128)(2,1)S(1)} collective-permute-done((bf16[144,256]{1,0:T(8,128)(2,1)S(1)}, bf16[144,256]{1,0:T(8,128)(2,1)S(1)}, u32[]{:S(2)}, u32[]{:S(2)}) %collective-permute-start.2) | collective-permute-done | bytes 73760 | tf_op jit(solution)/shard_map/ppermute | solution.py:386
  18.1 2.5 %collective-permute-done.3.m3 = bf16[144,256]{1,0:T(8,128)(2,1)S(1)} collective-permute-done((bf16[144,256]{1,0:T(8,128)(2,1)S(1)}, bf16[144,256]{1,0:T(8,128)(2,1)S(1)}, u32[]{:S(2)}, u32[]{:S(2)}) %collective-permute-start.3) | collective-permute-done | bytes 73760 | tf_op jit(solution)/shard_map/ppermute | solution.py:386
  21.1 6.1 %collective-permute-start.4 = (bf16[144,384]{1,0:T(8,128)(2,1)S(1)}, bf16[144,384]{1,0:T(8,128)(2,1)S(1)}, u32[]{:S(2)}, u32[]{:S(2)}) collective-permute-start(bf16[144,384]{1,0:T(8,128)(2,1)S(1)} %get-tuple-element.49.own), channel_id=1, source_target_pairs={{0,48},{4,52},{8,56},{12,60},{16,32},{20,36},{24,40},{28,44},{32,1... | collective-permute-start | bytes 331784 | tf_op jit(solution)/shard_map/ppermute | solution.py:440
  27.2 3.6 %collective-permute-done.4.got = bf16[144,384]{1,0:T(8,128)(2,1)S(1)} collective-permute-done((bf16[144,384]{1,0:T(8,128)(2,1)S(1)}, bf16[144,384]{1,0:T(8,128)(2,1)S(1)}, u32[]{:S(2)}, u32[]{:S(2)}) %collective-permute-start.4) | collective-permute-done | bytes 110624 | tf_op jit(solution)/shard_map/ppermute | solution.py:440
  31.0 1.4 %collective-permute-start.5 = (bf16[144,384]{1,0:T(8,128)(2,1)S(1)}, bf16[144,384]{1,0:T(8,128)(2,1)S(1)}, u32[]{:S(2)}, u32[]{:S(2)}) collective-permute-start(bf16[144,384]{1,0:T(8,128)(2,1)S(1)} %shard_map.108.r0), channel_id=1, source_target_pairs={{0,64},{4,68},{8,72},{12,76},{16,80},{20,84},{24,88},{28,92},{32,9... | collective-permute-start | bytes 331784 | tf_op jit(solution)/shard_map/ppermute | solution.py:386
  32.4 2.6 %collective-permute-start.6 = (bf16[144,384]{1,0:T(8,128)(2,1)S(1)}, bf16[144,384]{1,0:T(8,128)(2,1)S(1)}, u32[]{:S(2)}, u32[]{:S(2)}) collective-permute-start(bf16[144,384]{1,0:T(8,128)(2,1)S(1)} %shard_map.108.r0), channel_id=1, source_target_pairs={{0,128},{4,132},{8,136},{12,140},{16,144},{20,148},{24,152},{28,15... | collective-permute-start | bytes 331784 | tf_op jit(solution)/shard_map/ppermute | solution.py:386
  35.0 0.7 collective-permute-start.7
  36.0 2.9 %collective-permute-done.6.r2 = bf16[144,384]{1,0:T(8,128)(2,1)S(1)} collective-permute-done((bf16[144,384]{1,0:T(8,128)(2,1)S(1)}, bf16[144,384]{1,0:T(8,128)(2,1)S(1)}, u32[]{:S(2)}, u32[]{:S(2)}) %collective-permute-start.6) | collective-permute-done | bytes 110624 | tf_op jit(solution)/shard_map/ppermute | solution.py:386
  38.8 1.0 %shard_map.109 = (bf16[144,128]{1,0:T(8,128)(2,1)S(1)}, bf16[144,128]{1,0:T(8,128)(2,1)S(1)}, bf16[144,128]{1,0:T(8,128)(2,1)S(1)}, bf16[144,128]{1,0:T(8,128)(2,1)S(1)}) custom-call(bf16[144,384]{1,0:T(8,128)(2,1)S(1)} %shard_map.108.r0, bf16[144,384]{1,0:T(8,128)(2,1)S(1)} %collective-permute-done.5.r1, bf16[144,384]{1,0:T(8,128)(2,1)S(1)} %collective-permute-done.6.r2, ...), custom_call_target="tpu_custom_call" | custom-call | tf_op jit(solution)/shard_map/pallas_call | solution.py:375
  39.9 3.2 %collective-permute-start.9 = (bf16[144,128]{1,0:T(8,128)(2,1)S(1)}, bf16[144,128]{1,0:T(8,128)(2,1)S(1)}, u32[]{:S(2)}, u32[]{:S(2)}) collective-permute-start(bf16[144,128]{1,0:T(8,128)(2,1)S(1)} %get-tuple-element.54), channel_id=1, source_target_pairs={{0,16},{4,20},{8,24},{12,28},{16,0},{20,4},{24,8},{28,12},{32,48},... | collective-permute-start | bytes 110600 | tf_op jit(solution)/shard_map/ppermute | solution.py:386
  43.1 0.9 %collective-permute-start.10 = (bf16[144,128]{1,0:T(8,128)(2,1)S(1)}, bf16[144,128]{1,0:T(8,128)(2,1)S(1)}, u32[]{:S(2)}, u32[]{:S(2)}) collective-permute-start(bf16[144,128]{1,0:T(8,128)(2,1)S(1)} %get-tuple-element.55), channel_id=1, source_target_pairs={{0,24},{4,28},{8,16},{12,20},{16,8},{20,12},{24,0},{28,4},{32,56},... | collective-permute-start | bytes 110600 | tf_op jit(solution)/shard_map/ppermute | solution.py:386
  44.4 3.3 %collective-permute-done.10.s3 = bf16[144,128]{1,0:T(8,128)(2,1)S(1)} collective-permute-done((bf16[144,128]{1,0:T(8,128)(2,1)S(1)}, bf16[144,128]{1,0:T(8,128)(2,1)S(1)}, u32[]{:S(2)}, u32[]{:S(2)}) %collective-permute-start.10) | collective-permute-done | bytes 36896 | tf_op jit(solution)/shard_map/ppermute | solution.py:386
  48.1 3.8 %collective-permute-start.11 = (f32[4,136,128]{2,1,0:T(8,128)S(1)}, f32[4,136,128]{2,1,0:T(8,128)S(1)}, u32[]{:S(2)}, u32[]{:S(2)}) collective-permute-start(f32[4,136,128]{2,1,0:T(8,128)S(1)} %get-tuple-element.57), channel_id=1, source_target_pairs={{0,4},{4,0},{8,12},{12,8},{16,20},{20,16},{24,28},{28,24},{32,36},... | collective-permute-start | bytes 835592 | tf_op jit(solution)/shard_map/ppermute | solution.py:472
  53.1 1.2 %shard_map.112 = (f32[32,2048]{1,0:T(8,128)S(1)}, bf16[32,2176]{1,0:T(8,128)(2,1)S(1)}, bf16[32,2176]{1,0:T(8,128)(2,1)S(1)}, bf16[32,2176]{1,0:T(8,128)(2,1)S(1)}, bf16[32,128]{1,0:T(8,128)(2,1)S(1)}) custom-call(f32[4,136,128]{2,1,0:T(8,128)S(1)} %get-tuple-element.56.own, f32[4,136,128]{2,1,0:T(8,128)S(1)} %collective-permute-done.11.got, ...), custom_call_target="tpu_custom_call" | custom-call | tf_op jit(solution)/shard_map/pallas_call | solution.py:375
  54.3 1.3 %collective-permute-start.12 = (bf16[32,2176]{1,0:T(8,128)(2,1)S(1)}, bf16[32,2176]{1,0:T(8,128)(2,1)S(1)}, u32[]{:S(2)}, u32[]{:S(2)}) collective-permute-start(bf16[32,2176]{1,0:T(8,128)(2,1)S(1)} %get-tuple-element.68), channel_id=1, source_target_pairs={{0,1},{1,0},{2,3},{3,2},{4,5},{5,4},{6,7},{7,6},{8,9},{9,8},{10,11... | collective-permute-start | bytes 417800 | tf_op jit(solution)/shard_map/ppermute | solution.py:386
  55.6 2.5 %collective-permute-start.13 = (bf16[32,2176]{1,0:T(8,128)(2,1)S(1)}, bf16[32,2176]{1,0:T(8,128)(2,1)S(1)}, u32[]{:S(2)}, u32[]{:S(2)}) collective-permute-start(bf16[32,2176]{1,0:T(8,128)(2,1)S(1)} %get-tuple-element.69), channel_id=1, source_target_pairs={{0,2},{1,3},{2,0},{3,1},{4,6},{5,7},{6,4},{7,5},{8,10},{9,11},{10,... | collective-permute-start | bytes 417800 | tf_op jit(solution)/shard_map/ppermute | solution.py:386
  58.3 0.8 %collective-permute-done.12.r1 = bf16[32,2176]{1,0:T(8,128)(2,1)S(1)} collective-permute-done((bf16[32,2176]{1,0:T(8,128)(2,1)S(1)}, bf16[32,2176]{1,0:T(8,128)(2,1)S(1)}, u32[]{:S(2)}, u32[]{:S(2)}) %collective-permute-start.12) | collective-permute-done | bytes 139296 | tf_op jit(solution)/shard_map/ppermute | solution.py:386
  59.1 5.3 %collective-permute-done.13.r2 = bf16[32,2176]{1,0:T(8,128)(2,1)S(1)} collective-permute-done((bf16[32,2176]{1,0:T(8,128)(2,1)S(1)}, bf16[32,2176]{1,0:T(8,128)(2,1)S(1)}, u32[]{:S(2)}, u32[]{:S(2)}) %collective-permute-start.13) | collective-permute-done | bytes 139296 | tf_op jit(solution)/shard_map/ppermute | solution.py:386
  64.4 2.5 %collective-permute-done.14.r3 = bf16[32,2176]{1,0:T(8,128)(2,1)S(1)} collective-permute-done((bf16[32,2176]{1,0:T(8,128)(2,1)S(1)}, bf16[32,2176]{1,0:T(8,128)(2,1)S(1)}, u32[]{:S(2)}, u32[]{:S(2)}) %collective-permute-start.14) | collective-permute-done | bytes 139296 | tf_op jit(solution)/shard_map/ppermute | solution.py:386
  66.9 1.3 %shard_map.113 = (bf16[32,2048]{1,0:T(8,128)(2,1)}, f32[8,256]{1,0:T(8,128)}) custom-call(s32[32]{0:T(128)S(1)} %copy-done.1, f32[32,2048]{1,0:T(8,128)S(1)} %get-tuple-element.67.acc, bf16[32,2176]{1,0:T(8,128)(2,1)S(1)} %collective-permute-done.12.r1, bf16[32,2176]{1,0:T(8,128)(2,1)S(1)} %collective-permute-done.13.r2, ...), custom_call_target="tpu_custom_call" | custom-call | tf_op jit(solution)/shard_map/pallas_call | solution.py:375
  (22 shorter events, 4.8 us)
Async XLA Ops:
  0.6 51.3 %copy-start.2 = (bf16[128,1024]{1,0:T(8,128)(2,1)S(1)}, bf16[128,1024]{1,0:T(8,128)(2,1)}, u32[]{:S(2)}) copy-start(bf16[128,1024]{1,0:T(8,128)(2,1)} %gate.1) | copy-start | bytes 786436
  5.3 6.7 %collective-permute-start = (f32[4,136,256]{2,1,0:T(8,128)S(1)}, f32[4,136,256]{2,1,0:T(8,128)S(1)}, u32[]{:S(2)}, u32[]{:S(2)}) collective-permute-start(f32[4,136,256]{2,1,0:T(8,128)S(1)} %get-tuple-element.44), channel_id=1, source_target_pairs={{0,4},{4,0},{8,12},{12,8},{16,20},{20,16},{24,28},{28,24},{32,36},... | collective-permute-start | bytes 1671176 | tf_op jit(solution)/shard_map/ppermute | solution.py:418
  12.6 3.9 %collective-permute-start.1 = (bf16[144,256]{1,0:T(8,128)(2,1)S(1)}, bf16[144,256]{1,0:T(8,128)(2,1)S(1)}, u32[]{:S(2)}, u32[]{:S(2)}) collective-permute-start(bf16[144,256]{1,0:T(8,128)(2,1)S(1)} %get-tuple-element.46), channel_id=1, source_target_pairs={{0,8},{4,12},{8,0},{12,4},{16,24},{20,28},{24,16},{28,20},{32,40},... | collective-permute-start | bytes 221192 | tf_op jit(solution)/shard_map/ppermute | solution.py:386
  12.7 5.4 %collective-permute-start.2 = (bf16[144,256]{1,0:T(8,128)(2,1)S(1)}, bf16[144,256]{1,0:T(8,128)(2,1)S(1)}, u32[]{:S(2)}, u32[]{:S(2)}) collective-permute-start(bf16[144,256]{1,0:T(8,128)(2,1)S(1)} %get-tuple-element.47), channel_id=1, source_target_pairs={{0,16},{4,20},{8,24},{12,28},{16,0},{20,4},{24,8},{28,12},{32,48},... | collective-permute-start | bytes 221192 | tf_op jit(solution)/shard_map/ppermute | solution.py:386
  15.6 5.0 %collective-permute-start.3 = (bf16[144,256]{1,0:T(8,128)(2,1)S(1)}, bf16[144,256]{1,0:T(8,128)(2,1)S(1)}, u32[]{:S(2)}, u32[]{:S(2)}) collective-permute-start(bf16[144,256]{1,0:T(8,128)(2,1)S(1)} %get-tuple-element.48), channel_id=1, source_target_pairs={{0,24},{4,28},{8,16},{12,20},{16,8},{20,12},{24,0},{28,4},{32,56},... | collective-permute-start | bytes 221192 | tf_op jit(solution)/shard_map/ppermute | solution.py:386
  21.1 9.7 %collective-permute-start.4 = (bf16[144,384]{1,0:T(8,128)(2,1)S(1)}, bf16[144,384]{1,0:T(8,128)(2,1)S(1)}, u32[]{:S(2)}, u32[]{:S(2)}) collective-permute-start(bf16[144,384]{1,0:T(8,128)(2,1)S(1)} %get-tuple-element.49.own), channel_id=1, source_target_pairs={{0,48},{4,52},{8,56},{12,60},{16,32},{20,36},{24,40},{28,44},{32,1... | collective-permute-start | bytes 331784 | tf_op jit(solution)/shard_map/ppermute | solution.py:440
  31.0 5.0 %collective-permute-start.5 = (bf16[144,384]{1,0:T(8,128)(2,1)S(1)}, bf16[144,384]{1,0:T(8,128)(2,1)S(1)}, u32[]{:S(2)}, u32[]{:S(2)}) collective-permute-start(bf16[144,384]{1,0:T(8,128)(2,1)S(1)} %shard_map.108.r0), channel_id=1, source_target_pairs={{0,64},{4,68},{8,72},{12,76},{16,80},{20,84},{24,88},{28,92},{32,9... | collective-permute-start | bytes 331784 | tf_op jit(solution)/shard_map/ppermute | solution.py:386
  32.4 6.5 %collective-permute-start.6 = (bf16[144,384]{1,0:T(8,128)(2,1)S(1)}, bf16[144,384]{1,0:T(8,128)(2,1)S(1)}, u32[]{:S(2)}, u32[]{:S(2)}) collective-permute-start(bf16[144,384]{1,0:T(8,128)(2,1)S(1)} %shard_map.108.r0), channel_id=1, source_target_pairs={{0,128},{4,132},{8,136},{12,140},{16,144},{20,148},{24,152},{28,15... | collective-permute-start | bytes 331784 | tf_op jit(solution)/shard_map/ppermute | solution.py:386
  35.0 3.8 %collective-permute-start.7 = (bf16[144,384]{1,0:T(8,128)(2,1)S(1)}, bf16[144,384]{1,0:T(8,128)(2,1)S(1)}, u32[]{:S(2)}, u32[]{:S(2)}) collective-permute-start(bf16[144,384]{1,0:T(8,128)(2,1)S(1)} %shard_map.108.r0), channel_id=1, source_target_pairs={{128,64},{132,68},{136,72},{140,76},{144,80},{148,84},{152,88},{15... | collective-permute-start | bytes 331784 | tf_op jit(solution)/shard_map/ppermute | solution.py:386
  39.8 4.2 %collective-permute-start.8 = (bf16[144,128]{1,0:T(8,128)(2,1)S(1)}, bf16[144,128]{1,0:T(8,128)(2,1)S(1)}, u32[]{:S(2)}, u32[]{:S(2)}) collective-permute-start(bf16[144,128]{1,0:T(8,128)(2,1)S(1)} %get-tuple-element.53), channel_id=1, source_target_pairs={{0,8},{4,12},{8,0},{12,4},{16,24},{20,28},{24,16},{28,20},{32,40},... | collective-permute-start | bytes 110600 | tf_op jit(solution)/shard_map/ppermute | solution.py:386
  39.9 4.5 %collective-permute-start.9 = (bf16[144,128]{1,0:T(8,128)(2,1)S(1)}, bf16[144,128]{1,0:T(8,128)(2,1)S(1)}, u32[]{:S(2)}, u32[]{:S(2)}) collective-permute-start(bf16[144,128]{1,0:T(8,128)(2,1)S(1)} %get-tuple-element.54), channel_id=1, source_target_pairs={{0,16},{4,20},{8,24},{12,28},{16,0},{20,4},{24,8},{28,12},{32,48},... | collective-permute-start | bytes 110600 | tf_op jit(solution)/shard_map/ppermute | solution.py:386
  43.1 4.6 %collective-permute-start.10 = (bf16[144,128]{1,0:T(8,128)(2,1)S(1)}, bf16[144,128]{1,0:T(8,128)(2,1)S(1)}, u32[]{:S(2)}, u32[]{:S(2)}) collective-permute-start(bf16[144,128]{1,0:T(8,128)(2,1)S(1)} %get-tuple-element.55), channel_id=1, source_target_pairs={{0,24},{4,28},{8,16},{12,20},{16,8},{20,12},{24,0},{28,4},{32,56},... | collective-permute-start | bytes 110600 | tf_op jit(solution)/shard_map/ppermute | solution.py:386
  47.7 5.4 %copy-start = (bf16[1024,2048]{1,0:T(8,128)(2,1)S(1)}, bf16[1024,2048]{1,0:T(8,128)(2,1)}, u32[]{:S(2)}) copy-start(bf16[1024,2048]{1,0:T(8,128)(2,1)} %w.1) | copy-start | bytes 12582916
  48.1 5.0 %collective-permute-start.11 = (f32[4,136,128]{2,1,0:T(8,128)S(1)}, f32[4,136,128]{2,1,0:T(8,128)S(1)}, u32[]{:S(2)}, u32[]{:S(2)}) collective-permute-start(f32[4,136,128]{2,1,0:T(8,128)S(1)} %get-tuple-element.57), channel_id=1, source_target_pairs={{0,4},{4,0},{8,12},{12,8},{16,20},{20,16},{24,28},{28,24},{32,36},... | collective-permute-start | bytes 835592 | tf_op jit(solution)/shard_map/ppermute | solution.py:472
  52.4 14.5 %copy-start.1 = (s32[32]{0:T(128)S(1)}, s32[32]{0:T(128)}, u32[]{:S(2)}) copy-start(s32[32]{0:T(128)} %order.1) | copy-start | bytes 388
  54.3 4.8 %collective-permute-start.12 = (bf16[32,2176]{1,0:T(8,128)(2,1)S(1)}, bf16[32,2176]{1,0:T(8,128)(2,1)S(1)}, u32[]{:S(2)}, u32[]{:S(2)}) collective-permute-start(bf16[32,2176]{1,0:T(8,128)(2,1)S(1)} %get-tuple-element.68), channel_id=1, source_target_pairs={{0,1},{1,0},{2,3},{3,2},{4,5},{5,4},{6,7},{7,6},{8,9},{9,8},{10,11... | collective-permute-start | bytes 417800 | tf_op jit(solution)/shard_map/ppermute | solution.py:386
  55.6 8.8 %collective-permute-start.13 = (bf16[32,2176]{1,0:T(8,128)(2,1)S(1)}, bf16[32,2176]{1,0:T(8,128)(2,1)S(1)}, u32[]{:S(2)}, u32[]{:S(2)}) collective-permute-start(bf16[32,2176]{1,0:T(8,128)(2,1)S(1)} %get-tuple-element.69), channel_id=1, source_target_pairs={{0,2},{1,3},{2,0},{3,1},{4,6},{5,7},{6,4},{7,5},{8,10},{9,11},{10,... | collective-permute-start | bytes 417800 | tf_op jit(solution)/shard_map/ppermute | solution.py:386
  58.1 8.8 %collective-permute-start.14 = (bf16[32,2176]{1,0:T(8,128)(2,1)S(1)}, bf16[32,2176]{1,0:T(8,128)(2,1)S(1)}, u32[]{:S(2)}, u32[]{:S(2)}) collective-permute-start(bf16[32,2176]{1,0:T(8,128)(2,1)S(1)} %get-tuple-element.70), channel_id=1, source_target_pairs={{0,3},{1,2},{2,1},{3,0},{4,7},{5,6},{6,5},{7,4},{8,11},{9,10},{10,... | collective-permute-start | bytes 417800 | tf_op jit(solution)/shard_map/ppermute | solution.py:386

commit v3 on v2

--- a/solution.py
+++ b/solution.py
@@ -119,13 +119,25 @@
         squared = [mm_both(s, s) for s in squared]
         inv = [x + mm_both(x, s) for x, s in zip(inv, squared)]
     for size in (16, 32, 64):
-        ring = ((ii // (2 * size)) == (jj // (2 * size))) & ((ii // size) != (jj // size))
-        below = [mm_both(jnp.where(ring, c, 0.0), x) for c, x in zip(couplings, inv)]
-        inv = [x - mm_both(x, y) for x, y in zip(inv, below)]
+        odd = range(size, N, 2 * size)
+        sibling = (ii // (2 * size)) == (jj // (2 * size))
+        ring = sibling & ((ii // size) != (jj // size))
+
+        def take(x):
+            return jnp.concatenate([x[r : r + size] for r in odd], 0)
+
+        def spread(x):
+            gap = jnp.zeros((size, N), f32)
+            return jnp.concatenate([y for i in range(len(odd)) for y in (gap, x[i * size : (i + 1) * size])], 0)
+
+        below = [mm_both(take(jnp.where(ring, c, 0.0)), x) for c, x in zip(couplings, inv)]
+        inv = [x - spread(mm_both(take(x), spread(y))) for x, y in zip(inv, below)]
     return inv
 
 
-def local_maps(heads, groups, q_ref, k_ref, v_ref, g, beta, seg_ref, out, mixes, both, reads):
+def local_maps(heads, q_ref, k_ref, v_ref, g_ref, b_ref, seg_ref, out, mixes, both, reads, waits=None):
+    q_wait, v_wait = waits or (None, None)
+    groups = heads // 2
     ii, jj = iota((N, N), 0), iota((N, N), 1)
     doc_row = jnp.broadcast_to(seg_ref[...].astype(f32), (N, N))
     doc_col = doc_row.T
@@ -136,14 +148,15 @@
     last_col = doc_col[:, 0:1] == doc_row[:, N - 1 : N]
     first_doc, last_doc = doc_col[0:1], doc_col[N - 1 : N]
     upper = jnp.where(ii <= jj, 1.0, 0.0).astype(bf16)
-    count = g.shape[0]
+    count = out.shape[0]
+    g = g_ref[pl.ds(heads, count)]
+    beta = b_ref[pl.ds(heads, count)]
     g = jnp.concatenate([g, jnp.zeros((8 - count, N), f32)], 0)
     g0 = g.astype(bf16)
     g1 = (g - g0.astype(f32)).astype(bf16)
     g2 = (g - g0.astype(f32) - g1.astype(f32)).astype(bf16)
     rows = mm(g0, upper) + mm(g1, upper) + mm(g2, upper)
     ks = [k_ref[:, pl.ds(pl.multiple_of((groups + i) * DK, DK), DK)] for i in range(count // 2)]
-    qs = [q_ref[:, pl.ds(pl.multiple_of((groups + i) * DK, DK), DK)] for i in range(count // 2)]
 
     def unit(x):
         x = x.astype(f32)
@@ -152,19 +165,26 @@
     cols = jnp.concatenate([rows, beta, jnp.zeros((N - 8 - count, N), f32)], 0).T
     cum = cols[:, :count]
     rk = [unit(k) for k in ks]
-    rq = [unit(q) * DK ** (-0.5) for q in qs]
     rk_row = [jnp.broadcast_to(r, (N, N)).T[0:1] for r in rk]
     kts = [k.astype(f32).T.astype(bf16) for k in ks]
     kk = [mm(k, kt) for k, kt in zip(ks, kts)]
-    qk = [mm(q, kt) for q, kt in zip(qs, kts)]
-    couplings = []
+    couplings, mixed = [], []
     for h in range(count):
         i = h // 2
         gap = cum[:, h : h + 1] - rows[h : h + 1]
         mix = jnp.where(same, jnp.exp(jnp.minimum(gap, 0.0)), 0.0) * rk_row[i]
         couplings.append(jnp.where(strict, (cols[:, 8 + h : 9 + h] * rk[i]) * (mix * kk[i]), 0.0))
-        mixes[h] = rq[i] * (mix * qk[i])
+        mixed.append(mix)
+    if q_wait:
+        q_wait()
+    qs = [q_ref[:, pl.ds(pl.multiple_of((groups + i) * DK, DK), DK)] for i in range(count // 2)]
+    rq = [unit(q) * DK ** (-0.5) for q in qs]
+    qk = [mm(q, kt) for q, kt in zip(qs, kts)]
+    for h in range(count):
+        mixes[h] = rq[h // 2] * (mixed[h] * qk[h // 2])
     inv = inverses(couplings)
+    if v_wait:
+        v_wait()
     for h in range(count):
         i = h // 2
         entry_row = jnp.where(cont_row, jnp.exp(rows[h : h + 1]), 0.0)
@@ -190,23 +210,15 @@
     ]
     for move in moves:
         move.start()
-    for move in moves:
+    for move in moves[:4]:
         move.wait()
-    half = out.shape[0]
-    heads = (1 - places()[0]) * half
-    local_maps(
-        heads, heads // 2, q_in, k_in, v_in, g_in[pl.ds(heads, half)], b_in[pl.ds(heads, half)], seg_in,
-        out, mixes, both, reads,
-    )
+    heads = (1 - places()[0]) * out.shape[0]
+    waits = (moves[4].wait, moves[5].wait)
+    local_maps(heads, q_in, k_in, v_in, g_in, b_in, seg_in, out, mixes, both, reads, waits)
 
 
 def own_maps(q, k, v, g, b, seg, out, mixes, both, reads):
-    half = out.shape[0]
-    heads = places()[0] * half
-    local_maps(
-        heads, heads // 2, q, k, v, g[pl.ds(heads, half)], b[pl.ds(heads, half)], seg,
-        out, mixes, both, reads,
-    )
+    local_maps(places()[0] * out.shape[0], q, k, v, g, b, seg, out, mixes, both, reads)
 
 
 def local_reads(mixes0, both0, reads0, mixes1, both1, reads1, gate, local, read, silu):
@@ -382,10 +394,6 @@
     )(*args)
 
 
-def move(x, axis, pairs):
-    return lax.ppermute(x, axis, pairs)
-
-
 def xor_peers(count, bit):
     return [(i, i ^ bit) for i in range(count)]
 
@@ -399,7 +407,7 @@
     model = out_weight.shape[1]
     wide = (N + 8, 256)
     block = (ROWS, 256)
-    block3 = (ROWS, 384)
+    block3 = (ROWS, 256)
     seg = segment_ids.reshape(1, N)
     maps = [
         shape((half,) + wide, f32),
@@ -423,7 +431,7 @@
         [pltpu.VMEM((2, half) + wide, f32)],
         own, got,
     )
-    m1, m2, m3 = [move(m, "ctx", xor_peers(peers, 2 * s)) for s, m in ((1, m1), (2, m2), (3, m3))]
+    m1, m2, m3 = [lax.ppermute(m, "ctx", xor_peers(peers, 2 * s)) for s, m in ((1, m1), (2, m2), (3, m3))]
     local, read, silu = call(
         local_reads,
         [shape((heads, N, DV), f32), shape((heads, N, DK), f32), shape((N, heads * DV), f32)],
@@ -446,7 +454,7 @@
     )
     rows = [[(i, (i + 16 * s) % peers) for i in range(peers)] for s in (1, 2, 3)]
     rows[2] = [(i, i - 16) for i in range(peers // 2, peers)]
-    r1, r2, r3 = [move(r0, "ctx", pairs) for pairs in rows]
+    r1, r2, r3 = [lax.ppermute(r0, "ctx", pairs) for pairs in rows]
     s0, s1, s2, s3 = call(
         scan_states,
         [shape((ROWS, DV))] * 4,
@@ -458,7 +466,7 @@
         ],
         r0, r1, r2, r3, total, total_got, prefix, prefix_row,
     )
-    s1, s2, s3 = [move(m, "ctx", xor_peers(peers, 2 * s)) for s, m in ((1, s1), (2, s2), (3, s3))]
+    s1, s2, s3 = [lax.ppermute(m, "ctx", xor_peers(peers, 2 * s)) for s, m in ((1, s1), (2, s2), (3, s3))]
     own_state, send_state = call(
         pair_states,
         [shape((half, N + 8, DV), f32)] * 2,
@@ -480,7 +488,7 @@
         ],
         own_state, got_state, local, read, silu, out_weight,
     )
-    o1, o2, o3 = [move(o, "head", xor_peers(4, s)) for s, o in ((1, o1), (2, o2), (3, o3))]
+    o1, o2, o3 = [lax.ppermute(o, "head", xor_peers(4, s)) for s, o in ((1, o1), (2, o2), (3, o3))]
     return call(
         finish,
         [jax.ShapeDtypeStruct((32, model), bf16), jax.ShapeDtypeStruct((heads, 256), f32)],

time: 68.5 us -> 65.7 us (0.959)
  waiting for transfers between devices: 24.1 us -> 20.5 us
    ppermute x12, waiting for transfers between devices: 19.9 us -> 18 us  [the longest x3 8.63 us: per_device(): lax.ppermute(o, 'head', xor_peers(4, s))]
    ppermute x1, waiting for transfers between devices: 3.57 us -> 1.8 us  [per_device(): total_got = lax.ppermute(total, 'ctx', xor_peers(peers, 12))]
    ppermute x1, starting transfers between devices: 3.79 us -> 4.84 us  [per_device(): got_state = lax.ppermute(send_state, 'ctx', xor_peers(peers, 1))]
  transfers between devices with their start and end apart: 15 -> 15, of which waited for: 12 -> 11; matrix products, arithmetic and copies ran while one was open for 0% -> 0% of each run, Pallas kernels for 6% -> 6%
where the time goes in v3:
time: 65.7 us; the launch traced here: 64.8 us
  starting transfers between devices  30.1 us (46%)
  waiting for transfers between devices  20.5 us (31%)
  Pallas kernels  13.6 us (21%)
  between operations  0.74 us (1%)
    pallas_call x10, Pallas kernels, call(): pl.pallas_call(kernel, out_shape=outs, scratch_shapes=scratch, in_specs=s...  13.6 us
    ppermute x3, waiting for transfers between devices, per_device(): lax.ppermute(o, 'head', xor_peers(4, s))  8.63 us
    ppermute x6, waiting for transfers between devices, per_device(): lax.ppermute(m, 'ctx', xor_peers(peers, 2 * s))  7.5 us
    ppermute x6, starting transfers between devices, per_device(): lax.ppermute(m, 'ctx', xor_peers(peers, 2 * s))  7.25 us
    ppermute x1, starting transfers between devices, per_device(): total_got = lax.ppermute(total, 'ctx', xor_peers(peers, 12))  6.1 us
    ppermute x1, starting transfers between devices, per_device(): got_state = lax.ppermute(send_state, 'ctx', xor_peers(peers, 1))  4.84 us
    ppermute x3, starting transfers between devices, per_device(): r1, r2, r3 = [lax.ppermute(r0, 'ctx', pairs) for pairs in rows]  4.63 us
    ppermute x3, starting transfers between devices, per_device(): lax.ppermute(o, 'head', xor_peers(4, s))  3.95 us
  transfers between devices with their start and end apart: 15, of which 11 were waited for; matrix products, arithmetic and copies ran while one was open for 0% of the time, Pallas kernels for 6%

profile of v3, /device:TPU:1, one launch (start us, length us, event | category | flops | bytes accessed | tf_op | source)
XLA Modules:
  0.0 64.8 jit_solution(3415454486664639569)
XLA Ops:
  0.6 4.6 %shard_map.104 = (f32[4,136,256]{2,1,0:T(8,128)S(1)}, f32[4,128,128]{2,1,0:T(8,128)S(1)}, f32[4,128,256]{2,1,0:T(8,128)S(1)}, f32[4,128,128]{2,1,0:T(8,128)S(1)}...) custom-call(bf16[128,512]{1,0:T(8,128)(2,1)} %q.1, ...), custom_call_target="tpu_custom_call" | custom-call | tf_op jit(solution)/shard_map/pallas_call | solution.py:387
  5.2 3.3 %collective-permute-start = (f32[4,136,256]{2,1,0:T(8,128)S(1)}, f32[4,136,256]{2,1,0:T(8,128)S(1)}, u32[]{:S(2)}, u32[]{:S(2)}) collective-permute-start(f32[4,136,256]{2,1,0:T(8,128)S(1)} %get-tuple-element.44), channel_id=1, source_target_pairs={{0,4},{4,0},{8,12},{12,8},{16,20},{20,16},{24,28},{28,24},{32,36},... | collective-permute-start | bytes 1671176 | tf_op jit(solution)/shard_map/ppermute | solution.py:426
  8.5 3.4 %shard_map.105 = (f32[4,136,256]{2,1,0:T(8,128)S(1)}, f32[4,128,128]{2,1,0:T(8,128)S(1)}, f32[4,128,256]{2,1,0:T(8,128)S(1)}, f32[4,128,128]{2,1,0:T(8,128)S(1)}) custom-call(bf16[128,512]{1,0:T(8,128)(2,1)S(1)} %get-tuple-element.37.q, bf16[128,512]{1,0:T(8,128)(2,1)S(1)} %get-tuple-element.38.k, bf16[128,1024]{1,0:T(8,128)(2,1)S(1)} %get-tuple-element.39.v, ...), custom_call_target="tpu_custom_call" | custom-call | flops 1000000000 | tf_op jit(solution)/shard_map/pallas_call | solution.py:387
  12.5 2.9 %collective-permute-start.2 = (bf16[144,256]{1,0:T(8,128)(2,1)S(1)}, bf16[144,256]{1,0:T(8,128)(2,1)S(1)}, u32[]{:S(2)}, u32[]{:S(2)}) collective-permute-start(bf16[144,256]{1,0:T(8,128)(2,1)S(1)} %get-tuple-element.47), channel_id=1, source_target_pairs={{0,16},{4,20},{8,24},{12,28},{16,0},{20,4},{24,8},{28,12},{32,48},... | collective-permute-start | bytes 221192 | tf_op jit(solution)/shard_map/ppermute | solution.py:434
  16.3 1.6 %collective-permute-done.2.m2 = bf16[144,256]{1,0:T(8,128)(2,1)S(1)} collective-permute-done((bf16[144,256]{1,0:T(8,128)(2,1)S(1)}, bf16[144,256]{1,0:T(8,128)(2,1)S(1)}, u32[]{:S(2)}, u32[]{:S(2)}) %collective-permute-start.2) | collective-permute-done | bytes 73760 | tf_op jit(solution)/shard_map/ppermute | solution.py:434
  17.9 2.5 %collective-permute-done.3.m3 = bf16[144,256]{1,0:T(8,128)(2,1)S(1)} collective-permute-done((bf16[144,256]{1,0:T(8,128)(2,1)S(1)}, bf16[144,256]{1,0:T(8,128)(2,1)S(1)}, u32[]{:S(2)}, u32[]{:S(2)}) %collective-permute-start.3) | collective-permute-done | bytes 73760 | tf_op jit(solution)/shard_map/ppermute | solution.py:434
  20.9 6.1 %collective-permute-start.4 = (bf16[144,256]{1,0:T(8,128)(2,1)S(1)}, bf16[144,256]{1,0:T(8,128)(2,1)S(1)}, u32[]{:S(2)}, u32[]{:S(2)}) collective-permute-start(bf16[144,256]{1,0:T(8,128)(2,1)S(1)} %get-tuple-element.49.own), channel_id=1, source_target_pairs={{0,48},{4,52},{8,56},{12,60},{16,32},{20,36},{24,40},{28,44},{32,1... | collective-permute-start | bytes 221192 | tf_op jit(solution)/shard_map/ppermute | solution.py:448
  27.0 1.8 %collective-permute-done.4.got = bf16[144,256]{1,0:T(8,128)(2,1)S(1)} collective-permute-done((bf16[144,256]{1,0:T(8,128)(2,1)S(1)}, bf16[144,256]{1,0:T(8,128)(2,1)S(1)}, u32[]{:S(2)}, u32[]{:S(2)}) %collective-permute-start.4) | collective-permute-done | bytes 73760 | tf_op jit(solution)/shard_map/ppermute | solution.py:448
  29.0 1.4 %collective-permute-start.5 = (bf16[144,256]{1,0:T(8,128)(2,1)S(1)}, bf16[144,256]{1,0:T(8,128)(2,1)S(1)}, u32[]{:S(2)}, u32[]{:S(2)}) collective-permute-start(bf16[144,256]{1,0:T(8,128)(2,1)S(1)} %shard_map.108.r0), channel_id=1, source_target_pairs={{0,64},{4,68},{8,72},{12,76},{16,80},{20,84},{24,88},{28,92},{32,9... | collective-permute-start | bytes 221192 | tf_op jit(solution)/shard_map/ppermute | solution.py:457
  30.4 2.6 %collective-permute-start.6 = (bf16[144,256]{1,0:T(8,128)(2,1)S(1)}, bf16[144,256]{1,0:T(8,128)(2,1)S(1)}, u32[]{:S(2)}, u32[]{:S(2)}) collective-permute-start(bf16[144,256]{1,0:T(8,128)(2,1)S(1)} %shard_map.108.r0), channel_id=1, source_target_pairs={{0,128},{4,132},{8,136},{12,140},{16,144},{20,148},{24,152},{28,15... | collective-permute-start | bytes 221192 | tf_op jit(solution)/shard_map/ppermute | solution.py:457
  33.0 0.7 %collective-permute-start.7 = (bf16[144,256]{1,0:T(8,128)(2,1)S(1)}, bf16[144,256]{1,0:T(8,128)(2,1)S(1)}, u32[]{:S(2)}, u32[]{:S(2)}) collective-permute-start(bf16[144,256]{1,0:T(8,128)(2,1)S(1)} %shard_map.108.r0), channel_id=1, source_target_pairs={{128,64},{132,68},{136,72},{140,76},{144,80},{148,84},{152,88},{15... | collective-permute-start | bytes 221192 | tf_op jit(solution)/shard_map/ppermute | solution.py:457
  33.7 1.9 %collective-permute-done.6.r2 = bf16[144,256]{1,0:T(8,128)(2,1)S(1)} collective-permute-done((bf16[144,256]{1,0:T(8,128)(2,1)S(1)}, bf16[144,256]{1,0:T(8,128)(2,1)S(1)}, u32[]{:S(2)}, u32[]{:S(2)}) %collective-permute-start.6) | collective-permute-done | bytes 73760 | tf_op jit(solution)/shard_map/ppermute | solution.py:457
  35.6 1.0 %shard_map.109 = (bf16[144,128]{1,0:T(8,128)(2,1)S(1)}, bf16[144,128]{1,0:T(8,128)(2,1)S(1)}, bf16[144,128]{1,0:T(8,128)(2,1)S(1)}, bf16[144,128]{1,0:T(8,128)(2,1)S(1)}) custom-call(bf16[144,256]{1,0:T(8,128)(2,1)S(1)} %shard_map.108.r0, bf16[144,256]{1,0:T(8,128)(2,1)S(1)} %collective-permute-done.5.r1, bf16[144,256]{1,0:T(8,128)(2,1)S(1)} %collective-permute-done.6.r2, ...), custom_call_target="tpu_custom_call" | custom-call | tf_op jit(solution)/shard_map/pallas_call | solution.py:387
  36.6 2.0 %collective-permute-start.9 = (bf16[144,128]{1,0:T(8,128)(2,1)S(1)}, bf16[144,128]{1,0:T(8,128)(2,1)S(1)}, u32[]{:S(2)}, u32[]{:S(2)}) collective-permute-start(bf16[144,128]{1,0:T(8,128)(2,1)S(1)} %get-tuple-element.54), channel_id=1, source_target_pairs={{0,16},{4,20},{8,24},{12,28},{16,0},{20,4},{24,8},{28,12},{32,48},... | collective-permute-start | bytes 110600 | tf_op jit(solution)/shard_map/ppermute | solution.py:469
  38.6 1.6 %collective-permute-start.10 = (bf16[144,128]{1,0:T(8,128)(2,1)S(1)}, bf16[144,128]{1,0:T(8,128)(2,1)S(1)}, u32[]{:S(2)}, u32[]{:S(2)}) collective-permute-start(bf16[144,128]{1,0:T(8,128)(2,1)S(1)} %get-tuple-element.55), channel_id=1, source_target_pairs={{0,24},{4,28},{8,16},{12,20},{16,8},{20,12},{24,0},{28,4},{32,56},... | collective-permute-start | bytes 110600 | tf_op jit(solution)/shard_map/ppermute | solution.py:469
  40.4 2.9 %collective-permute-done.10.s3 = bf16[144,128]{1,0:T(8,128)(2,1)S(1)} collective-permute-done((bf16[144,128]{1,0:T(8,128)(2,1)S(1)}, bf16[144,128]{1,0:T(8,128)(2,1)S(1)}, u32[]{:S(2)}, u32[]{:S(2)}) %collective-permute-start.10) | collective-permute-done | bytes 36896 | tf_op jit(solution)/shard_map/ppermute | solution.py:469
  43.7 4.8 %collective-permute-start.11 = (f32[4,136,128]{2,1,0:T(8,128)S(1)}, f32[4,136,128]{2,1,0:T(8,128)S(1)}, u32[]{:S(2)}, u32[]{:S(2)}) collective-permute-start(f32[4,136,128]{2,1,0:T(8,128)S(1)} %get-tuple-element.57), channel_id=1, source_target_pairs={{0,4},{4,0},{8,12},{12,8},{16,20},{20,16},{24,28},{28,24},{32,36},... | collective-permute-start | bytes 835592 | tf_op jit(solution)/shard_map/ppermute | solution.py:480
  49.7 1.2 %shard_map.112 = (f32[32,2048]{1,0:T(8,128)S(1)}, bf16[32,2176]{1,0:T(8,128)(2,1)S(1)}, bf16[32,2176]{1,0:T(8,128)(2,1)S(1)}, bf16[32,2176]{1,0:T(8,128)(2,1)S(1)}, bf16[32,128]{1,0:T(8,128)(2,1)S(1)}) custom-call(f32[4,136,128]{2,1,0:T(8,128)S(1)} %get-tuple-element.56.own, f32[4,136,128]{2,1,0:T(8,128)S(1)} %collective-permute-done.11.got, ...), custom_call_target="tpu_custom_call" | custom-call | tf_op jit(solution)/shard_map/pallas_call | solution.py:387
  51.0 1.3 %collective-permute-start.12 = (bf16[32,2176]{1,0:T(8,128)(2,1)S(1)}, bf16[32,2176]{1,0:T(8,128)(2,1)S(1)}, u32[]{:S(2)}, u32[]{:S(2)}) collective-permute-start(bf16[32,2176]{1,0:T(8,128)(2,1)S(1)} %get-tuple-element.68), channel_id=1, source_target_pairs={{0,1},{1,0},{2,3},{3,2},{4,5},{5,4},{6,7},{7,6},{8,9},{9,8},{10,11... | collective-permute-start | bytes 417800 | tf_op jit(solution)/shard_map/ppermute | solution.py:491
  52.3 2.5 %collective-permute-start.13 = (bf16[32,2176]{1,0:T(8,128)(2,1)S(1)}, bf16[32,2176]{1,0:T(8,128)(2,1)S(1)}, u32[]{:S(2)}, u32[]{:S(2)}) collective-permute-start(bf16[32,2176]{1,0:T(8,128)(2,1)S(1)} %get-tuple-element.69), channel_id=1, source_target_pairs={{0,2},{1,3},{2,0},{3,1},{4,6},{5,7},{6,4},{7,5},{8,10},{9,11},{10,... | collective-permute-start | bytes 417800 | tf_op jit(solution)/shard_map/ppermute | solution.py:491
  54.9 0.8 %collective-permute-done.12.r1 = bf16[32,2176]{1,0:T(8,128)(2,1)S(1)} collective-permute-done((bf16[32,2176]{1,0:T(8,128)(2,1)S(1)}, bf16[32,2176]{1,0:T(8,128)(2,1)S(1)}, u32[]{:S(2)}, u32[]{:S(2)}) %collective-permute-start.12) | collective-permute-done | bytes 139296 | tf_op jit(solution)/shard_map/ppermute | solution.py:491
  55.7 5.3 %collective-permute-done.13.r2 = bf16[32,2176]{1,0:T(8,128)(2,1)S(1)} collective-permute-done((bf16[32,2176]{1,0:T(8,128)(2,1)S(1)}, bf16[32,2176]{1,0:T(8,128)(2,1)S(1)}, u32[]{:S(2)}, u32[]{:S(2)}) %collective-permute-start.13) | collective-permute-done | bytes 139296 | tf_op jit(solution)/shard_map/ppermute | solution.py:491
  61.0 2.5 %collective-permute-done.14.r3 = bf16[32,2176]{1,0:T(8,128)(2,1)S(1)} collective-permute-done((bf16[32,2176]{1,0:T(8,128)(2,1)S(1)}, bf16[32,2176]{1,0:T(8,128)(2,1)S(1)}, u32[]{:S(2)}, u32[]{:S(2)}) %collective-permute-start.14) | collective-permute-done | bytes 139296 | tf_op jit(solution)/shard_map/ppermute | solution.py:491
  63.5 1.3 %shard_map.113 = (bf16[32,2048]{1,0:T(8,128)(2,1)}, f32[8,256]{1,0:T(8,128)}) custom-call(s32[32]{0:T(128)S(1)} %copy-done.1, f32[32,2048]{1,0:T(8,128)S(1)} %get-tuple-element.67.acc, bf16[32,2176]{1,0:T(8,128)(2,1)S(1)} %collective-permute-done.12.r1, bf16[32,2176]{1,0:T(8,128)(2,1)S(1)} %collective-permute-done.13.r2, ...), custom_call_target="tpu_custom_call" | custom-call | tf_op jit(solution)/shard_map/pallas_call | solution.py:387
  (22 shorter events, 4.3 us)
Async XLA Ops:
  0.6 47.9 %copy-start.2 = (bf16[128,1024]{1,0:T(8,128)(2,1)S(1)}, bf16[128,1024]{1,0:T(8,128)(2,1)}, u32[]{:S(2)}) copy-start(bf16[128,1024]{1,0:T(8,128)(2,1)} %gate.1) | copy-start | bytes 786436
  5.2 6.7 %collective-permute-start = (f32[4,136,256]{2,1,0:T(8,128)S(1)}, f32[4,136,256]{2,1,0:T(8,128)S(1)}, u32[]{:S(2)}, u32[]{:S(2)}) collective-permute-start(f32[4,136,256]{2,1,0:T(8,128)S(1)} %get-tuple-element.44), channel_id=1, source_target_pairs={{0,4},{4,0},{8,12},{12,8},{16,20},{20,16},{24,28},{28,24},{32,36},... | collective-permute-start | bytes 1671176 | tf_op jit(solution)/shard_map/ppermute | solution.py:426
  12.4 3.9 %collective-permute-start.1 = (bf16[144,256]{1,0:T(8,128)(2,1)S(1)}, bf16[144,256]{1,0:T(8,128)(2,1)S(1)}, u32[]{:S(2)}, u32[]{:S(2)}) collective-permute-start(bf16[144,256]{1,0:T(8,128)(2,1)S(1)} %get-tuple-element.46), channel_id=1, source_target_pairs={{0,8},{4,12},{8,0},{12,4},{16,24},{20,28},{24,16},{28,20},{32,40},... | collective-permute-start | bytes 221192 | tf_op jit(solution)/shard_map/ppermute | solution.py:434
  12.5 5.4 %collective-permute-start.2 = (bf16[144,256]{1,0:T(8,128)(2,1)S(1)}, bf16[144,256]{1,0:T(8,128)(2,1)S(1)}, u32[]{:S(2)}, u32[]{:S(2)}) collective-permute-start(bf16[144,256]{1,0:T(8,128)(2,1)S(1)} %get-tuple-element.47), channel_id=1, source_target_pairs={{0,16},{4,20},{8,24},{12,28},{16,0},{20,4},{24,8},{28,12},{32,48},... | collective-permute-start | bytes 221192 | tf_op jit(solution)/shard_map/ppermute | solution.py:434
  15.4 5.0 %collective-permute-start.3 = (bf16[144,256]{1,0:T(8,128)(2,1)S(1)}, bf16[144,256]{1,0:T(8,128)(2,1)S(1)}, u32[]{:S(2)}, u32[]{:S(2)}) collective-permute-start(bf16[144,256]{1,0:T(8,128)(2,1)S(1)} %get-tuple-element.48), channel_id=1, source_target_pairs={{0,24},{4,28},{8,16},{12,20},{16,8},{20,12},{24,0},{28,4},{32,56},... | collective-permute-start | bytes 221192 | tf_op jit(solution)/shard_map/ppermute | solution.py:434
  20.9 7.9 %collective-permute-start.4 = (bf16[144,256]{1,0:T(8,128)(2,1)S(1)}, bf16[144,256]{1,0:T(8,128)(2,1)S(1)}, u32[]{:S(2)}, u32[]{:S(2)}) collective-permute-start(bf16[144,256]{1,0:T(8,128)(2,1)S(1)} %get-tuple-element.49.own), channel_id=1, source_target_pairs={{0,48},{4,52},{8,56},{12,60},{16,32},{20,36},{24,40},{28,44},{32,1... | collective-permute-start | bytes 221192 | tf_op jit(solution)/shard_map/ppermute | solution.py:448
  29.0 4.6 %collective-permute-start.5 = (bf16[144,256]{1,0:T(8,128)(2,1)S(1)}, bf16[144,256]{1,0:T(8,128)(2,1)S(1)}, u32[]{:S(2)}, u32[]{:S(2)}) collective-permute-start(bf16[144,256]{1,0:T(8,128)(2,1)S(1)} %shard_map.108.r0), channel_id=1, source_target_pairs={{0,64},{4,68},{8,72},{12,76},{16,80},{20,84},{24,88},{28,92},{32,9... | collective-permute-start | bytes 221192 | tf_op jit(solution)/shard_map/ppermute | solution.py:457
  30.4 5.2 %collective-permute-start.6 = (bf16[144,256]{1,0:T(8,128)(2,1)S(1)}, bf16[144,256]{1,0:T(8,128)(2,1)S(1)}, u32[]{:S(2)}, u32[]{:S(2)}) collective-permute-start(bf16[144,256]{1,0:T(8,128)(2,1)S(1)} %shard_map.108.r0), channel_id=1, source_target_pairs={{0,128},{4,132},{8,136},{12,140},{16,144},{20,148},{24,152},{28,15... | collective-permute-start | bytes 221192 | tf_op jit(solution)/shard_map/ppermute | solution.py:457
  33.0 2.6 %collective-permute-start.7 = (bf16[144,256]{1,0:T(8,128)(2,1)S(1)}, bf16[144,256]{1,0:T(8,128)(2,1)S(1)}, u32[]{:S(2)}, u32[]{:S(2)}) collective-permute-start(bf16[144,256]{1,0:T(8,128)(2,1)S(1)} %shard_map.108.r0), channel_id=1, source_target_pairs={{128,64},{132,68},{136,72},{140,76},{144,80},{148,84},{152,88},{15... | collective-permute-start | bytes 221192 | tf_op jit(solution)/shard_map/ppermute | solution.py:457
  36.5 3.6 %collective-permute-start.8 = (bf16[144,128]{1,0:T(8,128)(2,1)S(1)}, bf16[144,128]{1,0:T(8,128)(2,1)S(1)}, u32[]{:S(2)}, u32[]{:S(2)}) collective-permute-start(bf16[144,128]{1,0:T(8,128)(2,1)S(1)} %get-tuple-element.53), channel_id=1, source_target_pairs={{0,8},{4,12},{8,0},{12,4},{16,24},{20,28},{24,16},{28,20},{32,40},... | collective-permute-start | bytes 110600 | tf_op jit(solution)/shard_map/ppermute | solution.py:469
  36.6 3.8 %collective-permute-start.9 = (bf16[144,128]{1,0:T(8,128)(2,1)S(1)}, bf16[144,128]{1,0:T(8,128)(2,1)S(1)}, u32[]{:S(2)}, u32[]{:S(2)}) collective-permute-start(bf16[144,128]{1,0:T(8,128)(2,1)S(1)} %get-tuple-element.54), channel_id=1, source_target_pairs={{0,16},{4,20},{8,24},{12,28},{16,0},{20,4},{24,8},{28,12},{32,48},... | collective-permute-start | bytes 110600 | tf_op jit(solution)/shard_map/ppermute | solution.py:469
  38.6 4.7 %collective-permute-start.10 = (bf16[144,128]{1,0:T(8,128)(2,1)S(1)}, bf16[144,128]{1,0:T(8,128)(2,1)S(1)}, u32[]{:S(2)}, u32[]{:S(2)}) collective-permute-start(bf16[144,128]{1,0:T(8,128)(2,1)S(1)} %get-tuple-element.55), channel_id=1, source_target_pairs={{0,24},{4,28},{8,16},{12,20},{16,8},{20,12},{24,0},{28,4},{32,56},... | collective-permute-start | bytes 110600 | tf_op jit(solution)/shard_map/ppermute | solution.py:469
  43.3 6.4 %copy-start = (bf16[1024,2048]{1,0:T(8,128)(2,1)S(1)}, bf16[1024,2048]{1,0:T(8,128)(2,1)}, u32[]{:S(2)}) copy-start(bf16[1024,2048]{1,0:T(8,128)(2,1)} %w.1) | copy-start | bytes 12582916
  43.7 6.0 %collective-permute-start.11 = (f32[4,136,128]{2,1,0:T(8,128)S(1)}, f32[4,136,128]{2,1,0:T(8,128)S(1)}, u32[]{:S(2)}, u32[]{:S(2)}) collective-permute-start(f32[4,136,128]{2,1,0:T(8,128)S(1)} %get-tuple-element.57), channel_id=1, source_target_pairs={{0,4},{4,0},{8,12},{12,8},{16,20},{20,16},{24,28},{28,24},{32,36},... | collective-permute-start | bytes 835592 | tf_op jit(solution)/shard_map/ppermute | solution.py:480
  49.1 14.5 %copy-start.1 = (s32[32]{0:T(128)S(1)}, s32[32]{0:T(128)}, u32[]{:S(2)}) copy-start(s32[32]{0:T(128)} %order.1) | copy-start | bytes 388
  51.0 4.8 %collective-permute-start.12 = (bf16[32,2176]{1,0:T(8,128)(2,1)S(1)}, bf16[32,2176]{1,0:T(8,128)(2,1)S(1)}, u32[]{:S(2)}, u32[]{:S(2)}) collective-permute-start(bf16[32,2176]{1,0:T(8,128)(2,1)S(1)} %get-tuple-element.68), channel_id=1, source_target_pairs={{0,1},{1,0},{2,3},{3,2},{4,5},{5,4},{6,7},{7,6},{8,9},{9,8},{10,11... | collective-permute-start | bytes 417800 | tf_op jit(solution)/shard_map/ppermute | solution.py:491
  52.3 8.7 %collective-permute-start.13 = (bf16[32,2176]{1,0:T(8,128)(2,1)S(1)}, bf16[32,2176]{1,0:T(8,128)(2,1)S(1)}, u32[]{:S(2)}, u32[]{:S(2)}) collective-permute-start(bf16[32,2176]{1,0:T(8,128)(2,1)S(1)} %get-tuple-element.69), channel_id=1, source_target_pairs={{0,2},{1,3},{2,0},{3,1},{4,6},{5,7},{6,4},{7,5},{8,10},{9,11},{10,... | collective-permute-start | bytes 417800 | tf_op jit(solution)/shard_map/ppermute | solution.py:491
  54.7 8.8 %collective-permute-start.14 = (bf16[32,2176]{1,0:T(8,128)(2,1)S(1)}, bf16[32,2176]{1,0:T(8,128)(2,1)S(1)}, u32[]{:S(2)}, u32[]{:S(2)}) collective-permute-start(bf16[32,2176]{1,0:T(8,128)(2,1)S(1)} %get-tuple-element.70), channel_id=1, source_target_pairs={{0,3},{1,2},{2,1},{3,0},{4,7},{5,6},{6,5},{7,4},{8,11},{9,10},{10,... | collective-permute-start | bytes 417800 | tf_op jit(solution)/shard_map/ppermute | solution.py:491

commit v4 on v3

--- a/solution.py
+++ b/solution.py
@@ -135,8 +135,12 @@
     return inv
 
 
-def local_maps(heads, q_ref, k_ref, v_ref, g_ref, b_ref, seg_ref, out, mixes, both, reads, waits=None):
-    q_wait, v_wait = waits or (None, None)
+def unit(x):
+    x = x.astype(f32)
+    return lax.rsqrt(jnp.sum(x * x, axis=-1, keepdims=True) + EPS)
+
+
+def local_maps(heads, k_ref, v_ref, g_ref, b_ref, seg_ref, out, mixes, both, sums, v_wait=None):
     groups = heads // 2
     ii, jj = iota((N, N), 0), iota((N, N), 1)
     doc_row = jnp.broadcast_to(seg_ref[...].astype(f32), (N, N))
@@ -144,7 +148,6 @@
     same = (doc_row == doc_col) & (ii >= jj)
     strict = same & (ii > jj)
     cont_row = doc_row[0:1] == doc_col[0:1]
-    cont_col = doc_col[:, 0:1] == doc_row[:, 0:1]
     last_col = doc_col[:, 0:1] == doc_row[:, N - 1 : N]
     first_doc, last_doc = doc_col[0:1], doc_col[N - 1 : N]
     upper = jnp.where(ii <= jj, 1.0, 0.0).astype(bf16)
@@ -157,80 +160,74 @@
     g2 = (g - g0.astype(f32) - g1.astype(f32)).astype(bf16)
     rows = mm(g0, upper) + mm(g1, upper) + mm(g2, upper)
     ks = [k_ref[:, pl.ds(pl.multiple_of((groups + i) * DK, DK), DK)] for i in range(count // 2)]
-
-    def unit(x):
-        x = x.astype(f32)
-        return lax.rsqrt(jnp.sum(x * x, axis=-1, keepdims=True) + EPS)
-
     cols = jnp.concatenate([rows, beta, jnp.zeros((N - 8 - count, N), f32)], 0).T
     cum = cols[:, :count]
     rk = [unit(k) for k in ks]
     rk_row = [jnp.broadcast_to(r, (N, N)).T[0:1] for r in rk]
     kts = [k.astype(f32).T.astype(bf16) for k in ks]
     kk = [mm(k, kt) for k, kt in zip(ks, kts)]
-    couplings, mixed = [], []
+    couplings = []
+    sums[...] = cols
     for h in range(count):
         i = h // 2
         gap = cum[:, h : h + 1] - rows[h : h + 1]
         mix = jnp.where(same, jnp.exp(jnp.minimum(gap, 0.0)), 0.0) * rk_row[i]
         couplings.append(jnp.where(strict, (cols[:, 8 + h : 9 + h] * rk[i]) * (mix * kk[i]), 0.0))
-        mixed.append(mix)
-    if q_wait:
-        q_wait()
-    qs = [q_ref[:, pl.ds(pl.multiple_of((groups + i) * DK, DK), DK)] for i in range(count // 2)]
-    rq = [unit(q) * DK ** (-0.5) for q in qs]
-    qk = [mm(q, kt) for q, kt in zip(qs, kts)]
-    for h in range(count):
-        mixes[h] = rq[h // 2] * (mixed[h] * qk[h // 2])
+        mixes[h] = mix
     inv = inverses(couplings)
     if v_wait:
         v_wait()
     for h in range(count):
         i = h // 2
         entry_row = jnp.where(cont_row, jnp.exp(rows[h : h + 1]), 0.0)
-        entry_col = jnp.where(cont_col, jnp.exp(cum[:, h : h + 1]), 0.0)
         beta_row = beta[h : h + 1]
         weighted = mm_left(inv[h] * (beta_row * entry_row * rk_row[i]), ks[i])
         pseudo = mm_left(inv[h] * beta_row, v_ref[:, pl.ds(pl.multiple_of((heads + h) * DV, DV), DV)])
         pair = jnp.concatenate([weighted, pseudo], 1)
         both[h] = pair
-        reads[h] = (entry_col * rq[i]) * qs[i].astype(f32)
         last_gap = jnp.minimum(cum[N - 1 : N, h : h + 1] - cum[:, h : h + 1], 0.0)
         last_keys = jnp.where(last_col, jnp.exp(last_gap), 0.0) * rk[i]
         written = mm_right(kts[i], last_keys * pair)
         pack_wide(out, (h,), entry_row[:, N - 1 :], written[:, :DK], written[:, DK:], first_doc, last_doc)
 
 
-def send_maps(q, k, v, g, b, seg, out, mixes, both, reads, q_in, k_in, v_in, g_in, b_in, seg_in, sems):
+def send_maps(k, v, g, b, seg, out, mixes, both, sums, k_in, v_in, g_in, b_in, seg_in, sems):
     moves = [
         pltpu.make_async_copy(src, dst, sems.at[i])
-        for i, (src, dst) in enumerate(
-            ((seg, seg_in), (g, g_in), (b, b_in), (k, k_in), (q, q_in), (v, v_in))
-        )
+        for i, (src, dst) in enumerate(((k, k_in), (seg, seg_in), (g, g_in), (b, b_in), (v, v_in)))
     ]
     for move in moves:
         move.start()
     for move in moves[:4]:
         move.wait()
     heads = (1 - places()[0]) * out.shape[0]
-    waits = (moves[4].wait, moves[5].wait)
-    local_maps(heads, q_in, k_in, v_in, g_in, b_in, seg_in, out, mixes, both, reads, waits)
-
-
-def own_maps(q, k, v, g, b, seg, out, mixes, both, reads):
-    local_maps(places()[0] * out.shape[0], q, k, v, g, b, seg, out, mixes, both, reads)
-
-
-def local_reads(mixes0, both0, reads0, mixes1, both1, reads1, gate, local, read, silu):
+    local_maps(heads, k_in, v_in, g_in, b_in, seg_in, out, mixes, both, sums, moves[4].wait)
+
+
+def own_maps(k, v, g, b, seg, out, mixes, both, sums):
+    local_maps(places()[0] * out.shape[0], k, v, g, b, seg, out, mixes, both, sums)
+
+
+def local_reads(mixes0, both0, sums0, mixes1, both1, sums1, q_ref, k_ref, seg_ref, gate, local, read, silu):
     core = places()[0]
     half = mixes0.shape[0]
     width = half * DV
-    for part, (mixes, both, reads) in enumerate(((mixes0, both0, reads0), (mixes1, both1, reads1))):
+    docs = jnp.broadcast_to(seg_ref[...].astype(f32), (N, N))
+    cont_col = docs.T[:, 0:1] == docs[:, 0:1]
+    for part, (mixes, both, sums) in enumerate(((mixes0, both0, sums0), (mixes1, both1, sums1))):
+        first = (core ^ part) * half
         for h in range(half):
-            mixed = mm_both(mixes[h], both[h])
-            local[part * half + h] = mixed[:, DK:]
-            read[part * half + h] = reads[h] - mixed[:, :DK]
-        first = pl.multiple_of((core ^ part) * width, width)
+            if h % 2 == 0:
+                lanes = pl.ds(pl.multiple_of((first // 2 + h // 2) * DK, DK), DK)
+                q = q_ref[:, lanes]
+                rq = unit(q) * DK ** (-0.5)
+                qk = rq * lax.dot_general(q, k_ref[:, lanes], (((1,), (1,)), ((), ())), preferred_element_type=f32)
+            at = part * half + h
+            mixed = mm_both(mixes[h] * qk, both[h])
+            entry_col = jnp.where(cont_col, jnp.exp(sums[:, h : h + 1]), 0.0)
+            local[at] = mixed[:, DK:]
+            read[at] = (entry_col * rq) * q.astype(f32) - mixed[:, :DK]
+        first = pl.multiple_of(first * DV, width)
         z = gate[:, pl.ds(first, width)].astype(f32)
         silu[:, part * width : (part + 1) * width] = z / (1.0 + jnp.exp(-z))
 
@@ -275,16 +272,16 @@
         maps[(y + 4 - s) % 4] = r[...]
     halves[high] = own[...]
     halves[1 - high] = got[...]
-    state = jnp.zeros((DK, DV), f32)
-    incoming = state
-    before = jnp.full((1, DK), -1.0, f32)
-    for t in range(4):
-        row = parse(maps[t])
-        entering = jnp.where(before == row[3], 1.0, 0.0) * state
-        incoming = jnp.where(y == t, entering, incoming)
-        state = apply_map(row, 1.0, entering)
-        before = row[4]
-    final[...] = state
+
+    def after(newer, older, there):
+        link = jnp.where(older[4] == newer[3], there, 0.0)
+        return apply_map(newer, 1.0, link * older[2])
+
+    row = parse(maps[y])
+    last, older = parse(maps[(y + 3) % 4]), parse(maps[(y + 2) % 4])
+    reached = after(last, older, jnp.where(y >= 2, 1.0, 0.0))
+    incoming = jnp.where(last[4] == row[3], jnp.where(y >= 1, 1.0, 0.0), 0.0) * reached
+    final[...] = after(parse(maps[3]), parse(maps[2]), 1.0)
     first_half = parse(halves[0])
     link = jnp.where(first_half[4] == parse(halves[1])[3], 1.0, 0.0)
     start = jnp.where(high == 1, apply_map(first_half, link, incoming), incoming)
@@ -413,18 +410,18 @@
         shape((half,) + wide, f32),
         shape((half, N, N), f32),
         shape((half, N, 256), f32),
-        shape((half, N, DK), f32),
+        shape((N, N), f32),
     ]
-    inputs = (queries, keys, values, log_decay.T, write_strength.T, seg)
-    send, mixes1, both1, reads1, *held = call(
+    inputs = (keys, values, log_decay.T, write_strength.T, seg)
+    send, mixes1, both1, sums1, *held = call(
         send_maps,
         maps + [shape(a.shape, a.dtype) for a in inputs],
-        [pltpu.SemaphoreType.DMA((6,))],
+        [pltpu.SemaphoreType.DMA((5,))],
         *inputs,
-        hbm=range(6),
+        hbm=range(5),
     )
     got = lax.ppermute(send, "ctx", xor_peers(peers, 1))
-    own, mixes0, both0, reads0 = call(own_maps, maps, [], *held, flops=10**9)
+    own, mixes0, both0, sums0 = call(own_maps, maps, [], *held, flops=10**9)
     m0, m1, m2, m3 = call(
         pair_maps,
         [shape(block)] * 4,
@@ -436,7 +433,7 @@
         local_reads,
         [shape((heads, N, DV), f32), shape((heads, N, DK), f32), shape((N, heads * DV), f32)],
         [],
-        mixes0, both0, reads0, mixes1, both1, reads1, out_gate,
+        mixes0, both0, sums0, mixes1, both1, sums1, queries, held[0], held[4], out_gate,
         flops=2 * 10**9,
     )
     total, prefix, prefix_row = call(

time: 65.7 us -> 65.3 us (level)
  transfers between devices with their start and end apart: 15 -> 15, of which waited for: 11 -> 11; matrix products, arithmetic and copies ran while one was open for 0% -> 0% of each run, Pallas kernels for 6% -> 7%
where the time goes in v4:
time: 65.3 us; the launch traced here: 64.3 us
  starting transfers between devices  29.9 us (46%)
  waiting for transfers between devices  20.1 us (31%)
  Pallas kernels  13.6 us (21%)
  between operations  0.75 us (1%)
    pallas_call x10, Pallas kernels, call(): pl.pallas_call(kernel, out_shape=outs, scratch_shapes=scratch, in_specs=s...  13.6 us
    ppermute x3, waiting for transfers between devices, per_device(): lax.ppermute(o, 'head', xor_peers(4, s))  8.63 us
    ppermute x6, waiting for transfers between devices, per_device(): lax.ppermute(m, 'ctx', xor_peers(peers, 2 * s))  7.67 us
    ppermute x6, starting transfers between devices, per_device(): lax.ppermute(m, 'ctx', xor_peers(peers, 2 * s))  7.25 us
    ppermute x1, starting transfers between devices, per_device(): total_got = lax.ppermute(total, 'ctx', xor_peers(peers, 12))  6.08 us
    ppermute x1, starting transfers between devices, per_device(): got_state = lax.ppermute(send_state, 'ctx', xor_peers(peers, 1))  4.69 us
    ppermute x3, starting transfers between devices, per_device(): r1, r2, r3 = [lax.ppermute(r0, 'ctx', pairs) for pairs in rows]  4.65 us
    ppermute x3, starting transfers between devices, per_device(): lax.ppermute(o, 'head', xor_peers(4, s))  3.95 us
  transfers between devices with their start and end apart: 15, of which 11 were waited for; matrix products, arithmetic and copies ran while one was open for 0% of the time, Pallas kernels for 7%

profile of v4, /device:TPU:1, one launch (start us, length us, event | category | flops | bytes accessed | tf_op | source)
XLA Modules:
  0.0 64.3 jit_solution(8075899254974630311)
XLA Ops:
  0.7 4.5 %shard_map.104 = (f32[4,136,256]{2,1,0:T(8,128)S(1)}, f32[4,128,128]{2,1,0:T(8,128)S(1)}, f32[4,128,256]{2,1,0:T(8,128)S(1)}, f32[128,128]{1,0:T(8,128)S(1)}, bf...) custom-call(bf16[128,512]{1,0:T(8,128)(2,1)} %k.1, ...), custom_call_target="tpu_custom_call" | custom-call | tf_op jit(solution)/shard_map/pallas_call | solution.py:384
  5.1 3.3 %collective-permute-start = (f32[4,136,256]{2,1,0:T(8,128)S(1)}, f32[4,136,256]{2,1,0:T(8,128)S(1)}, u32[]{:S(2)}, u32[]{:S(2)}) collective-permute-start(f32[4,136,256]{2,1,0:T(8,128)S(1)} %get-tuple-element.42), channel_id=1, source_target_pairs={{0,4},{4,0},{8,12},{12,8},{16,20},{20,16},{24,28},{28,24},{32,36},... | collective-permute-start | bytes 1671176 | tf_op jit(solution)/shard_map/ppermute | solution.py:423
  8.4 3.3 %shard_map.105 = (f32[4,136,256]{2,1,0:T(8,128)S(1)}, f32[4,128,128]{2,1,0:T(8,128)S(1)}, f32[4,128,256]{2,1,0:T(8,128)S(1)}, f32[128,128]{1,0:T(8,128)S(1)}) custom-call(bf16[128,512]{1,0:T(8,128)(2,1)S(1)} %get-tuple-element.36.k.k_ref, bf16[128,1024]{1,0:T(8,128)(2,1)S(1)} %get-tuple-element.37.v, f32[8,128]{1,0:T(8,128)S(1)} %get-tuple-element.38.g, ...), custom_call_target="tpu_custom_call" | custom-call | flops 1000000000 | tf_op jit(solution)/shard_map/pallas_call | solution.py:384
  12.3 2.9 %collective-permute-start.2 = (bf16[144,256]{1,0:T(8,128)(2,1)S(1)}, bf16[144,256]{1,0:T(8,128)(2,1)S(1)}, u32[]{:S(2)}, u32[]{:S(2)}) collective-permute-start(bf16[144,256]{1,0:T(8,128)(2,1)S(1)} %get-tuple-element.45), channel_id=1, source_target_pairs={{0,16},{4,20},{8,24},{12,28},{16,0},{20,4},{24,8},{28,12},{32,48},... | collective-permute-start | bytes 221192 | tf_op jit(solution)/shard_map/ppermute | solution.py:431
  16.1 1.6 %collective-permute-done.2.m2 = bf16[144,256]{1,0:T(8,128)(2,1)S(1)} collective-permute-done((bf16[144,256]{1,0:T(8,128)(2,1)S(1)}, bf16[144,256]{1,0:T(8,128)(2,1)S(1)}, u32[]{:S(2)}, u32[]{:S(2)}) %collective-permute-start.2) | collective-permute-done | bytes 73760 | tf_op jit(solution)/shard_map/ppermute | solution.py:431
  17.7 2.5 %collective-permute-done.3.m3 = bf16[144,256]{1,0:T(8,128)(2,1)S(1)} collective-permute-done((bf16[144,256]{1,0:T(8,128)(2,1)S(1)}, bf16[144,256]{1,0:T(8,128)(2,1)S(1)}, u32[]{:S(2)}, u32[]{:S(2)}) %collective-permute-start.3) | collective-permute-done | bytes 73760 | tf_op jit(solution)/shard_map/ppermute | solution.py:431
  20.7 6.1 %collective-permute-start.4 = (bf16[144,256]{1,0:T(8,128)(2,1)S(1)}, bf16[144,256]{1,0:T(8,128)(2,1)S(1)}, u32[]{:S(2)}, u32[]{:S(2)}) collective-permute-start(bf16[144,256]{1,0:T(8,128)(2,1)S(1)} %get-tuple-element.47.own), channel_id=1, source_target_pairs={{0,48},{4,52},{8,56},{12,60},{16,32},{20,36},{24,40},{28,44},{32,1... | collective-permute-start | bytes 221192 | tf_op jit(solution)/shard_map/ppermute | solution.py:445
  26.8 1.8 %collective-permute-done.4.got = bf16[144,256]{1,0:T(8,128)(2,1)S(1)} collective-permute-done((bf16[144,256]{1,0:T(8,128)(2,1)S(1)}, bf16[144,256]{1,0:T(8,128)(2,1)S(1)}, u32[]{:S(2)}, u32[]{:S(2)}) %collective-permute-start.4) | collective-permute-done | bytes 73760 | tf_op jit(solution)/shard_map/ppermute | solution.py:445
  28.8 1.4 %collective-permute-start.5 = (bf16[144,256]{1,0:T(8,128)(2,1)S(1)}, bf16[144,256]{1,0:T(8,128)(2,1)S(1)}, u32[]{:S(2)}, u32[]{:S(2)}) collective-permute-start(bf16[144,256]{1,0:T(8,128)(2,1)S(1)} %shard_map.108.r0), channel_id=1, source_target_pairs={{0,64},{4,68},{8,72},{12,76},{16,80},{20,84},{24,88},{28,92},{32,9... | collective-permute-start | bytes 221192 | tf_op jit(solution)/shard_map/ppermute | solution.py:454
  30.2 2.6 %collective-permute-start.6 = (bf16[144,256]{1,0:T(8,128)(2,1)S(1)}, bf16[144,256]{1,0:T(8,128)(2,1)S(1)}, u32[]{:S(2)}, u32[]{:S(2)}) collective-permute-start(bf16[144,256]{1,0:T(8,128)(2,1)S(1)} %shard_map.108.r0), channel_id=1, source_target_pairs={{0,128},{4,132},{8,136},{12,140},{16,144},{20,148},{24,152},{28,15... | collective-permute-start | bytes 221192 | tf_op jit(solution)/shard_map/ppermute | solution.py:454
  32.8 0.7 %collective-permute-start.7 = (bf16[144,256]{1,0:T(8,128)(2,1)S(1)}, bf16[144,256]{1,0:T(8,128)(2,1)S(1)}, u32[]{:S(2)}, u32[]{:S(2)}) collective-permute-start(bf16[144,256]{1,0:T(8,128)(2,1)S(1)} %shard_map.108.r0), channel_id=1, source_target_pairs={{128,64},{132,68},{136,72},{140,76},{144,80},{148,84},{152,88},{15... | collective-permute-start | bytes 221192 | tf_op jit(solution)/shard_map/ppermute | solution.py:454
  33.5 1.9 %collective-permute-done.6.r2 = bf16[144,256]{1,0:T(8,128)(2,1)S(1)} collective-permute-done((bf16[144,256]{1,0:T(8,128)(2,1)S(1)}, bf16[144,256]{1,0:T(8,128)(2,1)S(1)}, u32[]{:S(2)}, u32[]{:S(2)}) %collective-permute-start.6) | collective-permute-done | bytes 73760 | tf_op jit(solution)/shard_map/ppermute | solution.py:454
  36.1 2.1 %collective-permute-start.9 = (bf16[144,128]{1,0:T(8,128)(2,1)S(1)}, bf16[144,128]{1,0:T(8,128)(2,1)S(1)}, u32[]{:S(2)}, u32[]{:S(2)}) collective-permute-start(bf16[144,128]{1,0:T(8,128)(2,1)S(1)} %get-tuple-element.52), channel_id=1, source_target_pairs={{0,16},{4,20},{8,24},{12,28},{16,0},{20,4},{24,8},{28,12},{32,48},... | collective-permute-start | bytes 110600 | tf_op jit(solution)/shard_map/ppermute | solution.py:466
  38.2 1.4 %collective-permute-start.10 = (bf16[144,128]{1,0:T(8,128)(2,1)S(1)}, bf16[144,128]{1,0:T(8,128)(2,1)S(1)}, u32[]{:S(2)}, u32[]{:S(2)}) collective-permute-start(bf16[144,128]{1,0:T(8,128)(2,1)S(1)} %get-tuple-element.53), channel_id=1, source_target_pairs={{0,24},{4,28},{8,16},{12,20},{16,8},{20,12},{24,0},{28,4},{32,56},... | collective-permute-start | bytes 110600 | tf_op jit(solution)/shard_map/ppermute | solution.py:466
  39.9 3.0 %collective-permute-done.10.s3 = bf16[144,128]{1,0:T(8,128)(2,1)S(1)} collective-permute-done((bf16[144,128]{1,0:T(8,128)(2,1)S(1)}, bf16[144,128]{1,0:T(8,128)(2,1)S(1)}, u32[]{:S(2)}, u32[]{:S(2)}) %collective-permute-start.10) | collective-permute-done | bytes 36896 | tf_op jit(solution)/shard_map/ppermute | solution.py:466
  43.3 4.7 %collective-permute-start.11 = (f32[4,136,128]{2,1,0:T(8,128)S(1)}, f32[4,136,128]{2,1,0:T(8,128)S(1)}, u32[]{:S(2)}, u32[]{:S(2)}) collective-permute-start(f32[4,136,128]{2,1,0:T(8,128)S(1)} %get-tuple-element.55), channel_id=1, source_target_pairs={{0,4},{4,0},{8,12},{12,8},{16,20},{20,16},{24,28},{28,24},{32,36},... | collective-permute-start | bytes 835592 | tf_op jit(solution)/shard_map/ppermute | solution.py:477
  48.0 1.1 %shard_map.111 = (f32[8,128,128]{2,1,0:T(8,128)S(1)}, f32[8,128,128]{2,1,0:T(8,128)S(1)}, f32[128,1024]{1,0:T(8,128)S(1)}) custom-call(f32[4,128,128]{2,1,0:T(8,128)S(1)} %get-tuple-element.56.mixes0, f32[4,128,256]{2,1,0:T(8,128)S(1)} %get-tuple-element.57.both0, f32[128,128]{1,0:T(8,128)S(1)} %get-tuple-element.58.sums0, ...), custom_call_target="tpu_custom_call" | custom-call | flops 2000000000 | tf_op jit(solution)/shard_map/pallas_call | solution.py:384
  49.2 1.3 %shard_map.112 = (f32[32,2048]{1,0:T(8,128)S(1)}, bf16[32,2176]{1,0:T(8,128)(2,1)S(1)}, bf16[32,2176]{1,0:T(8,128)(2,1)S(1)}, bf16[32,2176]{1,0:T(8,128)(2,1)S(1)}, bf16[32,128]{1,0:T(8,128)(2,1)S(1)}) custom-call(f32[4,136,128]{2,1,0:T(8,128)S(1)} %get-tuple-element.54.own, f32[4,136,128]{2,1,0:T(8,128)S(1)} %collective-permute-done.11.got, ...), custom_call_target="tpu_custom_call" | custom-call | tf_op jit(solution)/shard_map/pallas_call | solution.py:384
  50.5 1.3 %collective-permute-start.12 = (bf16[32,2176]{1,0:T(8,128)(2,1)S(1)}, bf16[32,2176]{1,0:T(8,128)(2,1)S(1)}, u32[]{:S(2)}, u32[]{:S(2)}) collective-permute-start(bf16[32,2176]{1,0:T(8,128)(2,1)S(1)} %get-tuple-element.66), channel_id=1, source_target_pairs={{0,1},{1,0},{2,3},{3,2},{4,5},{5,4},{6,7},{7,6},{8,9},{9,8},{10,11... | collective-permute-start | bytes 417800 | tf_op jit(solution)/shard_map/ppermute | solution.py:488
  51.8 2.5 %collective-permute-start.13 = (bf16[32,2176]{1,0:T(8,128)(2,1)S(1)}, bf16[32,2176]{1,0:T(8,128)(2,1)S(1)}, u32[]{:S(2)}, u32[]{:S(2)}) collective-permute-start(bf16[32,2176]{1,0:T(8,128)(2,1)S(1)} %get-tuple-element.67), channel_id=1, source_target_pairs={{0,2},{1,3},{2,0},{3,1},{4,6},{5,7},{6,4},{7,5},{8,10},{9,11},{10,... | collective-permute-start | bytes 417800 | tf_op jit(solution)/shard_map/ppermute | solution.py:488
  54.4 0.8 %collective-permute-done.12.r1 = bf16[32,2176]{1,0:T(8,128)(2,1)S(1)} collective-permute-done((bf16[32,2176]{1,0:T(8,128)(2,1)S(1)}, bf16[32,2176]{1,0:T(8,128)(2,1)S(1)}, u32[]{:S(2)}, u32[]{:S(2)}) %collective-permute-start.12) | collective-permute-done | bytes 139296 | tf_op jit(solution)/shard_map/ppermute | solution.py:488
  55.2 5.3 %collective-permute-done.13.r2 = bf16[32,2176]{1,0:T(8,128)(2,1)S(1)} collective-permute-done((bf16[32,2176]{1,0:T(8,128)(2,1)S(1)}, bf16[32,2176]{1,0:T(8,128)(2,1)S(1)}, u32[]{:S(2)}, u32[]{:S(2)}) %collective-permute-start.13) | collective-permute-done | bytes 139296 | tf_op jit(solution)/shard_map/ppermute | solution.py:488
  60.5 2.5 %collective-permute-done.14.r3 = bf16[32,2176]{1,0:T(8,128)(2,1)S(1)} collective-permute-done((bf16[32,2176]{1,0:T(8,128)(2,1)S(1)}, bf16[32,2176]{1,0:T(8,128)(2,1)S(1)}, u32[]{:S(2)}, u32[]{:S(2)}) %collective-permute-start.14) | collective-permute-done | bytes 139296 | tf_op jit(solution)/shard_map/ppermute | solution.py:488
  63.0 1.3 %shard_map.113 = (bf16[32,2048]{1,0:T(8,128)(2,1)}, f32[8,256]{1,0:T(8,128)}) custom-call(s32[32]{0:T(128)S(1)} %copy-done.1, f32[32,2048]{1,0:T(8,128)S(1)} %get-tuple-element.65.acc, bf16[32,2176]{1,0:T(8,128)(2,1)S(1)} %collective-permute-done.12.r1, bf16[32,2176]{1,0:T(8,128)(2,1)S(1)} %collective-permute-done.13.r2, ...), custom_call_target="tpu_custom_call" | custom-call | tf_op jit(solution)/shard_map/pallas_call | solution.py:384
  (24 shorter events, 3.8 us)
Async XLA Ops:
  0.6 47.4 %copy-start.3 = (bf16[128,512]{1,0:T(8,128)(2,1)S(1)}, bf16[128,512]{1,0:T(8,128)(2,1)}, u32[]{:S(2)}) copy-start(bf16[128,512]{1,0:T(8,128)(2,1)} %q_ref.1) | copy-start | bytes 393220
  0.6 47.4 %copy-start.2 = (bf16[128,1024]{1,0:T(8,128)(2,1)S(1)}, bf16[128,1024]{1,0:T(8,128)(2,1)}, u32[]{:S(2)}) copy-start(bf16[128,1024]{1,0:T(8,128)(2,1)} %gate.1) | copy-start | bytes 786436
  5.1 6.6 %collective-permute-start = (f32[4,136,256]{2,1,0:T(8,128)S(1)}, f32[4,136,256]{2,1,0:T(8,128)S(1)}, u32[]{:S(2)}, u32[]{:S(2)}) collective-permute-start(f32[4,136,256]{2,1,0:T(8,128)S(1)} %get-tuple-element.42), channel_id=1, source_target_pairs={{0,4},{4,0},{8,12},{12,8},{16,20},{20,16},{24,28},{28,24},{32,36},... | collective-permute-start | bytes 1671176 | tf_op jit(solution)/shard_map/ppermute | solution.py:423
  12.2 3.9 %collective-permute-start.1 = (bf16[144,256]{1,0:T(8,128)(2,1)S(1)}, bf16[144,256]{1,0:T(8,128)(2,1)S(1)}, u32[]{:S(2)}, u32[]{:S(2)}) collective-permute-start(bf16[144,256]{1,0:T(8,128)(2,1)S(1)} %get-tuple-element.44), channel_id=1, source_target_pairs={{0,8},{4,12},{8,0},{12,4},{16,24},{20,28},{24,16},{28,20},{32,40},... | collective-permute-start | bytes 221192 | tf_op jit(solution)/shard_map/ppermute | solution.py:431
  12.3 5.4 %collective-permute-start.2 = (bf16[144,256]{1,0:T(8,128)(2,1)S(1)}, bf16[144,256]{1,0:T(8,128)(2,1)S(1)}, u32[]{:S(2)}, u32[]{:S(2)}) collective-permute-start(bf16[144,256]{1,0:T(8,128)(2,1)S(1)} %get-tuple-element.45), channel_id=1, source_target_pairs={{0,16},{4,20},{8,24},{12,28},{16,0},{20,4},{24,8},{28,12},{32,48},... | collective-permute-start | bytes 221192 | tf_op jit(solution)/shard_map/ppermute | solution.py:431
  15.2 5.0 %collective-permute-start.3 = (bf16[144,256]{1,0:T(8,128)(2,1)S(1)}, bf16[144,256]{1,0:T(8,128)(2,1)S(1)}, u32[]{:S(2)}, u32[]{:S(2)}) collective-permute-start(bf16[144,256]{1,0:T(8,128)(2,1)S(1)} %get-tuple-element.46), channel_id=1, source_target_pairs={{0,24},{4,28},{8,16},{12,20},{16,8},{20,12},{24,0},{28,4},{32,56},... | collective-permute-start | bytes 221192 | tf_op jit(solution)/shard_map/ppermute | solution.py:431
  20.7 7.9 %collective-permute-start.4 = (bf16[144,256]{1,0:T(8,128)(2,1)S(1)}, bf16[144,256]{1,0:T(8,128)(2,1)S(1)}, u32[]{:S(2)}, u32[]{:S(2)}) collective-permute-start(bf16[144,256]{1,0:T(8,128)(2,1)S(1)} %get-tuple-element.47.own), channel_id=1, source_target_pairs={{0,48},{4,52},{8,56},{12,60},{16,32},{20,36},{24,40},{28,44},{32,1... | collective-permute-start | bytes 221192 | tf_op jit(solution)/shard_map/ppermute | solution.py:445
  28.8 4.7 %collective-permute-start.5 = (bf16[144,256]{1,0:T(8,128)(2,1)S(1)}, bf16[144,256]{1,0:T(8,128)(2,1)S(1)}, u32[]{:S(2)}, u32[]{:S(2)}) collective-permute-start(bf16[144,256]{1,0:T(8,128)(2,1)S(1)} %shard_map.108.r0), channel_id=1, source_target_pairs={{0,64},{4,68},{8,72},{12,76},{16,80},{20,84},{24,88},{28,92},{32,9... | collective-permute-start | bytes 221192 | tf_op jit(solution)/shard_map/ppermute | solution.py:454
  30.2 5.2 %collective-permute-start.6 = (bf16[144,256]{1,0:T(8,128)(2,1)S(1)}, bf16[144,256]{1,0:T(8,128)(2,1)S(1)}, u32[]{:S(2)}, u32[]{:S(2)}) collective-permute-start(bf16[144,256]{1,0:T(8,128)(2,1)S(1)} %shard_map.108.r0), channel_id=1, source_target_pairs={{0,128},{4,132},{8,136},{12,140},{16,144},{20,148},{24,152},{28,15... | collective-permute-start | bytes 221192 | tf_op jit(solution)/shard_map/ppermute | solution.py:454
  32.8 2.6 %collective-permute-start.7 = (bf16[144,256]{1,0:T(8,128)(2,1)S(1)}, bf16[144,256]{1,0:T(8,128)(2,1)S(1)}, u32[]{:S(2)}, u32[]{:S(2)}) collective-permute-start(bf16[144,256]{1,0:T(8,128)(2,1)S(1)} %shard_map.108.r0), channel_id=1, source_target_pairs={{128,64},{132,68},{136,72},{140,76},{144,80},{148,84},{152,88},{15... | collective-permute-start | bytes 221192 | tf_op jit(solution)/shard_map/ppermute | solution.py:454
  36.0 3.6 %collective-permute-start.8 = (bf16[144,128]{1,0:T(8,128)(2,1)S(1)}, bf16[144,128]{1,0:T(8,128)(2,1)S(1)}, u32[]{:S(2)}, u32[]{:S(2)}) collective-permute-start(bf16[144,128]{1,0:T(8,128)(2,1)S(1)} %get-tuple-element.51), channel_id=1, source_target_pairs={{0,8},{4,12},{8,0},{12,4},{16,24},{20,28},{24,16},{28,20},{32,40},... | collective-permute-start | bytes 110600 | tf_op jit(solution)/shard_map/ppermute | solution.py:466
  36.1 3.8 %collective-permute-start.9 = (bf16[144,128]{1,0:T(8,128)(2,1)S(1)}, bf16[144,128]{1,0:T(8,128)(2,1)S(1)}, u32[]{:S(2)}, u32[]{:S(2)}) collective-permute-start(bf16[144,128]{1,0:T(8,128)(2,1)S(1)} %get-tuple-element.52), channel_id=1, source_target_pairs={{0,16},{4,20},{8,24},{12,28},{16,0},{20,4},{24,8},{28,12},{32,48},... | collective-permute-start | bytes 110600 | tf_op jit(solution)/shard_map/ppermute | solution.py:466
  38.2 4.7 %collective-permute-start.10 = (bf16[144,128]{1,0:T(8,128)(2,1)S(1)}, bf16[144,128]{1,0:T(8,128)(2,1)S(1)}, u32[]{:S(2)}, u32[]{:S(2)}) collective-permute-start(bf16[144,128]{1,0:T(8,128)(2,1)S(1)} %get-tuple-element.53), channel_id=1, source_target_pairs={{0,24},{4,28},{8,16},{12,20},{16,8},{20,12},{24,0},{28,4},{32,56},... | collective-permute-start | bytes 110600 | tf_op jit(solution)/shard_map/ppermute | solution.py:466
  42.9 6.3 %copy-start = (bf16[1024,2048]{1,0:T(8,128)(2,1)S(1)}, bf16[1024,2048]{1,0:T(8,128)(2,1)}, u32[]{:S(2)}) copy-start(bf16[1024,2048]{1,0:T(8,128)(2,1)} %w.1) | copy-start | bytes 12582916
  43.3 5.9 %collective-permute-start.11 = (f32[4,136,128]{2,1,0:T(8,128)S(1)}, f32[4,136,128]{2,1,0:T(8,128)S(1)}, u32[]{:S(2)}, u32[]{:S(2)}) collective-permute-start(f32[4,136,128]{2,1,0:T(8,128)S(1)} %get-tuple-element.55), channel_id=1, source_target_pairs={{0,4},{4,0},{8,12},{12,8},{16,20},{20,16},{24,28},{28,24},{32,36},... | collective-permute-start | bytes 835592 | tf_op jit(solution)/shard_map/ppermute | solution.py:477
  49.1 13.9 %copy-start.1 = (s32[32]{0:T(128)S(1)}, s32[32]{0:T(128)}, u32[]{:S(2)}) copy-start(s32[32]{0:T(128)} %order.1) | copy-start | bytes 388
  50.5 4.8 %collective-permute-start.12 = (bf16[32,2176]{1,0:T(8,128)(2,1)S(1)}, bf16[32,2176]{1,0:T(8,128)(2,1)S(1)}, u32[]{:S(2)}, u32[]{:S(2)}) collective-permute-start(bf16[32,2176]{1,0:T(8,128)(2,1)S(1)} %get-tuple-element.66), channel_id=1, source_target_pairs={{0,1},{1,0},{2,3},{3,2},{4,5},{5,4},{6,7},{7,6},{8,9},{9,8},{10,11... | collective-permute-start | bytes 417800 | tf_op jit(solution)/shard_map/ppermute | solution.py:488
  51.8 8.7 %collective-permute-start.13 = (bf16[32,2176]{1,0:T(8,128)(2,1)S(1)}, bf16[32,2176]{1,0:T(8,128)(2,1)S(1)}, u32[]{:S(2)}, u32[]{:S(2)}) collective-permute-start(bf16[32,2176]{1,0:T(8,128)(2,1)S(1)} %get-tuple-element.67), channel_id=1, source_target_pairs={{0,2},{1,3},{2,0},{3,1},{4,6},{5,7},{6,4},{7,5},{8,10},{9,11},{10,... | collective-permute-start | bytes 417800 | tf_op jit(solution)/shard_map/ppermute | solution.py:488
  54.2 8.8 %collective-permute-start.14 = (bf16[32,2176]{1,0:T(8,128)(2,1)S(1)}, bf16[32,2176]{1,0:T(8,128)(2,1)S(1)}, u32[]{:S(2)}, u32[]{:S(2)}) collective-permute-start(bf16[32,2176]{1,0:T(8,128)(2,1)S(1)} %get-tuple-element.68), channel_id=1, source_target_pairs={{0,3},{1,2},{2,1},{3,0},{4,7},{5,6},{6,5},{7,4},{8,11},{9,10},{10,... | collective-permute-start | bytes 417800 | tf_op jit(solution)/shard_map/ppermute | solution.py:488

commit v5 on v4

--- a/solution.py
+++ b/solution.py
@@ -246,17 +246,16 @@
     low = places()[1]
     for s, m in enumerate((m0, m1, m2, m3)):
         maps[low ^ s] = m[...]
-    c, d, b, first, last = parse(maps[0])
-    current = (c, d.astype(f32), b, first, last)
-    for t in range(3):
-        later = parse(maps[t + 1])
-        prefix[t, :, :DK] = current[1]
-        prefix[t, :, DK:] = current[2]
-        row = iota((8, DK), 0)
-        link = jnp.where(current[4] == later[3], 1.0, 0.0)
-        prefix_row[t] = jnp.where(row == 0, current[0], link)
-        current = compose(current, later)
-    pack(total, *current)
+    parts = [parse(maps[t]) for t in range(4)]
+    wide = [(c, d.astype(f32), b, first, last) for c, d, b, first, last in parts]
+    two = compose(wide[0], parts[1])
+    pack(total, *compose(two, compose(wide[2], parts[3])))
+    row = iota((8, DK), 0)
+    for t, reached in enumerate((wide[0], two, compose(two, parts[2]))):
+        prefix[t, :, :DK] = reached[1]
+        prefix[t, :, DK:] = reached[2]
+        link = jnp.where(reached[4] == parts[t + 1][3], 1.0, 0.0)
+        prefix_row[t] = jnp.where(row == 0, reached[0], link)
 
 
 def row_map(own, got, out, maps):
@@ -308,12 +307,9 @@
         c, d, b, _, last = parse_wide(pair[0, j])
         link = jnp.where(last == parse_wide(pair[1, j])[3], 1.0, 0.0)
         start = starts[j, :DK]
-        states[0, j, :DK] = start.astype(f32)
-        states[1, j, :DK] = link * (c * start.astype(f32) - mm_left(d, start) + b)
-        rows = starts[j, DK:].astype(f32)
-        rows = jnp.concatenate([rows[:4] + rows[4:8], rows[8:12]], 0)
-        states[0, j, DK:] = rows
-        states[1, j, DK:] = rows
+        states[0, j] = starts[j]
+        states[1, j, :DK] = (link * (c * start.astype(f32) - mm_left(d, start) + b)).astype(bf16)
+        states[1, j, DK:] = starts[j, DK:]
     own_out[...] = states[core]
     send_out[...] = states[1 - core]
 
@@ -327,11 +323,12 @@
         gated = []
         for h in range(half):
             at = part * half + h
-            attention = local[at] + mm_both(read[at], states[h, :DK])
+            attention = local[at] + mm_left(read[at], states[h, :DK])
             mean_square = jnp.mean(attention * attention, axis=-1, keepdims=True)
             weight = lax.rsqrt(mean_square + EPS) * silu[:, at * DV : (at + 1) * DV]
             gated.append((attention * weight).astype(bf16))
-            lasts[(core ^ part) * half + h] = states[h, DK:]
+            rows = states[h, DK:].astype(f32)
+            lasts[(core ^ part) * half + h] = jnp.concatenate([rows[:4] + rows[4:8], rows[8:12]], 0)
         first = pl.multiple_of((core ^ part) * width, width)
         normed[:, pl.ds(first, width)] = jnp.concatenate(gated, 1)
     finals = []
@@ -466,10 +463,10 @@
     s1, s2, s3 = [lax.ppermute(m, "ctx", xor_peers(peers, 2 * s)) for s, m in ((1, s1), (2, s2), (3, s3))]
     own_state, send_state = call(
         pair_states,
-        [shape((half, N + 8, DV), f32)] * 2,
+        [shape((half, ROWS, DV))] * 2,
         [
             pltpu.VMEM((2, half) + wide, f32),
-            pltpu.VMEM((2, half, N + 8, DV), f32),
+            pltpu.VMEM((2, half, ROWS, DV), bf16),
             pltpu.VMEM((half, ROWS, DV), bf16),
         ],
         s0, s1, s2, s3, own, got,

time: 65.3 us -> 64.9 us (level)
  transfers between devices with their start and end apart: 15 -> 15, of which waited for: 11 -> 10; matrix products, arithmetic and copies ran while one was open for 0% -> 0% of each run, Pallas kernels for 7% -> 7%
where the time goes in v5:
time: 64.9 us; the launch traced here: 63.9 us
  starting transfers between devices  29.9 us (46%)
  waiting for transfers between devices  19.9 us (31%)
  Pallas kernels  13.3 us (20%)
  between operations  0.77 us (1%)
    pallas_call x10, Pallas kernels, call(): pl.pallas_call(kernel, out_shape=outs, scratch_shapes=scratch, in_specs=s...  13.3 us
    ppermute x3, waiting for transfers between devices, per_device(): lax.ppermute(o, 'head', xor_peers(4, s))  8.5 us
    ppermute x6, waiting for transfers between devices, per_device(): lax.ppermute(m, 'ctx', xor_peers(peers, 2 * s))  7.68 us
    ppermute x6, starting transfers between devices, per_device(): lax.ppermute(m, 'ctx', xor_peers(peers, 2 * s))  7.25 us
    ppermute x1, starting transfers between devices, per_device(): total_got = lax.ppermute(total, 'ctx', xor_peers(peers, 12))  6.09 us
    ppermute x1, starting transfers between devices, per_device(): got_state = lax.ppermute(send_state, 'ctx', xor_peers(peers, 1))  4.68 us
    ppermute x3, starting transfers between devices, per_device(): r1, r2, r3 = [lax.ppermute(r0, 'ctx', pairs) for pairs in rows]  4.63 us
    ppermute x3, starting transfers between devices, per_device(): lax.ppermute(o, 'head', xor_peers(4, s))  3.95 us
  transfers between devices with their start and end apart: 15, of which 10 were waited for; matrix products, arithmetic and copies ran while one was open for 0% of the time, Pallas kernels for 7%

profile of v5, /device:TPU:1, one launch (start us, length us, event | category | flops | bytes accessed | tf_op | source)
XLA Modules:
  0.0 63.9 jit_solution(17886209888157253567)
XLA Ops:
  0.7 4.5 %shard_map.104 = (f32[4,136,256]{2,1,0:T(8,128)S(1)}, f32[4,128,128]{2,1,0:T(8,128)S(1)}, f32[4,128,256]{2,1,0:T(8,128)S(1)}, f32[128,128]{1,0:T(8,128)S(1)}, bf...) custom-call(bf16[128,512]{1,0:T(8,128)(2,1)} %k.1, ...), custom_call_target="tpu_custom_call" | custom-call | tf_op jit(solution)/shard_map/pallas_call | solution.py:381
  5.1 3.3 %collective-permute-start = (f32[4,136,256]{2,1,0:T(8,128)S(1)}, f32[4,136,256]{2,1,0:T(8,128)S(1)}, u32[]{:S(2)}, u32[]{:S(2)}) collective-permute-start(f32[4,136,256]{2,1,0:T(8,128)S(1)} %get-tuple-element.42), channel_id=1, source_target_pairs={{0,4},{4,0},{8,12},{12,8},{16,20},{20,16},{24,28},{28,24},{32,36},... | collective-permute-start | bytes 1671176 | tf_op jit(solution)/shard_map/ppermute | solution.py:420
  8.4 3.3 %shard_map.105 = (f32[4,136,256]{2,1,0:T(8,128)S(1)}, f32[4,128,128]{2,1,0:T(8,128)S(1)}, f32[4,128,256]{2,1,0:T(8,128)S(1)}, f32[128,128]{1,0:T(8,128)S(1)}) custom-call(bf16[128,512]{1,0:T(8,128)(2,1)S(1)} %get-tuple-element.36.k.k_ref, bf16[128,1024]{1,0:T(8,128)(2,1)S(1)} %get-tuple-element.37.v, f32[8,128]{1,0:T(8,128)S(1)} %get-tuple-element.38.g, ...), custom_call_target="tpu_custom_call" | custom-call | flops 1000000000 | tf_op jit(solution)/shard_map/pallas_call | solution.py:381
  12.3 2.9 %collective-permute-start.2 = (bf16[144,256]{1,0:T(8,128)(2,1)S(1)}, bf16[144,256]{1,0:T(8,128)(2,1)S(1)}, u32[]{:S(2)}, u32[]{:S(2)}) collective-permute-start(bf16[144,256]{1,0:T(8,128)(2,1)S(1)} %get-tuple-element.45), channel_id=1, source_target_pairs={{0,16},{4,20},{8,24},{12,28},{16,0},{20,4},{24,8},{28,12},{32,48},... | collective-permute-start | bytes 221192 | tf_op jit(solution)/shard_map/ppermute | solution.py:428
  16.1 1.6 %collective-permute-done.2.m2 = bf16[144,256]{1,0:T(8,128)(2,1)S(1)} collective-permute-done((bf16[144,256]{1,0:T(8,128)(2,1)S(1)}, bf16[144,256]{1,0:T(8,128)(2,1)S(1)}, u32[]{:S(2)}, u32[]{:S(2)}) %collective-permute-start.2) | collective-permute-done | bytes 73760 | tf_op jit(solution)/shard_map/ppermute | solution.py:428
  17.7 2.5 %collective-permute-done.3.m3 = bf16[144,256]{1,0:T(8,128)(2,1)S(1)} collective-permute-done((bf16[144,256]{1,0:T(8,128)(2,1)S(1)}, bf16[144,256]{1,0:T(8,128)(2,1)S(1)}, u32[]{:S(2)}, u32[]{:S(2)}) %collective-permute-start.3) | collective-permute-done | bytes 73760 | tf_op jit(solution)/shard_map/ppermute | solution.py:428
  20.6 6.1 %collective-permute-start.4 = (bf16[144,256]{1,0:T(8,128)(2,1)S(1)}, bf16[144,256]{1,0:T(8,128)(2,1)S(1)}, u32[]{:S(2)}, u32[]{:S(2)}) collective-permute-start(bf16[144,256]{1,0:T(8,128)(2,1)S(1)} %get-tuple-element.47.own), channel_id=1, source_target_pairs={{0,48},{4,52},{8,56},{12,60},{16,32},{20,36},{24,40},{28,44},{32,1... | collective-permute-start | bytes 221192 | tf_op jit(solution)/shard_map/ppermute | solution.py:442
  26.7 1.8 %collective-permute-done.4.got = bf16[144,256]{1,0:T(8,128)(2,1)S(1)} collective-permute-done((bf16[144,256]{1,0:T(8,128)(2,1)S(1)}, bf16[144,256]{1,0:T(8,128)(2,1)S(1)}, u32[]{:S(2)}, u32[]{:S(2)}) %collective-permute-start.4) | collective-permute-done | bytes 73760 | tf_op jit(solution)/shard_map/ppermute | solution.py:442
  28.7 1.3 %collective-permute-start.5 = (bf16[144,256]{1,0:T(8,128)(2,1)S(1)}, bf16[144,256]{1,0:T(8,128)(2,1)S(1)}, u32[]{:S(2)}, u32[]{:S(2)}) collective-permute-start(bf16[144,256]{1,0:T(8,128)(2,1)S(1)} %shard_map.108.r0), channel_id=1, source_target_pairs={{0,64},{4,68},{8,72},{12,76},{16,80},{20,84},{24,88},{28,92},{32,9... | collective-permute-start | bytes 221192 | tf_op jit(solution)/shard_map/ppermute | solution.py:451
  30.1 2.6 %collective-permute-start.6 = (bf16[144,256]{1,0:T(8,128)(2,1)S(1)}, bf16[144,256]{1,0:T(8,128)(2,1)S(1)}, u32[]{:S(2)}, u32[]{:S(2)}) collective-permute-start(bf16[144,256]{1,0:T(8,128)(2,1)S(1)} %shard_map.108.r0), channel_id=1, source_target_pairs={{0,128},{4,132},{8,136},{12,140},{16,144},{20,148},{24,152},{28,15... | collective-permute-start | bytes 221192 | tf_op jit(solution)/shard_map/ppermute | solution.py:451
  32.7 0.7 %collective-permute-start.7 = (bf16[144,256]{1,0:T(8,128)(2,1)S(1)}, bf16[144,256]{1,0:T(8,128)(2,1)S(1)}, u32[]{:S(2)}, u32[]{:S(2)}) collective-permute-start(bf16[144,256]{1,0:T(8,128)(2,1)S(1)} %shard_map.108.r0), channel_id=1, source_target_pairs={{128,64},{132,68},{136,72},{140,76},{144,80},{148,84},{152,88},{15... | collective-permute-start | bytes 221192 | tf_op jit(solution)/shard_map/ppermute | solution.py:451
  33.4 1.9 %collective-permute-done.6.r2 = bf16[144,256]{1,0:T(8,128)(2,1)S(1)} collective-permute-done((bf16[144,256]{1,0:T(8,128)(2,1)S(1)}, bf16[144,256]{1,0:T(8,128)(2,1)S(1)}, u32[]{:S(2)}, u32[]{:S(2)}) %collective-permute-start.6) | collective-permute-done | bytes 73760 | tf_op jit(solution)/shard_map/ppermute | solution.py:451
  36.0 2.1 %collective-permute-start.9 = (bf16[144,128]{1,0:T(8,128)(2,1)S(1)}, bf16[144,128]{1,0:T(8,128)(2,1)S(1)}, u32[]{:S(2)}, u32[]{:S(2)}) collective-permute-start(bf16[144,128]{1,0:T(8,128)(2,1)S(1)} %get-tuple-element.52), channel_id=1, source_target_pairs={{0,16},{4,20},{8,24},{12,28},{16,0},{20,4},{24,8},{28,12},{32,48},... | collective-permute-start | bytes 110600 | tf_op jit(solution)/shard_map/ppermute | solution.py:463
  38.1 1.4 %collective-permute-start.10 = (bf16[144,128]{1,0:T(8,128)(2,1)S(1)}, bf16[144,128]{1,0:T(8,128)(2,1)S(1)}, u32[]{:S(2)}, u32[]{:S(2)}) collective-permute-start(bf16[144,128]{1,0:T(8,128)(2,1)S(1)} %get-tuple-element.53), channel_id=1, source_target_pairs={{0,24},{4,28},{8,16},{12,20},{16,8},{20,12},{24,0},{28,4},{32,56},... | collective-permute-start | bytes 110600 | tf_op jit(solution)/shard_map/ppermute | solution.py:463
  39.8 3.0 %collective-permute-done.10.s3 = bf16[144,128]{1,0:T(8,128)(2,1)S(1)} collective-permute-done((bf16[144,128]{1,0:T(8,128)(2,1)S(1)}, bf16[144,128]{1,0:T(8,128)(2,1)S(1)}, u32[]{:S(2)}, u32[]{:S(2)}) %collective-permute-start.10) | collective-permute-done | bytes 36896 | tf_op jit(solution)/shard_map/ppermute | solution.py:463
  43.1 4.7 %collective-permute-start.11 = (bf16[4,144,128]{2,1,0:T(8,128)(2,1)S(1)}, bf16[4,144,128]{2,1,0:T(8,128)(2,1)S(1)}, u32[]{:S(2)}, u32[]{:S(2)}) collective-permute-start(bf16[4,144,128]{2,1,0:T(8,128)(2,1)S(1)} %get-tuple-element.55), channel_id=1, source_target_pairs={{0,4},{4,0},{8,12},{12,8},{16,20},{20,16},{24,28},{28,24},{32,36},... | collective-permute-start | bytes 442376 | tf_op jit(solution)/shard_map/ppermute | solution.py:474
  47.8 1.1 %shard_map.111 = (f32[8,128,128]{2,1,0:T(8,128)S(1)}, f32[8,128,128]{2,1,0:T(8,128)S(1)}, f32[128,1024]{1,0:T(8,128)S(1)}) custom-call(f32[4,128,128]{2,1,0:T(8,128)S(1)} %get-tuple-element.56.mixes0, f32[4,128,256]{2,1,0:T(8,128)S(1)} %get-tuple-element.57.both0, f32[128,128]{1,0:T(8,128)S(1)} %get-tuple-element.58.sums0, ...), custom_call_target="tpu_custom_call" | custom-call | flops 2000000000 | tf_op jit(solution)/shard_map/pallas_call | solution.py:381
  49.0 1.2 %shard_map.112 = (f32[32,2048]{1,0:T(8,128)S(1)}, bf16[32,2176]{1,0:T(8,128)(2,1)S(1)}, bf16[32,2176]{1,0:T(8,128)(2,1)S(1)}, bf16[32,2176]{1,0:T(8,128)(2,1)S(1)}, bf16[32,128]{1,0:T(8,128)(2,1)S(1)}) custom-call(bf16[4,144,128]{2,1,0:T(8,128)(2,1)S(1)} %get-tuple-element.54.own, bf16[4,144,128]{2,1,0:T(8,128)(2,1)S(1)} %collective-permute-done.11.got, ...), custom_call_target="tpu_custom_call" | custom-call | tf_op jit(solution)/shard_map/pallas_call | solution.py:381
  50.1 1.3 %collective-permute-start.12 = (bf16[32,2176]{1,0:T(8,128)(2,1)S(1)}, bf16[32,2176]{1,0:T(8,128)(2,1)S(1)}, u32[]{:S(2)}, u32[]{:S(2)}) collective-permute-start(bf16[32,2176]{1,0:T(8,128)(2,1)S(1)} %get-tuple-element.66), channel_id=1, source_target_pairs={{0,1},{1,0},{2,3},{3,2},{4,5},{5,4},{6,7},{7,6},{8,9},{9,8},{10,11... | collective-permute-start | bytes 417800 | tf_op jit(solution)/shard_map/ppermute | solution.py:485
  51.4 2.5 %collective-permute-start.13 = (bf16[32,2176]{1,0:T(8,128)(2,1)S(1)}, bf16[32,2176]{1,0:T(8,128)(2,1)S(1)}, u32[]{:S(2)}, u32[]{:S(2)}) collective-permute-start(bf16[32,2176]{1,0:T(8,128)(2,1)S(1)} %get-tuple-element.67), channel_id=1, source_target_pairs={{0,2},{1,3},{2,0},{3,1},{4,6},{5,7},{6,4},{7,5},{8,10},{9,11},{10,... | collective-permute-start | bytes 417800 | tf_op jit(solution)/shard_map/ppermute | solution.py:485
  54.1 0.7 %collective-permute-done.12.r1 = bf16[32,2176]{1,0:T(8,128)(2,1)S(1)} collective-permute-done((bf16[32,2176]{1,0:T(8,128)(2,1)S(1)}, bf16[32,2176]{1,0:T(8,128)(2,1)S(1)}, u32[]{:S(2)}, u32[]{:S(2)}) %collective-permute-start.12) | collective-permute-done | bytes 139296 | tf_op jit(solution)/shard_map/ppermute | solution.py:485
  54.8 5.2 %collective-permute-done.13.r2 = bf16[32,2176]{1,0:T(8,128)(2,1)S(1)} collective-permute-done((bf16[32,2176]{1,0:T(8,128)(2,1)S(1)}, bf16[32,2176]{1,0:T(8,128)(2,1)S(1)}, u32[]{:S(2)}, u32[]{:S(2)}) %collective-permute-start.13) | collective-permute-done | bytes 139296 | tf_op jit(solution)/shard_map/ppermute | solution.py:485
  60.0 2.6 %collective-permute-done.14.r3 = bf16[32,2176]{1,0:T(8,128)(2,1)S(1)} collective-permute-done((bf16[32,2176]{1,0:T(8,128)(2,1)S(1)}, bf16[32,2176]{1,0:T(8,128)(2,1)S(1)}, u32[]{:S(2)}, u32[]{:S(2)}) %collective-permute-start.14) | collective-permute-done | bytes 139296 | tf_op jit(solution)/shard_map/ppermute | solution.py:485
  62.6 1.3 %shard_map.113 = (bf16[32,2048]{1,0:T(8,128)(2,1)}, f32[8,256]{1,0:T(8,128)}) custom-call(s32[32]{0:T(128)S(1)} %copy-done.1, f32[32,2048]{1,0:T(8,128)S(1)} %get-tuple-element.65.acc, bf16[32,2176]{1,0:T(8,128)(2,1)S(1)} %collective-permute-done.12.r1, bf16[32,2176]{1,0:T(8,128)(2,1)S(1)} %collective-permute-done.13.r2, ...), custom_call_target="tpu_custom_call" | custom-call | tf_op jit(solution)/shard_map/pallas_call | solution.py:381
  (24 shorter events, 3.6 us)
Async XLA Ops:
  0.6 47.2 %copy-start.3 = (bf16[128,512]{1,0:T(8,128)(2,1)S(1)}, bf16[128,512]{1,0:T(8,128)(2,1)}, u32[]{:S(2)}) copy-start(bf16[128,512]{1,0:T(8,128)(2,1)} %q_ref.1) | copy-start | bytes 393220
  0.6 47.2 %copy-start.2 = (bf16[128,1024]{1,0:T(8,128)(2,1)S(1)}, bf16[128,1024]{1,0:T(8,128)(2,1)}, u32[]{:S(2)}) copy-start(bf16[128,1024]{1,0:T(8,128)(2,1)} %gate.1) | copy-start | bytes 786436
  5.1 6.6 %collective-permute-start = (f32[4,136,256]{2,1,0:T(8,128)S(1)}, f32[4,136,256]{2,1,0:T(8,128)S(1)}, u32[]{:S(2)}, u32[]{:S(2)}) collective-permute-start(f32[4,136,256]{2,1,0:T(8,128)S(1)} %get-tuple-element.42), channel_id=1, source_target_pairs={{0,4},{4,0},{8,12},{12,8},{16,20},{20,16},{24,28},{28,24},{32,36},... | collective-permute-start | bytes 1671176 | tf_op jit(solution)/shard_map/ppermute | solution.py:420
  12.2 3.9 %collective-permute-start.1 = (bf16[144,256]{1,0:T(8,128)(2,1)S(1)}, bf16[144,256]{1,0:T(8,128)(2,1)S(1)}, u32[]{:S(2)}, u32[]{:S(2)}) collective-permute-start(bf16[144,256]{1,0:T(8,128)(2,1)S(1)} %get-tuple-element.44), channel_id=1, source_target_pairs={{0,8},{4,12},{8,0},{12,4},{16,24},{20,28},{24,16},{28,20},{32,40},... | collective-permute-start | bytes 221192 | tf_op jit(solution)/shard_map/ppermute | solution.py:428
  12.3 5.4 %collective-permute-start.2 = (bf16[144,256]{1,0:T(8,128)(2,1)S(1)}, bf16[144,256]{1,0:T(8,128)(2,1)S(1)}, u32[]{:S(2)}, u32[]{:S(2)}) collective-permute-start(bf16[144,256]{1,0:T(8,128)(2,1)S(1)} %get-tuple-element.45), channel_id=1, source_target_pairs={{0,16},{4,20},{8,24},{12,28},{16,0},{20,4},{24,8},{28,12},{32,48},... | collective-permute-start | bytes 221192 | tf_op jit(solution)/shard_map/ppermute | solution.py:428
  15.2 5.0 %collective-permute-start.3 = (bf16[144,256]{1,0:T(8,128)(2,1)S(1)}, bf16[144,256]{1,0:T(8,128)(2,1)S(1)}, u32[]{:S(2)}, u32[]{:S(2)}) collective-permute-start(bf16[144,256]{1,0:T(8,128)(2,1)S(1)} %get-tuple-element.46), channel_id=1, source_target_pairs={{0,24},{4,28},{8,16},{12,20},{16,8},{20,12},{24,0},{28,4},{32,56},... | collective-permute-start | bytes 221192 | tf_op jit(solution)/shard_map/ppermute | solution.py:428
  20.6 7.9 %collective-permute-start.4 = (bf16[144,256]{1,0:T(8,128)(2,1)S(1)}, bf16[144,256]{1,0:T(8,128)(2,1)S(1)}, u32[]{:S(2)}, u32[]{:S(2)}) collective-permute-start(bf16[144,256]{1,0:T(8,128)(2,1)S(1)} %get-tuple-element.47.own), channel_id=1, source_target_pairs={{0,48},{4,52},{8,56},{12,60},{16,32},{20,36},{24,40},{28,44},{32,1... | collective-permute-start | bytes 221192 | tf_op jit(solution)/shard_map/ppermute | solution.py:442
  28.7 4.6 %collective-permute-start.5 = (bf16[144,256]{1,0:T(8,128)(2,1)S(1)}, bf16[144,256]{1,0:T(8,128)(2,1)S(1)}, u32[]{:S(2)}, u32[]{:S(2)}) collective-permute-start(bf16[144,256]{1,0:T(8,128)(2,1)S(1)} %shard_map.108.r0), channel_id=1, source_target_pairs={{0,64},{4,68},{8,72},{12,76},{16,80},{20,84},{24,88},{28,92},{32,9... | collective-permute-start | bytes 221192 | tf_op jit(solution)/shard_map/ppermute | solution.py:451
  30.1 5.2 %collective-permute-start.6 = (bf16[144,256]{1,0:T(8,128)(2,1)S(1)}, bf16[144,256]{1,0:T(8,128)(2,1)S(1)}, u32[]{:S(2)}, u32[]{:S(2)}) collective-permute-start(bf16[144,256]{1,0:T(8,128)(2,1)S(1)} %shard_map.108.r0), channel_id=1, source_target_pairs={{0,128},{4,132},{8,136},{12,140},{16,144},{20,148},{24,152},{28,15... | collective-permute-start | bytes 221192 | tf_op jit(solution)/shard_map/ppermute | solution.py:451
  32.7 2.6 %collective-permute-start.7 = (bf16[144,256]{1,0:T(8,128)(2,1)S(1)}, bf16[144,256]{1,0:T(8,128)(2,1)S(1)}, u32[]{:S(2)}, u32[]{:S(2)}) collective-permute-start(bf16[144,256]{1,0:T(8,128)(2,1)S(1)} %shard_map.108.r0), channel_id=1, source_target_pairs={{128,64},{132,68},{136,72},{140,76},{144,80},{148,84},{152,88},{15... | collective-permute-start | bytes 221192 | tf_op jit(solution)/shard_map/ppermute | solution.py:451
  35.9 3.6 %collective-permute-start.8 = (bf16[144,128]{1,0:T(8,128)(2,1)S(1)}, bf16[144,128]{1,0:T(8,128)(2,1)S(1)}, u32[]{:S(2)}, u32[]{:S(2)}) collective-permute-start(bf16[144,128]{1,0:T(8,128)(2,1)S(1)} %get-tuple-element.51), channel_id=1, source_target_pairs={{0,8},{4,12},{8,0},{12,4},{16,24},{20,28},{24,16},{28,20},{32,40},... | collective-permute-start | bytes 110600 | tf_op jit(solution)/shard_map/ppermute | solution.py:463
  36.0 3.8 %collective-permute-start.9 = (bf16[144,128]{1,0:T(8,128)(2,1)S(1)}, bf16[144,128]{1,0:T(8,128)(2,1)S(1)}, u32[]{:S(2)}, u32[]{:S(2)}) collective-permute-start(bf16[144,128]{1,0:T(8,128)(2,1)S(1)} %get-tuple-element.52), channel_id=1, source_target_pairs={{0,16},{4,20},{8,24},{12,28},{16,0},{20,4},{24,8},{28,12},{32,48},... | collective-permute-start | bytes 110600 | tf_op jit(solution)/shard_map/ppermute | solution.py:463
  38.1 4.7 %collective-permute-start.10 = (bf16[144,128]{1,0:T(8,128)(2,1)S(1)}, bf16[144,128]{1,0:T(8,128)(2,1)S(1)}, u32[]{:S(2)}, u32[]{:S(2)}) collective-permute-start(bf16[144,128]{1,0:T(8,128)(2,1)S(1)} %get-tuple-element.53), channel_id=1, source_target_pairs={{0,24},{4,28},{8,16},{12,20},{16,8},{20,12},{24,0},{28,4},{32,56},... | collective-permute-start | bytes 110600 | tf_op jit(solution)/shard_map/ppermute | solution.py:463
  42.8 6.1 %copy-start = (bf16[1024,2048]{1,0:T(8,128)(2,1)S(1)}, bf16[1024,2048]{1,0:T(8,128)(2,1)}, u32[]{:S(2)}) copy-start(bf16[1024,2048]{1,0:T(8,128)(2,1)} %w.1) | copy-start | bytes 12582916
  43.1 5.8 %collective-permute-start.11 = (bf16[4,144,128]{2,1,0:T(8,128)(2,1)S(1)}, bf16[4,144,128]{2,1,0:T(8,128)(2,1)S(1)}, u32[]{:S(2)}, u32[]{:S(2)}) collective-permute-start(bf16[4,144,128]{2,1,0:T(8,128)(2,1)S(1)} %get-tuple-element.55), channel_id=1, source_target_pairs={{0,4},{4,0},{8,12},{12,8},{16,20},{20,16},{24,28},{28,24},{32,36},... | collective-permute-start | bytes 442376 | tf_op jit(solution)/shard_map/ppermute | solution.py:474
  48.9 13.7 %copy-start.1 = (s32[32]{0:T(128)S(1)}, s32[32]{0:T(128)}, u32[]{:S(2)}) copy-start(s32[32]{0:T(128)} %order.1) | copy-start | bytes 388
  50.1 4.7 %collective-permute-start.12 = (bf16[32,2176]{1,0:T(8,128)(2,1)S(1)}, bf16[32,2176]{1,0:T(8,128)(2,1)S(1)}, u32[]{:S(2)}, u32[]{:S(2)}) collective-permute-start(bf16[32,2176]{1,0:T(8,128)(2,1)S(1)} %get-tuple-element.66), channel_id=1, source_target_pairs={{0,1},{1,0},{2,3},{3,2},{4,5},{5,4},{6,7},{7,6},{8,9},{9,8},{10,11... | collective-permute-start | bytes 417800 | tf_op jit(solution)/shard_map/ppermute | solution.py:485
  51.4 8.6 %collective-permute-start.13 = (bf16[32,2176]{1,0:T(8,128)(2,1)S(1)}, bf16[32,2176]{1,0:T(8,128)(2,1)S(1)}, u32[]{:S(2)}, u32[]{:S(2)}) collective-permute-start(bf16[32,2176]{1,0:T(8,128)(2,1)S(1)} %get-tuple-element.67), channel_id=1, source_target_pairs={{0,2},{1,3},{2,0},{3,1},{4,6},{5,7},{6,4},{7,5},{8,10},{9,11},{10,... | collective-permute-start | bytes 417800 | tf_op jit(solution)/shard_map/ppermute | solution.py:485
  53.9 8.7 %collective-permute-start.14 = (bf16[32,2176]{1,0:T(8,128)(2,1)S(1)}, bf16[32,2176]{1,0:T(8,128)(2,1)S(1)}, u32[]{:S(2)}, u32[]{:S(2)}) collective-permute-start(bf16[32,2176]{1,0:T(8,128)(2,1)S(1)} %get-tuple-element.68), channel_id=1, source_target_pairs={{0,3},{1,2},{2,1},{3,0},{4,7},{5,6},{6,5},{7,4},{8,11},{9,10},{10,... | collective-permute-start | bytes 417800 | tf_op jit(solution)/shard_map/ppermute | solution.py:485

commit v6 on v5

--- a/solution.py
+++ b/solution.py
@@ -314,23 +314,35 @@
     send_out[...] = states[1 - core]
 
 
-def project(own, got, local, read, silu, w, acc, o1, o2, o3, tail, normed, total, lasts):
+def gated_heads(part, states, local, read, silu):
+    half = states.shape[0]
+    gated = []
+    for h in range(half):
+        at = part * half + h
+        attention = local[at] + mm_left(read[at], states[h, :DK])
+        mean_square = jnp.mean(attention * attention, axis=-1, keepdims=True)
+        weight = lax.rsqrt(mean_square + EPS) * silu[:, at * DV : (at + 1) * DV]
+        gated.append((attention * weight).astype(bf16))
+    return jnp.concatenate(gated, 1)
+
+
+def weight_rows(part, half):
+    width = half * DV
+    return pl.ds(pl.multiple_of((places()[0] ^ part) * width, width), width)
+
+
+def project_own(own, local, read, silu, w, total):
+    total[...] = mm(gated_heads(0, own, local, read, silu), w[weight_rows(0, own.shape[0])])
+
+
+def project(own, got, begun, local, read, silu, w, acc, o1, o2, o3, tail, total, lasts):
     core = places()[0]
     x = lax.axis_index("head")
     half = own.shape[0]
-    width = half * DV
     for part, states in enumerate((own, got)):
-        gated = []
         for h in range(half):
-            at = part * half + h
-            attention = local[at] + mm_left(read[at], states[h, :DK])
-            mean_square = jnp.mean(attention * attention, axis=-1, keepdims=True)
-            weight = lax.rsqrt(mean_square + EPS) * silu[:, at * DV : (at + 1) * DV]
-            gated.append((attention * weight).astype(bf16))
             rows = states[h, DK:].astype(f32)
             lasts[(core ^ part) * half + h] = jnp.concatenate([rows[:4] + rows[4:8], rows[8:12]], 0)
-        first = pl.multiple_of((core ^ part) * width, width)
-        normed[:, pl.ds(first, width)] = jnp.concatenate(gated, 1)
     finals = []
     for h in range(2 * half):
         rows = lasts[h]
@@ -338,7 +350,7 @@
     finals = jnp.concatenate(finals, 0)
     hi = finals.astype(bf16).astype(f32)
     tail[...] = jnp.concatenate([hi, finals - hi], 0).astype(bf16)
-    total[...] = mm(normed[...], w[...])
+    total[...] = begun[...] + mm(gated_heads(1, got, local, read, silu), w[weight_rows(1, half)])
     acc[...] = total[pl.ds(x * 32, 32)]
     width = total.shape[1]
     for s, o in enumerate((o1, o2, o3)):
@@ -386,6 +398,10 @@
         cost_estimate=cost,
         compiler_params=pltpu.CompilerParams(vmem_limit_bytes=24 * 2**20),
     )(*args)
+
+
+def move(x, axis, pairs):
+    return lax.ppermute(x, axis, pairs)
 
 
 def xor_peers(count, bit):
@@ -425,7 +441,7 @@
         [pltpu.VMEM((2, half) + wide, f32)],
         own, got,
     )
-    m1, m2, m3 = [lax.ppermute(m, "ctx", xor_peers(peers, 2 * s)) for s, m in ((1, m1), (2, m2), (3, m3))]
+    m1, m2, m3 = [move(m, "ctx", xor_peers(peers, 2 * s)) for s, m in ((1, m1), (2, m2), (3, m3))]
     local, read, silu = call(
         local_reads,
         [shape((heads, N, DV), f32), shape((heads, N, DK), f32), shape((N, heads * DV), f32)],
@@ -439,7 +455,7 @@
         [pltpu.VMEM((4,) + block, bf16)],
         m0, m1, m2, m3,
     )
-    total_got = lax.ppermute(total, "ctx", xor_peers(peers, 12))
+    total_got = move(total, "ctx", xor_peers(peers, 12))
     r0 = call(
         row_map,
         shape(block3),
@@ -448,7 +464,7 @@
     )
     rows = [[(i, (i + 16 * s) % peers) for i in range(peers)] for s in (1, 2, 3)]
     rows[2] = [(i, i - 16) for i in range(peers // 2, peers)]
-    r1, r2, r3 = [lax.ppermute(r0, "ctx", pairs) for pairs in rows]
+    r1, r2, r3 = [move(r0, "ctx", pairs) for pairs in rows]
     s0, s1, s2, s3 = call(
         scan_states,
         [shape((ROWS, DV))] * 4,
@@ -460,7 +476,7 @@
         ],
         r0, r1, r2, r3, total, total_got, prefix, prefix_row,
     )
-    s1, s2, s3 = [lax.ppermute(m, "ctx", xor_peers(peers, 2 * s)) for s, m in ((1, s1), (2, s2), (3, s3))]
+    s1, s2, s3 = [move(m, "ctx", xor_peers(peers, 2 * s)) for s, m in ((1, s1), (2, s2), (3, s3))]
     own_state, send_state = call(
         pair_states,
         [shape((half, ROWS, DV))] * 2,
@@ -471,18 +487,24 @@
         ],
         s0, s1, s2, s3, own, got,
     )
-    got_state = lax.ppermute(send_state, "ctx", xor_peers(peers, 1))
+    got_state = move(send_state, "ctx", xor_peers(peers, 1))
+    begun = call(
+        project_own,
+        shape((N, model), f32),
+        [],
+        own_state, local, read, silu, out_weight,
+        flops=10**9,
+    )
     acc, o1, o2, o3, tail = call(
         project,
         [shape((32, model), f32)] + [shape((32, model + DV))] * 3 + [shape((32, DV))],
         [
-            pltpu.VMEM((N, heads * DV), bf16),
             pltpu.VMEM((N, model), f32),
             pltpu.VMEM((heads, 8, DV), f32),
         ],
-        own_state, got_state, local, read, silu, out_weight,
-    )
-    o1, o2, o3 = [lax.ppermute(o, "head", xor_peers(4, s)) for s, o in ((1, o1), (2, o2), (3, o3))]
+        own_state, got_state, begun, local, read, silu, out_weight,
+    )
+    o1, o2, o3 = [move(o, "head", xor_peers(4, s)) for s, o in ((1, o1), (2, o2), (3, o3))]
     return call(
         finish,
         [jax.ShapeDtypeStruct((32, model), bf16), jax.ShapeDtypeStruct((heads, 256), f32)],

time: 64.9 us -> 65.1 us (level)
    pallas_call x10 -> x11, Pallas kernels: 13.3 us -> 13.5 us  [call(): pl.pallas_call(kernel, out_shape=outs, scratch_shapes=scratch, in_specs=s...]
  transfers between devices with their start and end apart: 15 -> 15, of which waited for: 10 -> 10; matrix products, arithmetic and copies ran while one was open for 0% -> 0% of each run, Pallas kernels for 7% -> 8%
where the time goes in v6:
time: 65.1 us; the launch traced here: 64.1 us
  starting transfers between devices  29.9 us (46%)
  waiting for transfers between devices  19.8 us (30%)
  Pallas kernels  13.5 us (21%)
  between operations  0.78 us (1%)
    ppermute x14, starting transfers between devices, move(): return lax.ppermute(x, axis, pairs)  26.6 us
    ppermute x14, waiting for transfers between devices, move(): return lax.ppermute(x, axis, pairs)  19.8 us
    pallas_call x11, Pallas kernels, call(): pl.pallas_call(kernel, out_shape=outs, scratch_shapes=scratch, in_specs=s...  13.5 us
    ppermute x1, starting transfers between devices, per_device(): got = lax.ppermute(send, 'ctx', xor_peers(peers, 1))  3.29 us
  transfers between devices with their start and end apart: 15, of which 10 were waited for; matrix products, arithmetic and copies ran while one was open for 0% of the time, Pallas kernels for 8%

profile of v6, /device:TPU:1, one launch (start us, length us, event | category | flops | bytes accessed | tf_op | source)
XLA Modules:
  0.0 64.1 jit_solution(15620586456926477252)
XLA Ops:
  0.7 4.5 %shard_map.104 = (f32[4,136,256]{2,1,0:T(8,128)S(1)}, f32[4,128,128]{2,1,0:T(8,128)S(1)}, f32[4,128,256]{2,1,0:T(8,128)S(1)}, f32[128,128]{1,0:T(8,128)S(1)}, bf...) custom-call(bf16[128,512]{1,0:T(8,128)(2,1)} %k.1, ...), custom_call_target="tpu_custom_call" | custom-call | tf_op jit(solution)/shard_map/pallas_call | solution.py:393
  5.1 3.3 %collective-permute-start = (f32[4,136,256]{2,1,0:T(8,128)S(1)}, f32[4,136,256]{2,1,0:T(8,128)S(1)}, u32[]{:S(2)}, u32[]{:S(2)}) collective-permute-start(f32[4,136,256]{2,1,0:T(8,128)S(1)} %get-tuple-element.42), channel_id=1, source_target_pairs={{0,4},{4,0},{8,12},{12,8},{16,20},{20,16},{24,28},{28,24},{32,36},... | collective-permute-start | bytes 1671176 | tf_op jit(solution)/shard_map/ppermute | solution.py:436
  8.4 3.3 %shard_map.105 = (f32[4,136,256]{2,1,0:T(8,128)S(1)}, f32[4,128,128]{2,1,0:T(8,128)S(1)}, f32[4,128,256]{2,1,0:T(8,128)S(1)}, f32[128,128]{1,0:T(8,128)S(1)}) custom-call(bf16[128,512]{1,0:T(8,128)(2,1)S(1)} %get-tuple-element.36.k.k_ref, bf16[128,1024]{1,0:T(8,128)(2,1)S(1)} %get-tuple-element.37.v, f32[8,128]{1,0:T(8,128)S(1)} %get-tuple-element.38.g, ...), custom_call_target="tpu_custom_call" | custom-call | flops 1000000000 | tf_op jit(solution)/shard_map/pallas_call | solution.py:393
  12.3 2.9 %collective-permute-start.2 = (bf16[144,256]{1,0:T(8,128)(2,1)S(1)}, bf16[144,256]{1,0:T(8,128)(2,1)S(1)}, u32[]{:S(2)}, u32[]{:S(2)}) collective-permute-start(bf16[144,256]{1,0:T(8,128)(2,1)S(1)} %get-tuple-element.45), channel_id=1, source_target_pairs={{0,16},{4,20},{8,24},{12,28},{16,0},{20,4},{24,8},{28,12},{32,48},... | collective-permute-start | bytes 221192 | tf_op jit(solution)/shard_map/ppermute | solution.py:404
  16.1 1.6 %collective-permute-done.2.m2 = bf16[144,256]{1,0:T(8,128)(2,1)S(1)} collective-permute-done((bf16[144,256]{1,0:T(8,128)(2,1)S(1)}, bf16[144,256]{1,0:T(8,128)(2,1)S(1)}, u32[]{:S(2)}, u32[]{:S(2)}) %collective-permute-start.2) | collective-permute-done | bytes 73760 | tf_op jit(solution)/shard_map/ppermute | solution.py:404
  17.7 2.5 %collective-permute-done.3.m3 = bf16[144,256]{1,0:T(8,128)(2,1)S(1)} collective-permute-done((bf16[144,256]{1,0:T(8,128)(2,1)S(1)}, bf16[144,256]{1,0:T(8,128)(2,1)S(1)}, u32[]{:S(2)}, u32[]{:S(2)}) %collective-permute-start.3) | collective-permute-done | bytes 73760 | tf_op jit(solution)/shard_map/ppermute | solution.py:404
  20.6 6.1 %collective-permute-start.4 = (bf16[144,256]{1,0:T(8,128)(2,1)S(1)}, bf16[144,256]{1,0:T(8,128)(2,1)S(1)}, u32[]{:S(2)}, u32[]{:S(2)}) collective-permute-start(bf16[144,256]{1,0:T(8,128)(2,1)S(1)} %get-tuple-element.47.own), channel_id=1, source_target_pairs={{0,48},{4,52},{8,56},{12,60},{16,32},{20,36},{24,40},{28,44},{32,1... | collective-permute-start | bytes 221192 | tf_op jit(solution)/shard_map/ppermute | solution.py:404
  26.7 1.8 %collective-permute-done.4.got = bf16[144,256]{1,0:T(8,128)(2,1)S(1)} collective-permute-done((bf16[144,256]{1,0:T(8,128)(2,1)S(1)}, bf16[144,256]{1,0:T(8,128)(2,1)S(1)}, u32[]{:S(2)}, u32[]{:S(2)}) %collective-permute-start.4) | collective-permute-done | bytes 73760 | tf_op jit(solution)/shard_map/ppermute | solution.py:404
  28.7 1.3 %collective-permute-start.5 = (bf16[144,256]{1,0:T(8,128)(2,1)S(1)}, bf16[144,256]{1,0:T(8,128)(2,1)S(1)}, u32[]{:S(2)}, u32[]{:S(2)}) collective-permute-start(bf16[144,256]{1,0:T(8,128)(2,1)S(1)} %shard_map.108.r0), channel_id=1, source_target_pairs={{0,64},{4,68},{8,72},{12,76},{16,80},{20,84},{24,88},{28,92},{32,9... | collective-permute-start | bytes 221192 | tf_op jit(solution)/shard_map/ppermute | solution.py:404
  30.1 2.6 %collective-permute-start.6 = (bf16[144,256]{1,0:T(8,128)(2,1)S(1)}, bf16[144,256]{1,0:T(8,128)(2,1)S(1)}, u32[]{:S(2)}, u32[]{:S(2)}) collective-permute-start(bf16[144,256]{1,0:T(8,128)(2,1)S(1)} %shard_map.108.r0), channel_id=1, source_target_pairs={{0,128},{4,132},{8,136},{12,140},{16,144},{20,148},{24,152},{28,15... | collective-permute-start | bytes 221192 | tf_op jit(solution)/shard_map/ppermute | solution.py:404
  33.4 1.9 %collective-permute-done.6.r2 = bf16[144,256]{1,0:T(8,128)(2,1)S(1)} collective-permute-done((bf16[144,256]{1,0:T(8,128)(2,1)S(1)}, bf16[144,256]{1,0:T(8,128)(2,1)S(1)}, u32[]{:S(2)}, u32[]{:S(2)}) %collective-permute-start.6) | collective-permute-done | bytes 73760 | tf_op jit(solution)/shard_map/ppermute | solution.py:404
  36.0 2.1 %collective-permute-start.9 = (bf16[144,128]{1,0:T(8,128)(2,1)S(1)}, bf16[144,128]{1,0:T(8,128)(2,1)S(1)}, u32[]{:S(2)}, u32[]{:S(2)}) collective-permute-start(bf16[144,128]{1,0:T(8,128)(2,1)S(1)} %get-tuple-element.52), channel_id=1, source_target_pairs={{0,16},{4,20},{8,24},{12,28},{16,0},{20,4},{24,8},{28,12},{32,48},... | collective-permute-start | bytes 110600 | tf_op jit(solution)/shard_map/ppermute | solution.py:404
  38.1 1.4 %collective-permute-start.10 = (bf16[144,128]{1,0:T(8,128)(2,1)S(1)}, bf16[144,128]{1,0:T(8,128)(2,1)S(1)}, u32[]{:S(2)}, u32[]{:S(2)}) collective-permute-start(bf16[144,128]{1,0:T(8,128)(2,1)S(1)} %get-tuple-element.53), channel_id=1, source_target_pairs={{0,24},{4,28},{8,16},{12,20},{16,8},{20,12},{24,0},{28,4},{32,56},... | collective-permute-start | bytes 110600 | tf_op jit(solution)/shard_map/ppermute | solution.py:404
  39.8 3.0 %collective-permute-done.10.s3 = bf16[144,128]{1,0:T(8,128)(2,1)S(1)} collective-permute-done((bf16[144,128]{1,0:T(8,128)(2,1)S(1)}, bf16[144,128]{1,0:T(8,128)(2,1)S(1)}, u32[]{:S(2)}, u32[]{:S(2)}) %collective-permute-start.10) | collective-permute-done | bytes 36896 | tf_op jit(solution)/shard_map/ppermute | solution.py:404
  43.1 4.7 %collective-permute-start.11 = (bf16[4,144,128]{2,1,0:T(8,128)(2,1)S(1)}, bf16[4,144,128]{2,1,0:T(8,128)(2,1)S(1)}, u32[]{:S(2)}, u32[]{:S(2)}) collective-permute-start(bf16[4,144,128]{2,1,0:T(8,128)(2,1)S(1)} %get-tuple-element.55), channel_id=1, source_target_pairs={{0,4},{4,0},{8,12},{12,8},{16,20},{20,16},{24,28},{28,24},{32,36},... | collective-permute-start | bytes 442376 | tf_op jit(solution)/shard_map/ppermute | solution.py:404
  47.8 1.1 %shard_map.111 = (f32[8,128,128]{2,1,0:T(8,128)S(1)}, f32[8,128,128]{2,1,0:T(8,128)S(1)}, f32[128,1024]{1,0:T(8,128)S(1)}) custom-call(f32[4,128,128]{2,1,0:T(8,128)S(1)} %get-tuple-element.56.mixes0, f32[4,128,256]{2,1,0:T(8,128)S(1)} %get-tuple-element.57.both0, f32[128,128]{1,0:T(8,128)S(1)} %get-tuple-element.58.sums0, ...), custom_call_target="tpu_custom_call" | custom-call | flops 2000000000 | tf_op jit(solution)/shard_map/pallas_call | solution.py:393
  48.9 0.7 %shard_map.112.begun = f32[128,2048]{1,0:T(8,128)S(1)} custom-call(bf16[4,144,128]{2,1,0:T(8,128)(2,1)S(1)} %get-tuple-element.54.own, f32[8,128,128]{2,1,0:T(8,128)S(1)} %get-tuple-element.62.local, f32[8,128,128]{2,1,0:T(8,128)S(1)} %get-tuple-element.63.read, f32[128,1024]{1,0:T(8,128)S(1)} %get-tuple-element.64.silu, bf16[1024,2048]{1,0:T(8,128)(2,1)S(1)} %copy-done), custom_call_target="tpu_custom_call" | custom-call | flops 1000000000 | tf_op jit(solution)/shard_map/pallas_call | solution.py:393
  49.6 0.7 %shard_map.113 = (f32[32,2048]{1,0:T(8,128)S(1)}, bf16[32,2176]{1,0:T(8,128)(2,1)S(1)}, bf16[32,2176]{1,0:T(8,128)(2,1)S(1)}, bf16[32,2176]{1,0:T(8,128)(2,1)S(1)}, bf16[32,128]{1,0:T(8,128)(2,1)S(1)}) custom-call(bf16[4,144,128]{2,1,0:T(8,128)(2,1)S(1)} %get-tuple-element.54.own, bf16[4,144,128]{2,1,0:T(8,128)(2,1)S(1)} %collective-permute-done.11.got, ...), custom_call_target="tpu_custom_call" | custom-call | tf_op jit(solution)/shard_map/pallas_call | solution.py:393
  50.4 1.3 %collective-permute-start.12 = (bf16[32,2176]{1,0:T(8,128)(2,1)S(1)}, bf16[32,2176]{1,0:T(8,128)(2,1)S(1)}, u32[]{:S(2)}, u32[]{:S(2)}) collective-permute-start(bf16[32,2176]{1,0:T(8,128)(2,1)S(1)} %get-tuple-element.66), channel_id=1, source_target_pairs={{0,1},{1,0},{2,3},{3,2},{4,5},{5,4},{6,7},{7,6},{8,9},{9,8},{10,11... | collective-permute-start | bytes 417800 | tf_op jit(solution)/shard_map/ppermute | solution.py:404
  51.7 2.5 %collective-permute-start.13 = (bf16[32,2176]{1,0:T(8,128)(2,1)S(1)}, bf16[32,2176]{1,0:T(8,128)(2,1)S(1)}, u32[]{:S(2)}, u32[]{:S(2)}) collective-permute-start(bf16[32,2176]{1,0:T(8,128)(2,1)S(1)} %get-tuple-element.67), channel_id=1, source_target_pairs={{0,2},{1,3},{2,0},{3,1},{4,6},{5,7},{6,4},{7,5},{8,10},{9,11},{10,... | collective-permute-start | bytes 417800 | tf_op jit(solution)/shard_map/ppermute | solution.py:404
  54.3 0.7 %collective-permute-done.12.r1 = bf16[32,2176]{1,0:T(8,128)(2,1)S(1)} collective-permute-done((bf16[32,2176]{1,0:T(8,128)(2,1)S(1)}, bf16[32,2176]{1,0:T(8,128)(2,1)S(1)}, u32[]{:S(2)}, u32[]{:S(2)}) %collective-permute-start.12) | collective-permute-done | bytes 139296 | tf_op jit(solution)/shard_map/ppermute | solution.py:404
  55.0 5.2 %collective-permute-done.13.r2 = bf16[32,2176]{1,0:T(8,128)(2,1)S(1)} collective-permute-done((bf16[32,2176]{1,0:T(8,128)(2,1)S(1)}, bf16[32,2176]{1,0:T(8,128)(2,1)S(1)}, u32[]{:S(2)}, u32[]{:S(2)}) %collective-permute-start.13) | collective-permute-done | bytes 139296 | tf_op jit(solution)/shard_map/ppermute | solution.py:404
  60.2 2.6 %collective-permute-done.14.r3 = bf16[32,2176]{1,0:T(8,128)(2,1)S(1)} collective-permute-done((bf16[32,2176]{1,0:T(8,128)(2,1)S(1)}, bf16[32,2176]{1,0:T(8,128)(2,1)S(1)}, u32[]{:S(2)}, u32[]{:S(2)}) %collective-permute-start.14) | collective-permute-done | bytes 139296 | tf_op jit(solution)/shard_map/ppermute | solution.py:404
  62.8 1.3 %shard_map.114 = (bf16[32,2048]{1,0:T(8,128)(2,1)}, f32[8,256]{1,0:T(8,128)}) custom-call(s32[32]{0:T(128)S(1)} %copy-done.1, f32[32,2048]{1,0:T(8,128)S(1)} %get-tuple-element.65.acc, bf16[32,2176]{1,0:T(8,128)(2,1)S(1)} %collective-permute-done.12.r1, bf16[32,2176]{1,0:T(8,128)(2,1)S(1)} %collective-permute-done.13.r2, ...), custom_call_target="tpu_custom_call" | custom-call | tf_op jit(solution)/shard_map/pallas_call | solution.py:393
  (25 shorter events, 4.2 us)
Async XLA Ops:
  0.6 47.2 %copy-start.3 = (bf16[128,512]{1,0:T(8,128)(2,1)S(1)}, bf16[128,512]{1,0:T(8,128)(2,1)}, u32[]{:S(2)}) copy-start(bf16[128,512]{1,0:T(8,128)(2,1)} %q_ref.1) | copy-start | bytes 393220
  0.6 47.2 %copy-start.2 = (bf16[128,1024]{1,0:T(8,128)(2,1)S(1)}, bf16[128,1024]{1,0:T(8,128)(2,1)}, u32[]{:S(2)}) copy-start(bf16[128,1024]{1,0:T(8,128)(2,1)} %gate.1) | copy-start | bytes 786436
  5.1 6.6 %collective-permute-start = (f32[4,136,256]{2,1,0:T(8,128)S(1)}, f32[4,136,256]{2,1,0:T(8,128)S(1)}, u32[]{:S(2)}, u32[]{:S(2)}) collective-permute-start(f32[4,136,256]{2,1,0:T(8,128)S(1)} %get-tuple-element.42), channel_id=1, source_target_pairs={{0,4},{4,0},{8,12},{12,8},{16,20},{20,16},{24,28},{28,24},{32,36},... | collective-permute-start | bytes 1671176 | tf_op jit(solution)/shard_map/ppermute | solution.py:436
  12.2 3.9 %collective-permute-start.1 = (bf16[144,256]{1,0:T(8,128)(2,1)S(1)}, bf16[144,256]{1,0:T(8,128)(2,1)S(1)}, u32[]{:S(2)}, u32[]{:S(2)}) collective-permute-start(bf16[144,256]{1,0:T(8,128)(2,1)S(1)} %get-tuple-element.44), channel_id=1, source_target_pairs={{0,8},{4,12},{8,0},{12,4},{16,24},{20,28},{24,16},{28,20},{32,40},... | collective-permute-start | bytes 221192 | tf_op jit(solution)/shard_map/ppermute | solution.py:404
  12.3 5.4 %collective-permute-start.2 = (bf16[144,256]{1,0:T(8,128)(2,1)S(1)}, bf16[144,256]{1,0:T(8,128)(2,1)S(1)}, u32[]{:S(2)}, u32[]{:S(2)}) collective-permute-start(bf16[144,256]{1,0:T(8,128)(2,1)S(1)} %get-tuple-element.45), channel_id=1, source_target_pairs={{0,16},{4,20},{8,24},{12,28},{16,0},{20,4},{24,8},{28,12},{32,48},... | collective-permute-start | bytes 221192 | tf_op jit(solution)/shard_map/ppermute | solution.py:404
  15.2 5.0 %collective-permute-start.3 = (bf16[144,256]{1,0:T(8,128)(2,1)S(1)}, bf16[144,256]{1,0:T(8,128)(2,1)S(1)}, u32[]{:S(2)}, u32[]{:S(2)}) collective-permute-start(bf16[144,256]{1,0:T(8,128)(2,1)S(1)} %get-tuple-element.46), channel_id=1, source_target_pairs={{0,24},{4,28},{8,16},{12,20},{16,8},{20,12},{24,0},{28,4},{32,56},... | collective-permute-start | bytes 221192 | tf_op jit(solution)/shard_map/ppermute | solution.py:404
  20.6 7.9 %collective-permute-start.4 = (bf16[144,256]{1,0:T(8,128)(2,1)S(1)}, bf16[144,256]{1,0:T(8,128)(2,1)S(1)}, u32[]{:S(2)}, u32[]{:S(2)}) collective-permute-start(bf16[144,256]{1,0:T(8,128)(2,1)S(1)} %get-tuple-element.47.own), channel_id=1, source_target_pairs={{0,48},{4,52},{8,56},{12,60},{16,32},{20,36},{24,40},{28,44},{32,1... | collective-permute-start | bytes 221192 | tf_op jit(solution)/shard_map/ppermute | solution.py:404
  28.7 4.6 %collective-permute-start.5 = (bf16[144,256]{1,0:T(8,128)(2,1)S(1)}, bf16[144,256]{1,0:T(8,128)(2,1)S(1)}, u32[]{:S(2)}, u32[]{:S(2)}) collective-permute-start(bf16[144,256]{1,0:T(8,128)(2,1)S(1)} %shard_map.108.r0), channel_id=1, source_target_pairs={{0,64},{4,68},{8,72},{12,76},{16,80},{20,84},{24,88},{28,92},{32,9... | collective-permute-start | bytes 221192 | tf_op jit(solution)/shard_map/ppermute | solution.py:404
  30.1 5.2 %collective-permute-start.6 = (bf16[144,256]{1,0:T(8,128)(2,1)S(1)}, bf16[144,256]{1,0:T(8,128)(2,1)S(1)}, u32[]{:S(2)}, u32[]{:S(2)}) collective-permute-start(bf16[144,256]{1,0:T(8,128)(2,1)S(1)} %shard_map.108.r0), channel_id=1, source_target_pairs={{0,128},{4,132},{8,136},{12,140},{16,144},{20,148},{24,152},{28,15... | collective-permute-start | bytes 221192 | tf_op jit(solution)/shard_map/ppermute | solution.py:404
  32.7 2.6 %collective-permute-start.7 = (bf16[144,256]{1,0:T(8,128)(2,1)S(1)}, bf16[144,256]{1,0:T(8,128)(2,1)S(1)}, u32[]{:S(2)}, u32[]{:S(2)}) collective-permute-start(bf16[144,256]{1,0:T(8,128)(2,1)S(1)} %shard_map.108.r0), channel_id=1, source_target_pairs={{128,64},{132,68},{136,72},{140,76},{144,80},{148,84},{152,88},{15... | collective-permute-start | bytes 221192 | tf_op jit(solution)/shard_map/ppermute | solution.py:404
  35.9 3.6 %collective-permute-start.8 = (bf16[144,128]{1,0:T(8,128)(2,1)S(1)}, bf16[144,128]{1,0:T(8,128)(2,1)S(1)}, u32[]{:S(2)}, u32[]{:S(2)}) collective-permute-start(bf16[144,128]{1,0:T(8,128)(2,1)S(1)} %get-tuple-element.51), channel_id=1, source_target_pairs={{0,8},{4,12},{8,0},{12,4},{16,24},{20,28},{24,16},{28,20},{32,40},... | collective-permute-start | bytes 110600 | tf_op jit(solution)/shard_map/ppermute | solution.py:404
  36.0 3.8 %collective-permute-start.9 = (bf16[144,128]{1,0:T(8,128)(2,1)S(1)}, bf16[144,128]{1,0:T(8,128)(2,1)S(1)}, u32[]{:S(2)}, u32[]{:S(2)}) collective-permute-start(bf16[144,128]{1,0:T(8,128)(2,1)S(1)} %get-tuple-element.52), channel_id=1, source_target_pairs={{0,16},{4,20},{8,24},{12,28},{16,0},{20,4},{24,8},{28,12},{32,48},... | collective-permute-start | bytes 110600 | tf_op jit(solution)/shard_map/ppermute | solution.py:404
  38.1 4.7 %collective-permute-start.10 = (bf16[144,128]{1,0:T(8,128)(2,1)S(1)}, bf16[144,128]{1,0:T(8,128)(2,1)S(1)}, u32[]{:S(2)}, u32[]{:S(2)}) collective-permute-start(bf16[144,128]{1,0:T(8,128)(2,1)S(1)} %get-tuple-element.53), channel_id=1, source_target_pairs={{0,24},{4,28},{8,16},{12,20},{16,8},{20,12},{24,0},{28,4},{32,56},... | collective-permute-start | bytes 110600 | tf_op jit(solution)/shard_map/ppermute | solution.py:404
  42.8 6.1 %copy-start = (bf16[1024,2048]{1,0:T(8,128)(2,1)S(1)}, bf16[1024,2048]{1,0:T(8,128)(2,1)}, u32[]{:S(2)}) copy-start(bf16[1024,2048]{1,0:T(8,128)(2,1)} %w.3) | copy-start | bytes 12582916
  43.1 6.5 %collective-permute-start.11 = (bf16[4,144,128]{2,1,0:T(8,128)(2,1)S(1)}, bf16[4,144,128]{2,1,0:T(8,128)(2,1)S(1)}, u32[]{:S(2)}, u32[]{:S(2)}) collective-permute-start(bf16[4,144,128]{2,1,0:T(8,128)(2,1)S(1)} %get-tuple-element.55), channel_id=1, source_target_pairs={{0,4},{4,0},{8,12},{12,8},{16,20},{20,16},{24,28},{28,24},{32,36},... | collective-permute-start | bytes 442376 | tf_op jit(solution)/shard_map/ppermute | solution.py:404
  49.6 13.2 %copy-start.1 = (s32[32]{0:T(128)S(1)}, s32[32]{0:T(128)}, u32[]{:S(2)}) copy-start(s32[32]{0:T(128)} %order.1) | copy-start | bytes 388
  50.4 4.6 %collective-permute-start.12 = (bf16[32,2176]{1,0:T(8,128)(2,1)S(1)}, bf16[32,2176]{1,0:T(8,128)(2,1)S(1)}, u32[]{:S(2)}, u32[]{:S(2)}) collective-permute-start(bf16[32,2176]{1,0:T(8,128)(2,1)S(1)} %get-tuple-element.66), channel_id=1, source_target_pairs={{0,1},{1,0},{2,3},{3,2},{4,5},{5,4},{6,7},{7,6},{8,9},{9,8},{10,11... | collective-permute-start | bytes 417800 | tf_op jit(solution)/shard_map/ppermute | solution.py:404
  51.7 8.5 %collective-permute-start.13 = (bf16[32,2176]{1,0:T(8,128)(2,1)S(1)}, bf16[32,2176]{1,0:T(8,128)(2,1)S(1)}, u32[]{:S(2)}, u32[]{:S(2)}) collective-permute-start(bf16[32,2176]{1,0:T(8,128)(2,1)S(1)} %get-tuple-element.67), channel_id=1, source_target_pairs={{0,2},{1,3},{2,0},{3,1},{4,6},{5,7},{6,4},{7,5},{8,10},{9,11},{10,... | collective-permute-start | bytes 417800 | tf_op jit(solution)/shard_map/ppermute | solution.py:404
  54.1 8.6 %collective-permute-start.14 = (bf16[32,2176]{1,0:T(8,128)(2,1)S(1)}, bf16[32,2176]{1,0:T(8,128)(2,1)S(1)}, u32[]{:S(2)}, u32[]{:S(2)}) collective-permute-start(bf16[32,2176]{1,0:T(8,128)(2,1)S(1)} %get-tuple-element.68), channel_id=1, source_target_pairs={{0,3},{1,2},{2,1},{3,0},{4,7},{5,6},{6,5},{7,4},{8,11},{9,10},{10,... | collective-permute-start | bytes 417800 | tf_op jit(solution)/shard_map/ppermute | solution.py:404

commit v7 on v6

--- a/solution.py
+++ b/solution.py
@@ -288,7 +288,7 @@
         here = start
         if t:
             c, link = prefix_row[t - 1, 0:1], prefix_row[t - 1, 1:2]
-            here = apply_map((c, prefix[t - 1, :, :DK], prefix[t - 1, :, DK:]), link, start)
+            here = apply_map((c, prefix[t - 1, :, :DK].astype(bf16), prefix[t - 1, :, DK:]), link, start)
         pay[t, :DK] = here.astype(bf16)
         rows = final[pl.ds(4 * (y * 8 + high * 4 + t), 4)]
         hi = rows.astype(bf16).astype(f32)
@@ -398,10 +398,6 @@
         cost_estimate=cost,
         compiler_params=pltpu.CompilerParams(vmem_limit_bytes=24 * 2**20),
     )(*args)
-
-
-def move(x, axis, pairs):
-    return lax.ppermute(x, axis, pairs)
 
 
 def xor_peers(count, bit):
@@ -441,7 +437,7 @@
         [pltpu.VMEM((2, half) + wide, f32)],
         own, got,
     )
-    m1, m2, m3 = [move(m, "ctx", xor_peers(peers, 2 * s)) for s, m in ((1, m1), (2, m2), (3, m3))]
+    m1, m2, m3 = [lax.ppermute(m, "ctx", xor_peers(peers, 2 * s)) for s, m in ((1, m1), (2, m2), (3, m3))]
     local, read, silu = call(
         local_reads,
         [shape((heads, N, DV), f32), shape((heads, N, DK), f32), shape((N, heads * DV), f32)],
@@ -455,7 +451,7 @@
         [pltpu.VMEM((4,) + block, bf16)],
         m0, m1, m2, m3,
     )
-    total_got = move(total, "ctx", xor_peers(peers, 12))
+    total_got = lax.ppermute(total, "ctx", xor_peers(peers, 12))
     r0 = call(
         row_map,
         shape(block3),
@@ -464,7 +460,7 @@
     )
     rows = [[(i, (i + 16 * s) % peers) for i in range(peers)] for s in (1, 2, 3)]
     rows[2] = [(i, i - 16) for i in range(peers // 2, peers)]
-    r1, r2, r3 = [move(r0, "ctx", pairs) for pairs in rows]
+    r1, r2, r3 = [lax.ppermute(r0, "ctx", pairs) for pairs in rows]
     s0, s1, s2, s3 = call(
         scan_states,
         [shape((ROWS, DV))] * 4,
@@ -476,7 +472,7 @@
         ],
         r0, r1, r2, r3, total, total_got, prefix, prefix_row,
     )
-    s1, s2, s3 = [move(m, "ctx", xor_peers(peers, 2 * s)) for s, m in ((1, s1), (2, s2), (3, s3))]
+    s1, s2, s3 = [lax.ppermute(m, "ctx", xor_peers(peers, 2 * s)) for s, m in ((1, s1), (2, s2), (3, s3))]
     own_state, send_state = call(
         pair_states,
         [shape((half, ROWS, DV))] * 2,
@@ -487,7 +483,7 @@
         ],
         s0, s1, s2, s3, own, got,
     )
-    got_state = move(send_state, "ctx", xor_peers(peers, 1))
+    got_state = lax.ppermute(send_state, "ctx", xor_peers(peers, 1))
     begun = call(
         project_own,
         shape((N, model), f32),
@@ -504,7 +500,7 @@
         ],
         own_state, got_state, begun, local, read, silu, out_weight,
     )
-    o1, o2, o3 = [move(o, "head", xor_peers(4, s)) for s, o in ((1, o1), (2, o2), (3, o3))]
+    o1, o2, o3 = [lax.ppermute(o, "head", xor_peers(4, s)) for s, o in ((1, o1), (2, o2), (3, o3))]
     return call(
         finish,
         [jax.ShapeDtypeStruct((32, model), bf16), jax.ShapeDtypeStruct((heads, 256), f32)],

time: 65.1 us -> 65 us (level)
  no operation moved by 1% of the time
where the time goes in v7:
time: 65 us; the launch traced here: 64 us
  starting transfers between devices  29.9 us (46%)
  waiting for transfers between devices  19.8 us (30%)
  Pallas kernels  13.5 us (21%)
  between operations  0.78 us (1%)
    pallas_call x11, Pallas kernels, call(): pl.pallas_call(kernel, out_shape=outs, scratch_shapes=scratch, in_specs=s...  13.5 us
    ppermute x3, waiting for transfers between devices, per_device(): lax.ppermute(o, 'head', xor_peers(4, s))  8.46 us
    ppermute x6, waiting for transfers between devices, per_device(): lax.ppermute(m, 'ctx', xor_peers(peers, 2 * s))  7.67 us
    ppermute x6, starting transfers between devices, per_device(): lax.ppermute(m, 'ctx', xor_peers(peers, 2 * s))  7.25 us
    ppermute x1, starting transfers between devices, per_device(): total_got = lax.ppermute(total, 'ctx', xor_peers(peers, 12))  6.09 us
    ppermute x1, starting transfers between devices, per_device(): got_state = lax.ppermute(send_state, 'ctx', xor_peers(peers, 1))  4.68 us
    ppermute x3, starting transfers between devices, per_device(): r1, r2, r3 = [lax.ppermute(r0, 'ctx', pairs) for pairs in rows]  4.63 us
    ppermute x3, starting transfers between devices, per_device(): lax.ppermute(o, 'head', xor_peers(4, s))  3.95 us
  transfers between devices with their start and end apart: 15, of which 10 were waited for; matrix products, arithmetic and copies ran while one was open for 0% of the time, Pallas kernels for 8%

profile of v7, /device:TPU:1, one launch (start us, length us, event | category | flops | bytes accessed | tf_op | source)
XLA Modules:
  0.0 64.0 jit_solution(2991197688280099711)
XLA Ops:
  0.7 4.5 %shard_map.104 = (f32[4,136,256]{2,1,0:T(8,128)S(1)}, f32[4,128,128]{2,1,0:T(8,128)S(1)}, f32[4,128,256]{2,1,0:T(8,128)S(1)}, f32[128,128]{1,0:T(8,128)S(1)}, bf...) custom-call(bf16[128,512]{1,0:T(8,128)(2,1)} %k.1, ...), custom_call_target="tpu_custom_call" | custom-call | tf_op jit(solution)/shard_map/pallas_call | solution.py:393
  5.1 3.3 %collective-permute-start = (f32[4,136,256]{2,1,0:T(8,128)S(1)}, f32[4,136,256]{2,1,0:T(8,128)S(1)}, u32[]{:S(2)}, u32[]{:S(2)}) collective-permute-start(f32[4,136,256]{2,1,0:T(8,128)S(1)} %get-tuple-element.42), channel_id=1, source_target_pairs={{0,4},{4,0},{8,12},{12,8},{16,20},{20,16},{24,28},{28,24},{32,36},... | collective-permute-start | bytes 1671176 | tf_op jit(solution)/shard_map/ppermute | solution.py:432
  8.4 3.3 %shard_map.105 = (f32[4,136,256]{2,1,0:T(8,128)S(1)}, f32[4,128,128]{2,1,0:T(8,128)S(1)}, f32[4,128,256]{2,1,0:T(8,128)S(1)}, f32[128,128]{1,0:T(8,128)S(1)}) custom-call(bf16[128,512]{1,0:T(8,128)(2,1)S(1)} %get-tuple-element.36.k.k_ref, bf16[128,1024]{1,0:T(8,128)(2,1)S(1)} %get-tuple-element.37.v, f32[8,128]{1,0:T(8,128)S(1)} %get-tuple-element.38.g, ...), custom_call_target="tpu_custom_call" | custom-call | flops 1000000000 | tf_op jit(solution)/shard_map/pallas_call | solution.py:393
  12.3 2.9 %collective-permute-start.2 = (bf16[144,256]{1,0:T(8,128)(2,1)S(1)}, bf16[144,256]{1,0:T(8,128)(2,1)S(1)}, u32[]{:S(2)}, u32[]{:S(2)}) collective-permute-start(bf16[144,256]{1,0:T(8,128)(2,1)S(1)} %get-tuple-element.45), channel_id=1, source_target_pairs={{0,16},{4,20},{8,24},{12,28},{16,0},{20,4},{24,8},{28,12},{32,48},... | collective-permute-start | bytes 221192 | tf_op jit(solution)/shard_map/ppermute | solution.py:440
  16.1 1.6 %collective-permute-done.2.m2 = bf16[144,256]{1,0:T(8,128)(2,1)S(1)} collective-permute-done((bf16[144,256]{1,0:T(8,128)(2,1)S(1)}, bf16[144,256]{1,0:T(8,128)(2,1)S(1)}, u32[]{:S(2)}, u32[]{:S(2)}) %collective-permute-start.2) | collective-permute-done | bytes 73760 | tf_op jit(solution)/shard_map/ppermute | solution.py:440
  17.7 2.5 %collective-permute-done.3.m3 = bf16[144,256]{1,0:T(8,128)(2,1)S(1)} collective-permute-done((bf16[144,256]{1,0:T(8,128)(2,1)S(1)}, bf16[144,256]{1,0:T(8,128)(2,1)S(1)}, u32[]{:S(2)}, u32[]{:S(2)}) %collective-permute-start.3) | collective-permute-done | bytes 73760 | tf_op jit(solution)/shard_map/ppermute | solution.py:440
  20.6 6.1 %collective-permute-start.4 = (bf16[144,256]{1,0:T(8,128)(2,1)S(1)}, bf16[144,256]{1,0:T(8,128)(2,1)S(1)}, u32[]{:S(2)}, u32[]{:S(2)}) collective-permute-start(bf16[144,256]{1,0:T(8,128)(2,1)S(1)} %get-tuple-element.47.own), channel_id=1, source_target_pairs={{0,48},{4,52},{8,56},{12,60},{16,32},{20,36},{24,40},{28,44},{32,1... | collective-permute-start | bytes 221192 | tf_op jit(solution)/shard_map/ppermute | solution.py:454
  26.7 1.8 %collective-permute-done.4.got = bf16[144,256]{1,0:T(8,128)(2,1)S(1)} collective-permute-done((bf16[144,256]{1,0:T(8,128)(2,1)S(1)}, bf16[144,256]{1,0:T(8,128)(2,1)S(1)}, u32[]{:S(2)}, u32[]{:S(2)}) %collective-permute-start.4) | collective-permute-done | bytes 73760 | tf_op jit(solution)/shard_map/ppermute | solution.py:454
  28.7 1.3 %collective-permute-start.5 = (bf16[144,256]{1,0:T(8,128)(2,1)S(1)}, bf16[144,256]{1,0:T(8,128)(2,1)S(1)}, u32[]{:S(2)}, u32[]{:S(2)}) collective-permute-start(bf16[144,256]{1,0:T(8,128)(2,1)S(1)} %shard_map.108.r0), channel_id=1, source_target_pairs={{0,64},{4,68},{8,72},{12,76},{16,80},{20,84},{24,88},{28,92},{32,9... | collective-permute-start | bytes 221192 | tf_op jit(solution)/shard_map/ppermute | solution.py:463
  30.1 2.6 %collective-permute-start.6 = (bf16[144,256]{1,0:T(8,128)(2,1)S(1)}, bf16[144,256]{1,0:T(8,128)(2,1)S(1)}, u32[]{:S(2)}, u32[]{:S(2)}) collective-permute-start(bf16[144,256]{1,0:T(8,128)(2,1)S(1)} %shard_map.108.r0), channel_id=1, source_target_pairs={{0,128},{4,132},{8,136},{12,140},{16,144},{20,148},{24,152},{28,15... | collective-permute-start | bytes 221192 | tf_op jit(solution)/shard_map/ppermute | solution.py:463
  33.4 1.9 %collective-permute-done.6.r2 = bf16[144,256]{1,0:T(8,128)(2,1)S(1)} collective-permute-done((bf16[144,256]{1,0:T(8,128)(2,1)S(1)}, bf16[144,256]{1,0:T(8,128)(2,1)S(1)}, u32[]{:S(2)}, u32[]{:S(2)}) %collective-permute-start.6) | collective-permute-done | bytes 73760 | tf_op jit(solution)/shard_map/ppermute | solution.py:463
  36.0 2.1 %collective-permute-start.9 = (bf16[144,128]{1,0:T(8,128)(2,1)S(1)}, bf16[144,128]{1,0:T(8,128)(2,1)S(1)}, u32[]{:S(2)}, u32[]{:S(2)}) collective-permute-start(bf16[144,128]{1,0:T(8,128)(2,1)S(1)} %get-tuple-element.52), channel_id=1, source_target_pairs={{0,16},{4,20},{8,24},{12,28},{16,0},{20,4},{24,8},{28,12},{32,48},... | collective-permute-start | bytes 110600 | tf_op jit(solution)/shard_map/ppermute | solution.py:475
  38.1 1.4 %collective-permute-start.10 = (bf16[144,128]{1,0:T(8,128)(2,1)S(1)}, bf16[144,128]{1,0:T(8,128)(2,1)S(1)}, u32[]{:S(2)}, u32[]{:S(2)}) collective-permute-start(bf16[144,128]{1,0:T(8,128)(2,1)S(1)} %get-tuple-element.53), channel_id=1, source_target_pairs={{0,24},{4,28},{8,16},{12,20},{16,8},{20,12},{24,0},{28,4},{32,56},... | collective-permute-start | bytes 110600 | tf_op jit(solution)/shard_map/ppermute | solution.py:475
  39.8 3.0 %collective-permute-done.10.s3 = bf16[144,128]{1,0:T(8,128)(2,1)S(1)} collective-permute-done((bf16[144,128]{1,0:T(8,128)(2,1)S(1)}, bf16[144,128]{1,0:T(8,128)(2,1)S(1)}, u32[]{:S(2)}, u32[]{:S(2)}) %collective-permute-start.10) | collective-permute-done | bytes 36896 | tf_op jit(solution)/shard_map/ppermute | solution.py:475
  43.1 4.7 %collective-permute-start.11 = (bf16[4,144,128]{2,1,0:T(8,128)(2,1)S(1)}, bf16[4,144,128]{2,1,0:T(8,128)(2,1)S(1)}, u32[]{:S(2)}, u32[]{:S(2)}) collective-permute-start(bf16[4,144,128]{2,1,0:T(8,128)(2,1)S(1)} %get-tuple-element.55), channel_id=1, source_target_pairs={{0,4},{4,0},{8,12},{12,8},{16,20},{20,16},{24,28},{28,24},{32,36},... | collective-permute-start | bytes 442376 | tf_op jit(solution)/shard_map/ppermute | solution.py:486
  47.8 1.1 %shard_map.111 = (f32[8,128,128]{2,1,0:T(8,128)S(1)}, f32[8,128,128]{2,1,0:T(8,128)S(1)}, f32[128,1024]{1,0:T(8,128)S(1)}) custom-call(f32[4,128,128]{2,1,0:T(8,128)S(1)} %get-tuple-element.56.mixes0, f32[4,128,256]{2,1,0:T(8,128)S(1)} %get-tuple-element.57.both0, f32[128,128]{1,0:T(8,128)S(1)} %get-tuple-element.58.sums0, ...), custom_call_target="tpu_custom_call" | custom-call | flops 2000000000 | tf_op jit(solution)/shard_map/pallas_call | solution.py:393
  48.9 0.7 %shard_map.112.begun = f32[128,2048]{1,0:T(8,128)S(1)} custom-call(bf16[4,144,128]{2,1,0:T(8,128)(2,1)S(1)} %get-tuple-element.54.own, f32[8,128,128]{2,1,0:T(8,128)S(1)} %get-tuple-element.62.local, f32[8,128,128]{2,1,0:T(8,128)S(1)} %get-tuple-element.63.read, f32[128,1024]{1,0:T(8,128)S(1)} %get-tuple-element.64.silu, bf16[1024,2048]{1,0:T(8,128)(2,1)S(1)} %copy-done), custom_call_target="tpu_custom_call" | custom-call | flops 1000000000 | tf_op jit(solution)/shard_map/pallas_call | solution.py:393
  49.6 0.7 %shard_map.113 = (f32[32,2048]{1,0:T(8,128)S(1)}, bf16[32,2176]{1,0:T(8,128)(2,1)S(1)}, bf16[32,2176]{1,0:T(8,128)(2,1)S(1)}, bf16[32,2176]{1,0:T(8,128)(2,1)S(1)}, bf16[32,128]{1,0:T(8,128)(2,1)S(1)}) custom-call(bf16[4,144,128]{2,1,0:T(8,128)(2,1)S(1)} %get-tuple-element.54.own, bf16[4,144,128]{2,1,0:T(8,128)(2,1)S(1)} %collective-permute-done.11.got, ...), custom_call_target="tpu_custom_call" | custom-call | tf_op jit(solution)/shard_map/pallas_call | solution.py:393
  50.3 1.3 %collective-permute-start.12 = (bf16[32,2176]{1,0:T(8,128)(2,1)S(1)}, bf16[32,2176]{1,0:T(8,128)(2,1)S(1)}, u32[]{:S(2)}, u32[]{:S(2)}) collective-permute-start(bf16[32,2176]{1,0:T(8,128)(2,1)S(1)} %get-tuple-element.66), channel_id=1, source_target_pairs={{0,1},{1,0},{2,3},{3,2},{4,5},{5,4},{6,7},{7,6},{8,9},{9,8},{10,11... | collective-permute-start | bytes 417800 | tf_op jit(solution)/shard_map/ppermute | solution.py:503
  51.6 2.5 %collective-permute-start.13 = (bf16[32,2176]{1,0:T(8,128)(2,1)S(1)}, bf16[32,2176]{1,0:T(8,128)(2,1)S(1)}, u32[]{:S(2)}, u32[]{:S(2)}) collective-permute-start(bf16[32,2176]{1,0:T(8,128)(2,1)S(1)} %get-tuple-element.67), channel_id=1, source_target_pairs={{0,2},{1,3},{2,0},{3,1},{4,6},{5,7},{6,4},{7,5},{8,10},{9,11},{10,... | collective-permute-start | bytes 417800 | tf_op jit(solution)/shard_map/ppermute | solution.py:503
  54.3 0.7 %collective-permute-done.12.r1 = bf16[32,2176]{1,0:T(8,128)(2,1)S(1)} collective-permute-done((bf16[32,2176]{1,0:T(8,128)(2,1)S(1)}, bf16[32,2176]{1,0:T(8,128)(2,1)S(1)}, u32[]{:S(2)}, u32[]{:S(2)}) %collective-permute-start.12) | collective-permute-done | bytes 139296 | tf_op jit(solution)/shard_map/ppermute | solution.py:503
  55.0 5.2 %collective-permute-done.13.r2 = bf16[32,2176]{1,0:T(8,128)(2,1)S(1)} collective-permute-done((bf16[32,2176]{1,0:T(8,128)(2,1)S(1)}, bf16[32,2176]{1,0:T(8,128)(2,1)S(1)}, u32[]{:S(2)}, u32[]{:S(2)}) %collective-permute-start.13) | collective-permute-done | bytes 139296 | tf_op jit(solution)/shard_map/ppermute | solution.py:503
  60.2 2.6 %collective-permute-done.14.r3 = bf16[32,2176]{1,0:T(8,128)(2,1)S(1)} collective-permute-done((bf16[32,2176]{1,0:T(8,128)(2,1)S(1)}, bf16[32,2176]{1,0:T(8,128)(2,1)S(1)}, u32[]{:S(2)}, u32[]{:S(2)}) %collective-permute-start.14) | collective-permute-done | bytes 139296 | tf_op jit(solution)/shard_map/ppermute | solution.py:503
  62.7 1.3 %shard_map.114 = (bf16[32,2048]{1,0:T(8,128)(2,1)}, f32[8,256]{1,0:T(8,128)}) custom-call(s32[32]{0:T(128)S(1)} %copy-done.1, f32[32,2048]{1,0:T(8,128)S(1)} %get-tuple-element.65.acc, bf16[32,2176]{1,0:T(8,128)(2,1)S(1)} %collective-permute-done.12.r1, bf16[32,2176]{1,0:T(8,128)(2,1)S(1)} %collective-permute-done.13.r2, ...), custom_call_target="tpu_custom_call" | custom-call | tf_op jit(solution)/shard_map/pallas_call | solution.py:393
  (25 shorter events, 4.2 us)
Async XLA Ops:
  0.6 47.1 %copy-start.3 = (bf16[128,512]{1,0:T(8,128)(2,1)S(1)}, bf16[128,512]{1,0:T(8,128)(2,1)}, u32[]{:S(2)}) copy-start(bf16[128,512]{1,0:T(8,128)(2,1)} %q_ref.1) | copy-start | bytes 393220
  0.6 47.1 %copy-start.2 = (bf16[128,1024]{1,0:T(8,128)(2,1)S(1)}, bf16[128,1024]{1,0:T(8,128)(2,1)}, u32[]{:S(2)}) copy-start(bf16[128,1024]{1,0:T(8,128)(2,1)} %gate.1) | copy-start | bytes 786436
  5.1 6.6 %collective-permute-start = (f32[4,136,256]{2,1,0:T(8,128)S(1)}, f32[4,136,256]{2,1,0:T(8,128)S(1)}, u32[]{:S(2)}, u32[]{:S(2)}) collective-permute-start(f32[4,136,256]{2,1,0:T(8,128)S(1)} %get-tuple-element.42), channel_id=1, source_target_pairs={{0,4},{4,0},{8,12},{12,8},{16,20},{20,16},{24,28},{28,24},{32,36},... | collective-permute-start | bytes 1671176 | tf_op jit(solution)/shard_map/ppermute | solution.py:432
  12.2 3.9 %collective-permute-start.1 = (bf16[144,256]{1,0:T(8,128)(2,1)S(1)}, bf16[144,256]{1,0:T(8,128)(2,1)S(1)}, u32[]{:S(2)}, u32[]{:S(2)}) collective-permute-start(bf16[144,256]{1,0:T(8,128)(2,1)S(1)} %get-tuple-element.44), channel_id=1, source_target_pairs={{0,8},{4,12},{8,0},{12,4},{16,24},{20,28},{24,16},{28,20},{32,40},... | collective-permute-start | bytes 221192 | tf_op jit(solution)/shard_map/ppermute | solution.py:440
  12.3 5.4 %collective-permute-start.2 = (bf16[144,256]{1,0:T(8,128)(2,1)S(1)}, bf16[144,256]{1,0:T(8,128)(2,1)S(1)}, u32[]{:S(2)}, u32[]{:S(2)}) collective-permute-start(bf16[144,256]{1,0:T(8,128)(2,1)S(1)} %get-tuple-element.45), channel_id=1, source_target_pairs={{0,16},{4,20},{8,24},{12,28},{16,0},{20,4},{24,8},{28,12},{32,48},... | collective-permute-start | bytes 221192 | tf_op jit(solution)/shard_map/ppermute | solution.py:440
  15.2 5.0 %collective-permute-start.3 = (bf16[144,256]{1,0:T(8,128)(2,1)S(1)}, bf16[144,256]{1,0:T(8,128)(2,1)S(1)}, u32[]{:S(2)}, u32[]{:S(2)}) collective-permute-start(bf16[144,256]{1,0:T(8,128)(2,1)S(1)} %get-tuple-element.46), channel_id=1, source_target_pairs={{0,24},{4,28},{8,16},{12,20},{16,8},{20,12},{24,0},{28,4},{32,56},... | collective-permute-start | bytes 221192 | tf_op jit(solution)/shard_map/ppermute | solution.py:440
  20.6 7.9 %collective-permute-start.4 = (bf16[144,256]{1,0:T(8,128)(2,1)S(1)}, bf16[144,256]{1,0:T(8,128)(2,1)S(1)}, u32[]{:S(2)}, u32[]{:S(2)}) collective-permute-start(bf16[144,256]{1,0:T(8,128)(2,1)S(1)} %get-tuple-element.47.own), channel_id=1, source_target_pairs={{0,48},{4,52},{8,56},{12,60},{16,32},{20,36},{24,40},{28,44},{32,1... | collective-permute-start | bytes 221192 | tf_op jit(solution)/shard_map/ppermute | solution.py:454
  28.7 4.6 %collective-permute-start.5 = (bf16[144,256]{1,0:T(8,128)(2,1)S(1)}, bf16[144,256]{1,0:T(8,128)(2,1)S(1)}, u32[]{:S(2)}, u32[]{:S(2)}) collective-permute-start(bf16[144,256]{1,0:T(8,128)(2,1)S(1)} %shard_map.108.r0), channel_id=1, source_target_pairs={{0,64},{4,68},{8,72},{12,76},{16,80},{20,84},{24,88},{28,92},{32,9... | collective-permute-start | bytes 221192 | tf_op jit(solution)/shard_map/ppermute | solution.py:463
  30.1 5.2 %collective-permute-start.6 = (bf16[144,256]{1,0:T(8,128)(2,1)S(1)}, bf16[144,256]{1,0:T(8,128)(2,1)S(1)}, u32[]{:S(2)}, u32[]{:S(2)}) collective-permute-start(bf16[144,256]{1,0:T(8,128)(2,1)S(1)} %shard_map.108.r0), channel_id=1, source_target_pairs={{0,128},{4,132},{8,136},{12,140},{16,144},{20,148},{24,152},{28,15... | collective-permute-start | bytes 221192 | tf_op jit(solution)/shard_map/ppermute | solution.py:463
  32.7 2.6 %collective-permute-start.7 = (bf16[144,256]{1,0:T(8,128)(2,1)S(1)}, bf16[144,256]{1,0:T(8,128)(2,1)S(1)}, u32[]{:S(2)}, u32[]{:S(2)}) collective-permute-start(bf16[144,256]{1,0:T(8,128)(2,1)S(1)} %shard_map.108.r0), channel_id=1, source_target_pairs={{128,64},{132,68},{136,72},{140,76},{144,80},{148,84},{152,88},{15... | collective-permute-start | bytes 221192 | tf_op jit(solution)/shard_map/ppermute | solution.py:463
  35.9 3.6 %collective-permute-start.8 = (bf16[144,128]{1,0:T(8,128)(2,1)S(1)}, bf16[144,128]{1,0:T(8,128)(2,1)S(1)}, u32[]{:S(2)}, u32[]{:S(2)}) collective-permute-start(bf16[144,128]{1,0:T(8,128)(2,1)S(1)} %get-tuple-element.51), channel_id=1, source_target_pairs={{0,8},{4,12},{8,0},{12,4},{16,24},{20,28},{24,16},{28,20},{32,40},... | collective-permute-start | bytes 110600 | tf_op jit(solution)/shard_map/ppermute | solution.py:475
  36.0 3.8 %collective-permute-start.9 = (bf16[144,128]{1,0:T(8,128)(2,1)S(1)}, bf16[144,128]{1,0:T(8,128)(2,1)S(1)}, u32[]{:S(2)}, u32[]{:S(2)}) collective-permute-start(bf16[144,128]{1,0:T(8,128)(2,1)S(1)} %get-tuple-element.52), channel_id=1, source_target_pairs={{0,16},{4,20},{8,24},{12,28},{16,0},{20,4},{24,8},{28,12},{32,48},... | collective-permute-start | bytes 110600 | tf_op jit(solution)/shard_map/ppermute | solution.py:475
  38.1 4.7 %collective-permute-start.10 = (bf16[144,128]{1,0:T(8,128)(2,1)S(1)}, bf16[144,128]{1,0:T(8,128)(2,1)S(1)}, u32[]{:S(2)}, u32[]{:S(2)}) collective-permute-start(bf16[144,128]{1,0:T(8,128)(2,1)S(1)} %get-tuple-element.53), channel_id=1, source_target_pairs={{0,24},{4,28},{8,16},{12,20},{16,8},{20,12},{24,0},{28,4},{32,56},... | collective-permute-start | bytes 110600 | tf_op jit(solution)/shard_map/ppermute | solution.py:475
  42.8 6.1 %copy-start = (bf16[1024,2048]{1,0:T(8,128)(2,1)S(1)}, bf16[1024,2048]{1,0:T(8,128)(2,1)}, u32[]{:S(2)}) copy-start(bf16[1024,2048]{1,0:T(8,128)(2,1)} %w.3) | copy-start | bytes 12582916
  43.1 6.5 %collective-permute-start.11 = (bf16[4,144,128]{2,1,0:T(8,128)(2,1)S(1)}, bf16[4,144,128]{2,1,0:T(8,128)(2,1)S(1)}, u32[]{:S(2)}, u32[]{:S(2)}) collective-permute-start(bf16[4,144,128]{2,1,0:T(8,128)(2,1)S(1)} %get-tuple-element.55), channel_id=1, source_target_pairs={{0,4},{4,0},{8,12},{12,8},{16,20},{20,16},{24,28},{28,24},{32,36},... | collective-permute-start | bytes 442376 | tf_op jit(solution)/shard_map/ppermute | solution.py:486
  49.6 13.2 %copy-start.1 = (s32[32]{0:T(128)S(1)}, s32[32]{0:T(128)}, u32[]{:S(2)}) copy-start(s32[32]{0:T(128)} %order.1) | copy-start | bytes 388
  50.3 4.6 %collective-permute-start.12 = (bf16[32,2176]{1,0:T(8,128)(2,1)S(1)}, bf16[32,2176]{1,0:T(8,128)(2,1)S(1)}, u32[]{:S(2)}, u32[]{:S(2)}) collective-permute-start(bf16[32,2176]{1,0:T(8,128)(2,1)S(1)} %get-tuple-element.66), channel_id=1, source_target_pairs={{0,1},{1,0},{2,3},{3,2},{4,5},{5,4},{6,7},{7,6},{8,9},{9,8},{10,11... | collective-permute-start | bytes 417800 | tf_op jit(solution)/shard_map/ppermute | solution.py:503
  51.6 8.5 %collective-permute-start.13 = (bf16[32,2176]{1,0:T(8,128)(2,1)S(1)}, bf16[32,2176]{1,0:T(8,128)(2,1)S(1)}, u32[]{:S(2)}, u32[]{:S(2)}) collective-permute-start(bf16[32,2176]{1,0:T(8,128)(2,1)S(1)} %get-tuple-element.67), channel_id=1, source_target_pairs={{0,2},{1,3},{2,0},{3,1},{4,6},{5,7},{6,4},{7,5},{8,10},{9,11},{10,... | collective-permute-start | bytes 417800 | tf_op jit(solution)/shard_map/ppermute | solution.py:503
  54.1 8.6 %collective-permute-start.14 = (bf16[32,2176]{1,0:T(8,128)(2,1)S(1)}, bf16[32,2176]{1,0:T(8,128)(2,1)S(1)}, u32[]{:S(2)}, u32[]{:S(2)}) collective-permute-start(bf16[32,2176]{1,0:T(8,128)(2,1)S(1)} %get-tuple-element.68), channel_id=1, source_target_pairs={{0,3},{1,2},{2,1},{3,0},{4,7},{5,6},{6,5},{7,4},{8,11},{9,10},{10,... | collective-permute-start | bytes 417800 | tf_op jit(solution)/shard_map/ppermute | solution.py:503
